TPU v7x, 32 devices: a whole 2x2x4 slice. The times are simulated.
32 devices in a mesh: seq: 16 (over z, y, x), bat: 2 (over core).
Axes of the slice: x: 2, y: 2, z: 4, core: 2. Of those that a mesh axis runs over, the one named last changes fastest.
Arguments:
- tokens: bfloat16 [2, 65536, 256], P('bat', 'seq'), may hold values from -6 to 6
- filter_spectrum: bfloat16 [2, 256, 256, 256], P(None, 'seq', None, 'bat'), may hold values from -6 to 6
- skip_gain: float32 [256], replicated, may hold values from 0.5 to 1.5
Outputs:
- mixed: bfloat16 [2, 65536, 256], P('bat', 'seq')
All inputs are finite; a program needn't handle non-finite values.
Results may differ from a plain program's by a relative error of at most 0.012.
Values may be sent and summed in bfloat16 or wider, within the bound.
No kernel may reach another device: no remote copies, remote signals or barrier semaphores. Data moves between devices by JAX's collectives and lax.ppermute only.
A program may use at most 64 MiB of HBM per device.

v0:
```python
import math

import jax
import jax.numpy as jnp
from jax import lax
from jax.sharding import PartitionSpec as P

N1 = 256
N2 = 256


def cos_sin(points):
    steps_range = jnp.arange(points, dtype=jnp.int32)
    index_grid = steps_range[:, None] * steps_range[None, :] % points
    phase_angle = index_grid.astype(jnp.float32) * (2.0 * math.pi / points)
    return (jnp.cos(phase_angle), jnp.sin(phase_angle))


def real_table(points):
    cosine, sine_vals = cos_sin(points)
    return jnp.stack([cosine, -sine_vals], axis=1).astype(jnp.bfloat16)


def complex_table(points, signum, factor):
    cosine, sine_vals = cos_sin(points)
    top_rows = jnp.stack([cosine, signum * sine_vals], axis=1)
    low_rows = jnp.stack([-signum * sine_vals, cosine], axis=1)
    return (jnp.stack([top_rows, low_rows], axis=0) * factor).astype(jnp.bfloat16)


def final_table(points):
    cosine, sine_vals = cos_sin(points)
    return (jnp.stack([cosine, -sine_vals], axis=0) / points).astype(jnp.bfloat16)


def twiddle_phase(first_rows, second_rows, period):
    index_grid = first_rows[:, None] * second_rows[None, :] % period
    phase_angle = index_grid.astype(jnp.float32) * (2.0 * math.pi / period)
    return (jnp.cos(phase_angle)[..., None], jnp.sin(phase_angle)[..., None])


def multiply(values, filters):
    chosen = values.astype(jnp.float32)
    weights = lax.all_gather(filters, "bat", axis=3, tiled=True).astype(jnp.float32)[:, None]
    real_part = chosen[0] * weights[0] - chosen[1] * weights[1]
    imag_part = chosen[0] * weights[1] + chosen[1] * weights[0]
    return jnp.stack([real_part, imag_part]).astype(jnp.bfloat16)


def body(tokens, filter_spectrum, skip_gain):
    seq_count = lax.axis_size("seq")
    device_index = lax.axis_index("seq")
    batch_rows, local_length, channels = tokens.shape
    rows_local = N1 // seq_count
    cols_local = N2 // seq_count
    period = N1 * N2
    laid_out = tokens.reshape(batch_rows, rows_local, N2, channels)
    columns = lax.all_to_all(laid_out, "seq", split_axis=2, concat_axis=1, tiled=True)
    first_section = jnp.einsum(
        "bnmc,nsk->sbkmc", columns, real_table(N1), preferred_element_type=jnp.float32
    )
    own_cols = device_index * cols_local + jnp.arange(cols_local, dtype=jnp.int32)
    cos_tw, sin_tw = twiddle_phase(jnp.arange(N1, dtype=jnp.int32), own_cols, period)
    real_part = first_section[0] * cos_tw + first_section[1] * sin_tw
    imag_part = first_section[1] * cos_tw - first_section[0] * sin_tw
    turned = jnp.stack([real_part, imag_part]).astype(jnp.bfloat16)
    rows_block = lax.all_to_all(turned, "seq", split_axis=2, concat_axis=3, tiled=True)
    spectrum = jnp.einsum(
        "rbknc,rnsj->sbkjc",
        rows_block,
        complex_table(N2, -1.0, 1.0),
        preferred_element_type=jnp.float32,
    ).astype(jnp.bfloat16)
    product = multiply(spectrum, filter_spectrum)
    back_section = jnp.einsum(
        "rbkjc,rjsn->sbknc",
        product,
        complex_table(N2, 1.0, 1.0 / N2),
        preferred_element_type=jnp.float32,
    )
    own_rows = device_index * rows_local + jnp.arange(rows_local, dtype=jnp.int32)
    cos_back, sin_back = twiddle_phase(own_rows, jnp.arange(N2, dtype=jnp.int32), period)
    real_back = back_section[0] * cos_back - back_section[1] * sin_back
    imag_back = back_section[0] * sin_back + back_section[1] * cos_back
    turned_back = jnp.stack([real_back, imag_back]).astype(jnp.bfloat16)
    mixed_cols = lax.all_to_all(turned_back, "seq", split_axis=3, concat_axis=2, tiled=True)
    filtered = jnp.einsum(
        "rbknc,rkm->bmnc", mixed_cols, final_table(N1), preferred_element_type=jnp.float32
    )
    result = (filtered + skip_gain * columns.astype(jnp.float32)).astype(jnp.bfloat16)
    restored = lax.all_to_all(result, "seq", split_axis=1, concat_axis=2, tiled=True)
    return restored.reshape(batch_rows, local_length, channels)


def solution(mesh):
    placed = (P("bat", "seq", None), P(None, "seq", None, "bat"), P())
    return jax.shard_map(
        body, mesh=mesh, in_specs=placed, out_specs=P("bat", "seq", None), check_vma=False
    )
```

profile of v0, /device:TPU:0, one launch (start us, length us, event | category | flops | bytes accessed | tf_op | source)
XLA Modules:
  0.0 355.4 jit_solution(5459308199365572002)
XLA Ops:
  6.5 4.1 %copy.31 = bf16[1,16,256,256]{3,1,0,2:T(8,128)(2,1)} copy(bf16[1,16,256,256]{3,2,1,0:T(8,128)(2,1)} %bitcast.109) | data formatting | bytes 4194304 | tf_op jit(solution)/shard_map/reshape | solution.py:57
  10.6 8.3 %all-to-all-start = ((bf16[1,16,256,256]{3,1,0,2:T(8,128)(2,1)}), bf16[1,16,256,256]{3,1,0,2:T(8,128)(2,1)S(1)}, u32[]{:S(2)}, u32[]{:S(2)}) async-start(bf16[1,16,256,256]{3,1,0,2:T(8,128)(2,1)} %copy.31), calls=%async_computation | async-start | bytes 4194304 | tf_op jit(solution)/shard_map/all_to_all | solution.py:58
  19.0 1.1 negate_convert_fusion
  20.2 41.8 %all-to-all-done = bf16[1,16,256,256]{3,1,0,2:T(8,128)(2,1)S(1)} async-done(((bf16[1,16,256,256]{3,1,0,2:T(8,128)(2,1)}), bf16[1,16,256,256]{3,1,0,2:T(8,128)(2,1)S(1)}, u32[]{:S(2)}, u32[]{:S(2)}) %all-to-all-start) | async-done | bytes 2097184 | tf_op jit(solution)/shard_map/all_to_all | solution.py:58
  62.0 0.7 copy.32
  62.7 1.2 copy.33
  63.9 1.3 fusion.18
  65.2 1.5 fusion.8
  67.0 4.3 %copy.34 = bf16[2,1,256,16,256]{4,3,1,0,2:T(8,128)(2,1)} copy(bf16[2,1,256,16,256]{4,2,3,1,0:T(8,128)(2,1)S(1)} %pad_maximum_fusion) | data formatting | bytes 8388608 | tf_op jit(solution)/shard_map/stack | solution.py:66
  71.3 10.1 %all-to-all-start.1 = ((bf16[2,1,256,16,256]{4,3,1,0,2:T(8,128)(2,1)}), bf16[2,1,256,16,256]{4,3,1,0,2:T(8,128)(2,1)}, u32[]{:S(2)}, u32[]{:S(2)}) async-start(bf16[2,1,256,16,256]{4,3,1,0,2:T(8,128)(2,1)} %copy.34), calls=%async_computation.1 | async-start | bytes 8388608 | tf_op jit(solution)/shard_map/all_to_all | solution.py:67
  82.1 1.0 fusion.38
  83.1 1.0 fusion.37
  84.1 1.0 broadcast_multiply_fusion
  85.1 0.9 maximum_bitcast_fusion
  86.2 11.6 %all-gather.2.cloned.1.call-done = bf16[2,16,256,256]{3,2,1,0:T(8,128)(2,1)} async-done(((bf16[2,16,256,128]{3,2,1,0:T(8,128)(2,1)}), bf16[2,16,256,256]{3,2,1,0:T(8,128)(2,1)}) %all-gather.2.cloned.1.call-update) | async-done | bytes 4194320 | tf_op jit(solution)/shard_map/all_gather | solution.py:44
  97.8 6.5 %convert_element_type.144 = f32[2,16,256,256]{3,2,1,0:T(8,128)} convert(bf16[2,16,256,256]{3,2,1,0:T(8,128)(2,1)} %all-gather.2.cloned.1.call-done) | non-fusion elementwise | flops 2097152 | bytes 12582912 | tf_op jit(solution)/shard_map/convert_element_type | solution.py:44
  104.3 55.5 %all-to-all-done.1 = bf16[2,1,256,16,256]{4,3,1,0,2:T(8,128)(2,1)} async-done(((bf16[2,1,256,16,256]{4,3,1,0,2:T(8,128)(2,1)}), bf16[2,1,256,16,256]{4,3,1,0,2:T(8,128)(2,1)}, u32[]{:S(2)}, u32[]{:S(2)}) %all-to-all-start.1) | async-done | bytes 4194336 | tf_op jit(solution)/shard_map/all_to_all | solution.py:67
  159.8 2.7 copy.35
  162.5 2.4 convert_bitcast_fusion.1
  164.9 1.1 slice-done.1
  166.0 1.8 subtract_convert_fusion.1
  167.8 2.4 fusion.5
  170.2 1.5 subtract_convert_fusion
  172.0 4.4 %copy.40 = bf16[2,1,16,256,256]{4,2,0,1,3:T(8,128)(2,1)} copy(bf16[2,1,16,256,256]{4,3,2,0,1:T(8,128)(2,1)S(1)} %pad_maximum_fusion.2) | data formatting | bytes 8388608 | tf_op jit(solution)/shard_map/stack | solution.py:85
  176.4 19.4 %all-to-all-start.2 = ((bf16[2,1,16,256,256]{4,2,0,1,3:T(8,128)(2,1)}), bf16[2,1,16,256,256]{4,2,0,1,3:T(8,128)(2,1)}, u32[]{:S(2)}, u32[]{:S(2)}) async-start(bf16[2,1,16,256,256]{4,2,0,1,3:T(8,128)(2,1)} %copy.40), calls=%async_computation.2 | async-start | bytes 8388608 | tf_op jit(solution)/shard_map/all_to_all | solution.py:86
  195.8 1.0 sine_negate_fusion
  196.9 77.4 %all-to-all-done.2 = bf16[2,1,16,256,256]{4,2,0,1,3:T(8,128)(2,1)} async-done(((bf16[2,1,16,256,256]{4,2,0,1,3:T(8,128)(2,1)}), bf16[2,1,16,256,256]{4,2,0,1,3:T(8,128)(2,1)}, u32[]{:S(2)}, u32[]{:S(2)}) %all-to-all-start.2) | async-done | bytes 4194336 | tf_op jit(solution)/shard_map/all_to_all | solution.py:86
  274.3 2.7 copy.41
  277.0 1.3 fusion.10
  278.4 1.2 copy.42
  279.6 67.4 %all_to_all.60 = bf16[1,256,16,256]{3,2,0,1:T(8,128)(2,1)S(1)} all-to-all(bf16[1,256,16,256]{3,2,0,1:T(8,128)(2,1)S(1)} %copy.42), channel_id=1, replica_groups=mesh['seq'=16,'bat'=2] {'seq'}, dimensions={1} | all-to-all | bytes 4194304 | tf_op jit(solution)/shard_map/all_to_all | solution.py:91
  347.0 1.5 copy.43
  (16 shorter events, 1.9 us)
Async XLA Ops:
  10.6 51.4 %all-to-all-start = ((bf16[1,16,256,256]{3,1,0,2:T(8,128)(2,1)}), bf16[1,16,256,256]{3,1,0,2:T(8,128)(2,1)S(1)}, u32[]{:S(2)}, u32[]{:S(2)}) async-start(bf16[1,16,256,256]{3,1,0,2:T(8,128)(2,1)} %copy.31), calls=%async_computation | async-start | bytes 4194304 | tf_op jit(solution)/shard_map/all_to_all | solution.py:58
  71.3 88.5 %all-to-all-start.1 = ((bf16[2,1,256,16,256]{4,3,1,0,2:T(8,128)(2,1)}), bf16[2,1,256,16,256]{4,3,1,0,2:T(8,128)(2,1)}, u32[]{:S(2)}, u32[]{:S(2)}) async-start(bf16[2,1,256,16,256]{4,3,1,0,2:T(8,128)(2,1)} %copy.34), calls=%async_computation.1 | async-start | bytes 8388608 | tf_op jit(solution)/shard_map/all_to_all | solution.py:67
  81.4 16.4 %all-gather.2.cloned.1.call-start = ((), (), s32[]{:S(2)}) async-start(), calls=%async_computation.4 | async-start | bytes 6291456 | tf_op jit(solution)/shard_map/all_gather | solution.py:44
  162.5 2.4 slice-start
  162.5 3.5 slice-start.1
  166.0 1.8 copy-start
  176.4 97.9 %all-to-all-start.2 = ((bf16[2,1,16,256,256]{4,2,0,1,3:T(8,128)(2,1)}), bf16[2,1,16,256,256]{4,2,0,1,3:T(8,128)(2,1)}, u32[]{:S(2)}, u32[]{:S(2)}) async-start(bf16[2,1,16,256,256]{4,2,0,1,3:T(8,128)(2,1)} %copy.40), calls=%async_computation.2 | async-start | bytes 8388608 | tf_op jit(solution)/shard_map/all_to_all | solution.py:86
  274.3 2.8 copy-start.1
Sparse Core Ops, SparseCore 0:
  83.7 13.9 all-gather.1
where the time goes:
time: 356 us; the launch traced here: 355 us
  waiting for transfers between devices  187 us (53%)
  blocking collectives  67.4 us (19%)
  starting transfers between devices  38 us (11%)
  local copies, waits for them, and re-layouts  24 us (7%)
  other arithmetic  18.3 us (5%)
  between operations  13.6 us (4%)
  matrix products  7.29 us (2%)
    all_to_all x1, waiting for transfers between devices, body(): lax.all_to_all(turned_back, 'seq', split_axis=3, concat_axis=2, tiled=True)  77.4 us
    all_to_all x1, blocking collectives, body(): lax.all_to_all(result, 'seq', split_axis=1, concat_axis=2, tiled=True)  67.4 us
    all_to_all x1, waiting for transfers between devices, body(): lax.all_to_all(turned, 'seq', split_axis=2, concat_axis=3, tiled=True)  55.5 us
    all_to_all x1, waiting for transfers between devices, body(): lax.all_to_all(laid_out, 'seq', split_axis=2, concat_axis=1, tiled=True)  41.8 us
    all_to_all x1, starting transfers between devices, body(): lax.all_to_all(turned_back, 'seq', split_axis=3, concat_axis=2, tiled=True)  19.4 us
    all_gather x1, waiting for transfers between devices, multiply(): lax.all_gather(filters, 'bat', axis=3, tiled=True).astype(jnp.float32)  11.6 us
    all_to_all x1, starting transfers between devices, body(): lax.all_to_all(turned, 'seq', split_axis=2, concat_axis=3, tiled=True)  10.1 us
    all_to_all x1, starting transfers between devices, body(): lax.all_to_all(laid_out, 'seq', split_axis=2, concat_axis=1, tiled=True)  8.34 us
  transfers between devices with their start and end apart: 4, of which 4 were waited for; matrix products, arithmetic and copies ran while one was open for 4% of the time, Pallas kernels for 0%

commit v1 on v0

v1 whole, which is shorter than its diff:
```python
import functools
import math

import jax
import jax.numpy as jnp
from jax import lax
from jax.experimental import pallas as pl
from jax.experimental.pallas import tpu as pltpu
from jax.sharding import PartitionSpec as P

N1 = 256
N2 = 256


def cos_sin(points):
    steps_range = jnp.arange(points, dtype=jnp.int32)
    index_grid = steps_range[:, None] * steps_range[None, :] % points
    phase_angle = index_grid.astype(jnp.float32) * (2.0 * math.pi / points)
    return (jnp.cos(phase_angle), jnp.sin(phase_angle))


def dft_tables():
    cos1, sin1 = cos_sin(N1)
    cos2, sin2 = cos_sin(N2)
    forward_rows = jnp.stack([cos1, -sin1]).astype(jnp.bfloat16)
    top = jnp.concatenate([cos2, -sin2], axis=1)
    low = jnp.concatenate([sin2, cos2], axis=1)
    forward_cols = jnp.stack([top, low]).astype(jnp.bfloat16)
    top = jnp.concatenate([cos2, sin2], axis=1)
    low = jnp.concatenate([-sin2, cos2], axis=1)
    inverse_cols = (jnp.stack([top, low]) / N2).astype(jnp.bfloat16)
    inverse_rows = (jnp.stack([cos1, -sin1]) / N1).astype(jnp.bfloat16)
    period = N1 * N2
    rows = jnp.arange(N1, dtype=jnp.int32)
    cols = jnp.arange(N2, dtype=jnp.int32)
    angle = (rows[:, None] * cols[None, :] % period).astype(jnp.float32) * (2.0 * math.pi / period)
    twiddle = jnp.stack([jnp.cos(angle), jnp.sin(angle)])
    return forward_rows, twiddle, forward_cols, inverse_cols, inverse_rows


def dot(left, right):
    return jnp.dot(left, right, preferred_element_type=jnp.float32)


def span(block, step, held):
    if held <= step:
        return pl.ds(block * step // held, step // held), pl.ds(0, held)
    return pl.ds(block * step // held, 1), pl.ds(block * step % held, step)


def convolve_kernel(blocks, gain, tokens, filters, rows_t, twiddle, cols_t, back_t, final_t, out, turned_back):
    signal = tokens[0, :, 0].reshape(N1, N2)
    step = N1 // blocks
    for block in range(blocks):
        rows = pl.ds(block * step, step)
        real = dot(rows_t[0, rows], signal)
        imag = dot(rows_t[1, rows], signal)
        cosine = twiddle[0, rows]
        sine = twiddle[1, rows]
        turned_real = (real * cosine + imag * sine).astype(jnp.bfloat16)
        turned_imag = (imag * cosine - real * sine).astype(jnp.bfloat16)
        spectrum = dot(turned_real, cols_t[0]) + dot(turned_imag, cols_t[1])
        spectrum = spectrum.astype(jnp.bfloat16).astype(jnp.float32)
        parts, inner = span(block, step, filters.shape[3])
        weight_real = filters[parts, 0, 0, inner].reshape(step, N2).astype(jnp.float32)
        weight_imag = filters[parts, 0, 1, inner].reshape(step, N2).astype(jnp.float32)
        spec_real, spec_imag = spectrum[:, :N2], spectrum[:, N2:]
        prod_real = (spec_real * weight_real - spec_imag * weight_imag).astype(jnp.bfloat16)
        prod_imag = (spec_real * weight_imag + spec_imag * weight_real).astype(jnp.bfloat16)
        back = dot(prod_real, back_t[0]) + dot(prod_imag, back_t[1])
        back_real, back_imag = back[:, :N2], back[:, N2:]
        turned_back[0, rows] = (back_real * cosine - back_imag * sine).astype(jnp.bfloat16)
        turned_back[1, rows] = (back_real * sine + back_imag * cosine).astype(jnp.bfloat16)
    weight = gain[pl.program_id(0)]
    for block in range(blocks):
        rows = pl.ds(block * step, step)
        parts, inner = span(block, step, tokens.shape[3])
        filtered = dot(final_t[0, rows], turned_back[0]) + dot(final_t[1, rows], turned_back[1])
        direct = tokens[0, parts, 0, inner].reshape(step, N2).astype(jnp.float32)
        result = (filtered + weight * direct).astype(jnp.bfloat16)
        out[0, parts, 0, inner] = result.reshape(parts.size, inner.size, N2)


def convolve(tokens, filters, gain, tables, start, count):
    batch, pieces, _, rows, _ = tokens.shape
    blocks = 2

    def whole(array):
        return pl.BlockSpec(array.shape, lambda c, b: (0,) * array.ndim)

    block = (1, pieces, 1, rows, N2)
    return pl.pallas_call(
        functools.partial(convolve_kernel, blocks),
        grid=(count, batch),
        in_specs=[
            pl.BlockSpec(memory_space=pltpu.SMEM),
            pl.BlockSpec(block, lambda c, b: (b, 0, c + start, 0, 0)),
            pl.BlockSpec((pieces, 1, 2, rows, N2), lambda c, b: (0, c + start, 0, 0, 0)),
            *[whole(table) for table in tables],
        ],
        out_specs=pl.BlockSpec(block, lambda c, b: (b, 0, c, 0, 0)),
        out_shape=jax.ShapeDtypeStruct((batch, pieces, count, rows, N2), jnp.bfloat16),
        scratch_shapes=[pltpu.VMEM((2, N1, N2), jnp.bfloat16)],
        name="convolve",
    )(gain[start : start + count], tokens, filters, *tables)


def body(tokens, filter_spectrum, skip_gain):
    seq_count = lax.axis_size("seq")
    bat_count = lax.axis_size("bat")
    seq_index = lax.axis_index("seq")
    bat_index = lax.axis_index("bat")
    batch_rows, local_length, channels = tokens.shape
    rows_local = N1 // seq_count
    spread = channels % (seq_count * bat_count) == 0
    if spread:
        axes, groups = ("bat", "seq"), bat_count
        own = channels // (seq_count * bat_count)
        first = (bat_index * seq_count + seq_index) * own
        sequences = batch_rows * bat_count
    else:
        axes, groups = ("seq",), 1
        own = channels // seq_count
        first = seq_index * own
        sequences = batch_rows
        filter_spectrum = lax.all_gather(filter_spectrum, "bat", axis=3, tiled=True)
    ranks = seq_count * groups

    laid = tokens.reshape(batch_rows, rows_local, N2, channels).transpose(3, 0, 1, 2)
    laid = laid.reshape(ranks, own, batch_rows, rows_local, N2)
    columns = lax.all_to_all(laid, axes, split_axis=0, concat_axis=0, tiled=True)
    columns = columns.reshape(groups, seq_count, own, batch_rows, rows_local, N2)
    if batch_rows == 1:
        columns = columns.reshape(sequences, seq_count, own, rows_local, N2)
    else:
        columns = columns.transpose(0, 3, 1, 2, 4, 5).reshape(sequences, seq_count, own, rows_local, N2)

    spread_filters = filter_spectrum.transpose(3, 0, 1, 2).reshape(seq_count, own, 2, rows_local, N2)
    filters = lax.all_to_all(spread_filters, "seq", split_axis=0, concat_axis=0, tiled=True)
    gain = lax.dynamic_slice(skip_gain, (first,), (own,))
    tables = dft_tables()
    aligned = rows_local % 16 == 0
    if not aligned:
        columns = columns.transpose(0, 2, 1, 3, 4).reshape(sequences, 1, own, N1, N2)
        filters = filters.transpose(1, 2, 0, 3, 4).reshape(1, own, 2, N1, N2)
    chunks = 2 if own % 2 == 0 else 1
    count = own // chunks
    results = []
    for chunk in range(chunks):
        result = convolve(columns, filters, gain, tables, chunk * count, count)
        if not aligned:
            result = result.reshape(sequences, count, seq_count, rows_local, N2).transpose(0, 2, 1, 3, 4)
        if batch_rows == 1:
            result = result.reshape(ranks, count, 1, rows_local, N2)
        else:
            result = result.reshape(groups, batch_rows, seq_count, count, rows_local, N2)
            result = result.transpose(0, 2, 3, 1, 4, 5).reshape(ranks, count, batch_rows, rows_local, N2)
        results.append(lax.all_to_all(result, axes, split_axis=0, concat_axis=0, tiled=True))
    restored = jnp.concatenate(results, axis=1).reshape(channels, batch_rows, rows_local, N2)
    return restored.transpose(1, 2, 3, 0).reshape(batch_rows, local_length, channels)


def solution(mesh):
    placed = (P("bat", "seq", None), P(None, "seq", None, "bat"), P())
    return jax.shard_map(
        body, mesh=mesh, in_specs=placed, out_specs=P("bat", "seq", None), check_vma=False
    )
```

time: 356 us -> 194 us (0.54)
  waiting for transfers between devices: 187 us -> 93.8 us
  blocking collectives: 67.4 us -> 30.7 us
  Pallas kernels: 0 us -> 24.5 us
  starting transfers between devices: 38 us -> 20.1 us
  between operations: 13.6 us -> 0.08 us
  local copies, waits for them, and re-layouts: 24 us -> 13.8 us
  other arithmetic: 18.3 us -> 10.6 us
  matrix products: 7.29 us -> 0 us
    all_to_all x3, waiting for transfers between devices: 175 us -> 93.8 us  [the longest x1 39.5 us: body(): lax.all_to_all(laid, axes, split_axis=0, concat_axis=0, tiled=True)]
    all_to_all x1, blocking collectives: 67.4 us -> 30.7 us  [body(): lax.all_to_all(result, axes, split_axis=0, concat_axis=0, tiled=True)]
    pallas_call x0 -> x2, Pallas kernels: none -> 24.5 us  [convolve(): pl.pallas_call(functools.partial(convolve_kernel, blocks), grid=(count, b...]
    all_to_all x3, starting transfers between devices: 37.8 us -> 20.1 us  [the longest x1 9.11 us: body(): lax.all_to_all(laid, axes, split_axis=0, concat_axis=0, tiled=True)]
    all_gather x1 -> x0, waiting for transfers between devices: 11.6 us -> none  [multiply(): lax.all_gather(filters, 'bat', axis=3, tiled=True).astype(jnp.float32)]
    all_to_all x5 -> x0, local copies, waits for them, and re-layouts: 8.92 us -> none  [the longest x1 2.75 us: body(): lax.all_to_all(turned_back, 'seq', split_axis=3, concat_axis=2, tiled=True)]
    another operation x2 -> x0, local copies, waits for them, and re-layouts: 8.71 us -> none  [the longest x1 4.4 us: body(): turned_back = jnp.stack([real_back, imag_back]).astype(jnp.bfloat16)]
    transpose x0 -> x2, local copies, waits for them, and re-layouts: none -> 7.33 us  [the longest x1 4.6 us: body(): filter_spectrum.transpose(3, 0, 1, 2)]
  transfers between devices with their start and end apart: 4 -> 3, of which waited for: 4 -> 3; matrix products, arithmetic and copies ran while one was open for 4% -> 8% of each run, Pallas kernels for 0% -> 6%
where the time goes in v1:
time: 194 us
  waiting for transfers between devices  93.8 us (48%)
  blocking collectives  30.7 us (16%)
  Pallas kernels  24.5 us (13%)
  starting transfers between devices  20.1 us (10%)
  local copies, waits for them, and re-layouts  13.8 us (7%)
  other arithmetic  10.6 us (5%)
    all_to_all x1, waiting for transfers between devices, body(): lax.all_to_all(laid, axes, split_axis=0, concat_axis=0, tiled=True)  39.5 us
    all_to_all x1, waiting for transfers between devices, body(): lax.all_to_all(spread_filters, 'seq', split_axis=0, concat_axis=0, tiled=...  38.5 us
    all_to_all x1, blocking collectives, body(): lax.all_to_all(result, axes, split_axis=0, concat_axis=0, tiled=True)  30.7 us
    pallas_call x2, Pallas kernels, convolve(): pl.pallas_call(functools.partial(convolve_kernel, blocks), grid=(count, b...  24.5 us
    all_to_all x1, waiting for transfers between devices, body(): lax.all_to_all(result, axes, split_axis=0, concat_axis=0, tiled=True)  15.7 us
    all_to_all x1, starting transfers between devices, body(): lax.all_to_all(laid, axes, split_axis=0, concat_axis=0, tiled=True)  9.11 us
    all_to_all x1, starting transfers between devices, body(): lax.all_to_all(spread_filters, 'seq', split_axis=0, concat_axis=0, tiled=...  8.34 us
    transpose x1, local copies, waits for them, and re-layouts, body(): filter_spectrum.transpose(3, 0, 1, 2)  4.6 us
  transfers between devices with their start and end apart: 3, of which 3 were waited for; matrix products, arithmetic and copies ran while one was open for 8% of the time, Pallas kernels for 6%

profile of v1, /device:TPU:0, one launch (start us, length us, event | category | flops | bytes accessed | tf_op | source)
XLA Modules:
  0.0 193.5 jit_solution(3191810350155969412)
XLA Ops:
  0.0 4.6 %copy.8 = bf16[128,2,16,256]{3,2,1,0:T(8,128)(2,1)} copy(bf16[128,2,16,256]{0,3,2,1:T(8,128)(2,1)} %bitcast.30) | data formatting | bytes 4194304 | tf_op jit(solution)/shard_map/transpose | solution.py:138
  4.6 8.3 %all-to-all-start.1 = ((bf16[16,8,2,16,256]{4,3,2,1,0:T(8,128)(2,1)}), bf16[16,8,2,16,256]{4,3,2,1,0:T(8,128)(2,1)S(1)}, u32[]{:S(2)}, u32[]{:S(2)}) async-start(bf16[16,8,2,16,256]{4,3,2,1,0:T(8,128)(2,1)} %bitcast.26), calls=%async_computation.1 | async-start | bytes 4194304 | tf_op jit(solution)/shard_map/all_to_all | solution.py:139
  12.9 4.5 %copy.7 = bf16[1,16,256,256]{2,1,3,0:T(8,128)(2,1)} copy(bf16[1,16,256,256]{3,2,1,0:T(8,128)(2,1)} %bitcast.31) | data formatting | bytes 4194304 | tf_op jit(solution)/shard_map/reshape | solution.py:129
  17.4 38.5 %all-to-all-done.1.filters = bf16[16,8,2,16,256]{4,3,2,1,0:T(8,128)(2,1)S(1)} async-done(((bf16[16,8,2,16,256]{4,3,2,1,0:T(8,128)(2,1)}), bf16[16,8,2,16,256]{4,3,2,1,0:T(8,128)(2,1)S(1)}, u32[]{:S(2)}, u32[]{:S(2)}) %all-to-all-start.1) | async-done | bytes 2097184 | tf_op jit(solution)/shard_map/all_to_all | solution.py:139
  56.0 0.0 copy-start
  56.0 0.0 copy-start.1
  56.0 1.3 copy-done
  57.3 9.1 %all-to-all-start = ((bf16[32,8,1,16,256]{4,3,1,2,0:T(8,128)(2,1)}), bf16[32,8,1,16,256]{4,3,1,2,0:T(8,128)(2,1)}, u32[]{:S(2)}, u32[]{:S(2)}) async-start(bf16[32,8,1,16,256]{4,3,1,2,0:T(8,128)(2,1)} %bitcast.25), calls=%async_computation | async-start | bytes 4194304 | tf_op jit(solution)/shard_map/all_to_all | solution.py:131
  66.4 0.0 copy-done.1
  66.4 0.1 dynamic_slice.3
  66.5 1.0 fusion.27
  67.5 1.0 fusion.21
  68.5 1.0 fusion.22
  69.5 1.0 sine_negate_fusion
  70.5 0.8 fusion.1.rows_t
  71.3 0.8 multiply_convert_fusion.final_t
  72.0 1.0 fusion.23
  73.1 1.0 fusion.19
  74.1 0.9 pad_maximum_fusion.2.twiddle
  75.0 0.9 pad_maximum_fusion.3.cols_t
  75.9 0.1 maximum_bitcast_fusion
  76.0 0.9 fusion.back_t
  76.9 0.6 fusion.28
  77.5 39.5 %all-to-all-done = bf16[32,8,1,16,256]{4,3,1,2,0:T(8,128)(2,1)} async-done(((bf16[32,8,1,16,256]{4,3,1,2,0:T(8,128)(2,1)}), bf16[32,8,1,16,256]{4,3,1,2,0:T(8,128)(2,1)}, u32[]{:S(2)}, u32[]{:S(2)}) %all-to-all-start) | async-done | bytes 2097184 | tf_op jit(solution)/shard_map/all_to_all | solution.py:131
  117.0 12.2 %convolve.3 = bf16[2,16,4,16,256]{4,3,2,1,0:T(8,128)(2,1)} custom-call(f32[4]{0:T(128)} %get-tuple-element.10.gain, bf16[2,16,8,16,256]{4,3,2,1,0:T(8,128)(2,1)} %bitcast.3.tokens, bf16[16,8,2,16,256]{4,3,2,1,0:T(8,128)(2,1)} %copy-done, bf16[2,256,256]{2,1,0:T(8,128)(2,1)} %fusion.1.rows_t, f32[2,256,256]{2,1,0:T(8,128)} %pad_maximum_fusion.2.twiddle, ...), custom_call_target="tpu_custom_call" | custom-call | tf_op jit(solution)/shard_map/convolve/pallas_call | solution.py:92
  129.2 2.6 %all-to-all-start.3 = ((bf16[32,4,1,16,256]{4,3,1,2,0:T(8,128)(2,1)}), bf16[32,4,1,16,256]{4,3,1,2,0:T(8,128)(2,1)S(1)}, u32[]{:S(2)}, u32[]{:S(2)}) async-start(bf16[32,4,1,16,256]{4,3,1,2,0:T(8,128)(2,1)} %bitcast.28), calls=%async_computation.3 | async-start | bytes 2097152 | tf_op jit(solution)/shard_map/all_to_all | solution.py:158
  131.9 12.3 %convolve.2 = bf16[2,16,4,16,256]{4,3,2,1,0:T(8,128)(2,1)} custom-call(f32[4]{0:T(128)} %get-tuple-element.9.gain, bf16[2,16,8,16,256]{4,3,2,1,0:T(8,128)(2,1)} %bitcast.3.tokens, bf16[16,8,2,16,256]{4,3,2,1,0:T(8,128)(2,1)} %copy-done, bf16[2,256,256]{2,1,0:T(8,128)(2,1)} %fusion.1.rows_t, f32[2,256,256]{2,1,0:T(8,128)} %pad_maximum_fusion.2.twiddle, ...), custom_call_target="tpu_custom_call" | custom-call | tf_op jit(solution)/shard_map/convolve/pallas_call | solution.py:92
  144.2 15.7 %all-to-all-done.3 = bf16[32,4,1,16,256]{4,3,1,2,0:T(8,128)(2,1)S(1)} async-done(((bf16[32,4,1,16,256]{4,3,1,2,0:T(8,128)(2,1)}), bf16[32,4,1,16,256]{4,3,1,2,0:T(8,128)(2,1)S(1)}, u32[]{:S(2)}, u32[]{:S(2)}) %all-to-all-start.3) | async-done | bytes 1048608 | tf_op jit(solution)/shard_map/all_to_all | solution.py:158
  159.9 30.7 %all_to_all.20 = bf16[32,4,1,16,256]{4,3,1,2,0:T(8,128)(2,1)S(1)} all-to-all(bf16[32,4,1,16,256]{4,3,1,2,0:T(8,128)(2,1)} %bitcast.29), channel_id=1, replica_groups=mesh['seq'=16,'bat'=2] {'bat','seq'}, dimensions={0} | all-to-all | bytes 2097152 | tf_op jit(solution)/shard_map/all_to_all | solution.py:158
  190.6 0.2 pad_maximum_fusion
  190.8 2.7 %copy.11 = bf16[1,16,256,256]{3,2,1,0:T(8,128)(2,1)} copy(bf16[1,16,256,256]{2,1,3,0:T(8,128)(2,1)S(1)} %bitcast.27) | data formatting | bytes 4194304 | tf_op jit(solution)/shard_map/transpose | solution.py:160
  (1 shorter events, 0.0 us)
Async XLA Ops:
  4.6 51.4 %all-to-all-start.1 = ((bf16[16,8,2,16,256]{4,3,2,1,0:T(8,128)(2,1)}), bf16[16,8,2,16,256]{4,3,2,1,0:T(8,128)(2,1)S(1)}, u32[]{:S(2)}, u32[]{:S(2)}) async-start(bf16[16,8,2,16,256]{4,3,2,1,0:T(8,128)(2,1)} %bitcast.26), calls=%async_computation.1 | async-start | bytes 4194304 | tf_op jit(solution)/shard_map/all_to_all | solution.py:139
  56.0 1.3 copy-start
  56.0 10.5 %copy-start.1 = (f32[256]{0:T(256)S(1)}, f32[256]{0:T(256)}, u32[]{:S(2)}) copy-start(f32[256]{0:T(256)} %param.5) | copy-start | bytes 3076
  57.3 59.7 %all-to-all-start = ((bf16[32,8,1,16,256]{4,3,1,2,0:T(8,128)(2,1)}), bf16[32,8,1,16,256]{4,3,1,2,0:T(8,128)(2,1)}, u32[]{:S(2)}, u32[]{:S(2)}) async-start(bf16[32,8,1,16,256]{4,3,1,2,0:T(8,128)(2,1)} %bitcast.25), calls=%async_computation | async-start | bytes 4194304 | tf_op jit(solution)/shard_map/all_to_all | solution.py:131
  129.2 30.7 %all-to-all-start.3 = ((bf16[32,4,1,16,256]{4,3,1,2,0:T(8,128)(2,1)}), bf16[32,4,1,16,256]{4,3,1,2,0:T(8,128)(2,1)S(1)}, u32[]{:S(2)}, u32[]{:S(2)}) async-start(bf16[32,4,1,16,256]{4,3,1,2,0:T(8,128)(2,1)} %bitcast.28), calls=%async_computation.3 | async-start | bytes 2097152 | tf_op jit(solution)/shard_map/all_to_all | solution.py:158

commit v2 on v1

--- a/solution.py
+++ b/solution.py
@@ -8,6 +8,7 @@
 from jax.experimental.pallas import tpu as pltpu
 from jax.sharding import PartitionSpec as P
 
+
 N1 = 256
 N2 = 256
 
@@ -19,8 +20,10 @@
     return (jnp.cos(phase_angle), jnp.sin(phase_angle))
 
 
-def dft_tables():
-    cos1, sin1 = cos_sin(N1)
+def dft_tables(order):
+    index_grid = order[:, None] * order[None, :] % N1
+    phase_angle = index_grid.astype(jnp.float32) * (2.0 * math.pi / N1)
+    cos1, sin1 = jnp.cos(phase_angle), jnp.sin(phase_angle)
     cos2, sin2 = cos_sin(N2)
     forward_rows = jnp.stack([cos1, -sin1]).astype(jnp.bfloat16)
     top = jnp.concatenate([cos2, -sin2], axis=1)
@@ -31,9 +34,8 @@
     inverse_cols = (jnp.stack([top, low]) / N2).astype(jnp.bfloat16)
     inverse_rows = (jnp.stack([cos1, -sin1]) / N1).astype(jnp.bfloat16)
     period = N1 * N2
-    rows = jnp.arange(N1, dtype=jnp.int32)
     cols = jnp.arange(N2, dtype=jnp.int32)
-    angle = (rows[:, None] * cols[None, :] % period).astype(jnp.float32) * (2.0 * math.pi / period)
+    angle = (order[:, None] * cols[None, :] % period).astype(jnp.float32) * (2.0 * math.pi / period)
     twiddle = jnp.stack([jnp.cos(angle), jnp.sin(angle)])
     return forward_rows, twiddle, forward_cols, inverse_cols, inverse_rows
 
@@ -105,7 +107,7 @@
     )(gain[start : start + count], tokens, filters, *tables)
 
 
-def body(tokens, filter_spectrum, skip_gain):
+def spread_body(tokens, filter_spectrum, skip_gain):
     seq_count = lax.axis_size("seq")
     bat_count = lax.axis_size("bat")
     seq_index = lax.axis_index("seq")
@@ -138,7 +140,7 @@
     spread_filters = filter_spectrum.transpose(3, 0, 1, 2).reshape(seq_count, own, 2, rows_local, N2)
     filters = lax.all_to_all(spread_filters, "seq", split_axis=0, concat_axis=0, tiled=True)
     gain = lax.dynamic_slice(skip_gain, (first,), (own,))
-    tables = dft_tables()
+    tables = dft_tables(jnp.arange(N1, dtype=jnp.int32))
     aligned = rows_local % 16 == 0
     if not aligned:
         columns = columns.transpose(0, 2, 1, 3, 4).reshape(sequences, 1, own, N1, N2)
@@ -160,6 +162,342 @@
     return restored.transpose(1, 2, 3, 0).reshape(batch_rows, local_length, channels)
 
 
+def relative_rows(index, count, held):
+    half = count // 2
+    near = index // half * half + jnp.arange(half, dtype=jnp.int32)
+    far = index ^ (half + jnp.arange(half, dtype=jnp.int32))
+    pieces = jnp.concatenate([near, far])
+    return (pieces[:, None] * held + jnp.arange(held, dtype=jnp.int32)[None, :]).reshape(-1)
+
+
+PAD = 8
+LANES = 4
+
+
+def blocks_of(half, place, kept, far):
+    index, base = place[0], place[1]
+    near = [(base + block, kept.at[block]) for block in range(half)]
+    return near + [(index ^ (half + step), ref) for step, ref in enumerate(far)]
+
+
+def put_rows(scratch, at, turned):
+    for side in range(2):
+        scratch[side, at] = turned[:, side * 128 : side * 128 + 128]
+
+
+def send_rows(scratch, start, stride, message, slot):
+    rows = message.shape[1]
+    for side in range(2):
+        piece = scratch[side, pl.ds(start, rows, stride=stride)]
+        message[slot, :, side * 128 : side * 128 + 128] = piece.astype(jnp.bfloat16)
+
+
+def pack_tokens_kernel(half, groups, place, tokens, kept, *rest):
+    far, scratch = rest[:half], rest[half]
+    step = pl.program_id(0)
+    rows, _, channels = tokens.shape
+    stride = channels + PAD
+    own = channels // (groups * 2 * half)
+    for row in range(rows):
+        at = pl.ds(pl.multiple_of((step * rows + row) * stride, PAD), channels)
+        put_rows(scratch, at, tokens[row].T.astype(jnp.float32))
+
+    @pl.when(step == pl.num_programs(0) - 1)
+    def _():
+        for target, message in blocks_of(half, place, kept, far):
+
+            def fill(lane, _):
+                for group in range(groups):
+                    start = group * (channels // groups) + target * own + lane
+                    send_rows(scratch, start, stride, message, group * own + lane)
+                return 0
+
+            lax.fori_loop(0, own, fill, 0, unroll=2)
+
+
+def pack_filters_kernel(half, place, filters, kept, *rest):
+    far, scratch = rest[:half], rest[half]
+    step = pl.program_id(0)
+    _, rows, _, held = filters.shape
+    stride = held + PAD
+    total = rows * pl.num_programs(0)
+    own = held // (2 * half)
+    for part in range(2):
+        for row in range(rows):
+            at = pl.ds(pl.multiple_of((part * total + step * rows + row) * stride, PAD), held)
+            put_rows(scratch, at, filters[part, row].T.astype(jnp.float32))
+
+    @pl.when(step == pl.num_programs(0) - 1)
+    def _():
+        for target, message in blocks_of(half, place, kept, far):
+
+            def fill(lane, _):
+                for part in range(2):
+                    start = part * total * stride + target * own + lane
+                    send_rows(scratch, start, stride, message, 2 * lane + part)
+                return 0
+
+            lax.fori_loop(0, own, fill, 0, unroll=2)
+
+
+VMEM = pl.BlockSpec(memory_space=pltpu.VMEM)
+SMEM = pl.BlockSpec(memory_space=pltpu.SMEM)
+
+
+def message_shapes(half, slots, rows):
+    message = jax.ShapeDtypeStruct((slots, rows, N2), jnp.bfloat16)
+    return [jax.ShapeDtypeStruct((half, slots, rows, N2), jnp.bfloat16)] + [message] * half
+
+
+def pack_tokens(place, tokens, half, groups):
+    rows, _, channels = tokens.shape
+    steps = 2
+    return pl.pallas_call(
+        functools.partial(pack_tokens_kernel, half, groups),
+        grid=(steps,),
+        in_specs=[SMEM, pl.BlockSpec((rows // steps, N2, channels), lambda s: (s, 0, 0))],
+        out_specs=[VMEM] * (half + 1),
+        out_shape=message_shapes(half, channels // (2 * half), rows),
+        scratch_shapes=[pltpu.VMEM((2, rows * (channels + PAD), 128), jnp.float32)],
+        name="pack_tokens",
+    )(place, tokens)
+
+
+def pack_filters(place, filters, half):
+    _, rows, _, held = filters.shape
+    steps = 2
+    return pl.pallas_call(
+        functools.partial(pack_filters_kernel, half),
+        grid=(steps,),
+        in_specs=[SMEM, pl.BlockSpec((2, rows // steps, N2, held), lambda s: (0, s, 0, 0))],
+        out_specs=[VMEM] * (half + 1),
+        out_shape=message_shapes(half, held // half, rows),
+        scratch_shapes=[pltpu.VMEM((2, 2 * rows * (held + PAD), 128), jnp.float32)],
+        name="pack_filters",
+    )(place, filters)
+
+
+def gather_kernel(*refs):
+    *far, out = refs
+    for step, block in enumerate(far):
+        out[step] = block[...]
+
+
+def gather(far):
+    return pl.pallas_call(
+        gather_kernel,
+        in_specs=[VMEM] * len(far),
+        out_specs=VMEM,
+        out_shape=jax.ShapeDtypeStruct((len(far), *far[0].shape), jnp.bfloat16),
+        name="gather",
+    )(*far)
+
+
+def take(kept, far, slot):
+    near = kept[:, pl.ds(slot, 1)].reshape(N1 // 2, N2)
+    if not isinstance(far, (list, tuple)):
+        return near, far[:, pl.ds(slot, 1)].reshape(N1 // 2, N2)
+    across = [ref[pl.ds(slot, 1)].reshape(ref.shape[1], N2) for ref in far]
+    return near, jnp.concatenate(across, axis=0)
+
+
+def forward_kernel(half, lanes, kept, *rest):
+    far = rest[:half]
+    rows_t, twiddle, cols_t, spectrum = rest[half:]
+    slots = [pl.program_id(0) * lanes + lane for lane in range(lanes)]
+    turned = []
+    for slot in slots:
+        signal = jnp.concatenate(take(kept, far, slot), axis=0)
+        section = dot(rows_t[...].reshape(2 * N1, N1), signal)
+        real, imag = section[:N1], section[N1:]
+        turned_real = (real * twiddle[0] + imag * twiddle[1]).astype(jnp.bfloat16)
+        turned_imag = (imag * twiddle[0] - real * twiddle[1]).astype(jnp.bfloat16)
+        turned.append(jnp.concatenate([turned_real, turned_imag], axis=1))
+    result = dot(jnp.concatenate(turned, axis=0), cols_t[...].reshape(2 * N2, 2 * N2))
+    for lane, slot in enumerate(slots):
+        spectrum[slot] = result[lane * N1 : (lane + 1) * N1].astype(jnp.bfloat16)
+
+
+def forward(messages, rows_t, twiddle, cols_t):
+    kept, *far = messages
+    half, slots = kept.shape[:2]
+    return pl.pallas_call(
+        functools.partial(forward_kernel, half, LANES),
+        grid=(slots // LANES,),
+        in_specs=[VMEM] * (half + 4),
+        out_specs=VMEM,
+        out_shape=jax.ShapeDtypeStruct((slots, N1, 2 * N2), jnp.bfloat16),
+        name="forward",
+    )(kept, *far, rows_t, twiddle, cols_t)
+
+
+def inverse_kernel(half, own, other, whole, parts, lanes, place, gain, kept, *rest):
+    far = rest[:half]
+    spectrum, twiddle, back_t, final_t, near_filter = rest[half : half + 5]
+    far_filter = rest[half + 5 : half + 5 + parts]
+    if parts == 1:
+        far_filter = far_filter[0]
+    outs = rest[half + 5 + parts :]
+    index, base, core = place[0], place[1], place[2]
+    piece = kept.shape[2]
+    group = core ^ other
+    products = []
+    lanes_all = [pl.program_id(0) * lanes + number for number in range(lanes)]
+    for lane in lanes_all:
+        slot = group * own + lane
+        weight_real = jnp.concatenate(take(near_filter, far_filter, 2 * lane), axis=0).astype(jnp.float32)
+        weight_imag = jnp.concatenate(take(near_filter, far_filter, 2 * lane + 1), axis=0).astype(jnp.float32)
+        spec_real = spectrum[slot, :, :N2].astype(jnp.float32)
+        spec_imag = spectrum[slot, :, N2:].astype(jnp.float32)
+        prod_real = (spec_real * weight_real - spec_imag * weight_imag).astype(jnp.bfloat16)
+        prod_imag = (spec_real * weight_imag + spec_imag * weight_real).astype(jnp.bfloat16)
+        products.append(jnp.concatenate([prod_real, prod_imag], axis=1))
+    back = dot(jnp.concatenate(products, axis=0), back_t[...].reshape(2 * N2, 2 * N2))
+    for number, lane in enumerate(lanes_all):
+        back_real = back[number * N1 : (number + 1) * N1, :N2]
+        back_imag = back[number * N1 : (number + 1) * N1, N2:]
+        turned_real = (back_real * twiddle[0] - back_imag * twiddle[1]).astype(jnp.bfloat16)
+        turned_imag = (back_real * twiddle[1] + back_imag * twiddle[0]).astype(jnp.bfloat16)
+        filtered = dot(final_t[...], jnp.concatenate([turned_real, turned_imag], axis=0))
+        slot = group * own + lane
+        weight = gain[(group * 2 * half + index) * own + lane]
+        direct = jnp.concatenate(take(kept, far, slot), axis=0).astype(jnp.float32)
+        result = (filtered + weight * direct).astype(jnp.bfloat16)
+        near = pl.ds(base, half) if whole else pl.ds(0, half)
+        outs[0][near, pl.ds(lane, 1)] = result[: N1 // 2].reshape(half, 1, piece, N2)
+        for step in range(half):
+            start = N1 // 2 + step * piece
+            rows = result[start : start + piece].reshape(1, piece, N2)
+            if whole:
+                outs[0][index ^ (half + step), pl.ds(lane, 1)] = rows
+            else:
+                outs[1 + step][pl.ds(lane, 1)] = rows
+
+
+def inverse(place, gain, messages, spectrum, tables, filters, own, other, whole):
+    kept, *far = messages
+    half, _, rows, _ = kept.shape
+    if whole:
+        out_shape = [jax.ShapeDtypeStruct((2 * half, own, rows, N2), jnp.bfloat16)]
+    else:
+        out_shape = message_shapes(half, own, rows)
+    inputs = [kept, *far, spectrum, *tables, *filters]
+    return pl.pallas_call(
+        functools.partial(inverse_kernel, half, own, other, whole, len(filters) - 1, LANES),
+        grid=(own // LANES,),
+        in_specs=[SMEM, SMEM] + [VMEM] * len(inputs),
+        out_specs=[VMEM] * len(out_shape),
+        out_shape=out_shape,
+    )(place, gain, *inputs)
+
+
+def unpack_kernel(half, whole, place, *rest):
+    inputs, out, scratch = rest[: 1 if whole else half + 1], rest[-2], rest[-1]
+    step = pl.program_id(0)
+    rows, _, held = out.shape
+    stride = held + PAD
+    total = rows * pl.num_programs(0)
+
+    @pl.when(step == 0)
+    def _():
+        own = held // (2 * half)
+        if whole:
+            blocks = [(block, inputs[0].at[block]) for block in range(2 * half)]
+        else:
+            blocks = blocks_of(half, place, inputs[0], inputs[1:])
+        for source, message in blocks:
+
+            def place_rows(lane, _):
+                piece = message[lane].astype(jnp.float32)
+                put_rows(scratch, pl.ds(source * own + lane, total, stride=stride), piece)
+                return 0
+
+            lax.fori_loop(0, own, place_rows, 0, unroll=2)
+
+    for row in range(rows):
+        at = pl.ds(pl.multiple_of((step * rows + row) * stride, PAD), held)
+        block = jnp.concatenate([scratch[0, at], scratch[1, at]], axis=1)
+        out[row] = block.astype(jnp.bfloat16).T
+
+
+def unpack(place, received, rows, channels, groups, half, other, partial):
+    whole = len(received) == 1
+    held = channels // groups
+    steps = 2
+    inputs = [*received, *partial]
+    return pl.pallas_call(
+        functools.partial(unpack_kernel, half, whole),
+        grid_spec=pltpu.PrefetchScalarGridSpec(
+            num_scalar_prefetch=1,
+            grid=(steps,),
+            in_specs=[VMEM] * len(received) + [pl.BlockSpec(memory_space=pl.ANY)] * len(partial),
+            out_specs=pl.BlockSpec((rows // steps, N2, held), lambda s, place: (s, 0, place[2] ^ other)),
+            scratch_shapes=[pltpu.VMEM((2, rows * (held + PAD), 128), jnp.float32)],
+        ),
+        out_shape=jax.ShapeDtypeStruct((rows, N2, channels), jnp.bfloat16),
+        input_output_aliases={1 + len(received): 0} if partial else {},
+    )(place, *inputs)
+
+
+def exchange(messages, count):
+    kept, *far = messages
+    half = count // 2
+    halves = [list(range(half)), list(range(half, count))]
+    across = [
+        lax.ppermute(block, "seq", [(s, s ^ (half + step)) for s in range(count)])
+        for step, block in enumerate(far)
+    ]
+    near = lax.all_to_all(kept, "seq", split_axis=0, concat_axis=0, tiled=True, axis_index_groups=halves)
+    return [near, *across]
+
+
+def swap(array):
+    return lax.ppermute(array, "bat", [(0, 1), (1, 0)])
+
+
+def direct_body(tokens, filter_spectrum, skip_gain):
+    count = lax.axis_size("seq")
+    groups = lax.axis_size("bat")
+    index = lax.axis_index("seq")
+    core = lax.axis_index("bat")
+    _, local_length, channels = tokens.shape
+    rows = N1 // count
+    half = count // 2
+    own = channels // (groups * count)
+    place = jnp.stack([index, index // half * half, core]).astype(jnp.int32)
+    messages = pack_tokens(place, tokens.reshape(rows, N2, channels), half, groups)
+    signal = exchange(messages, count)
+    messages = pack_filters(place, filter_spectrum, half)
+    filters = exchange(messages, count)
+    rows_t, twiddle, cols_t, back_t, final_t = dft_tables(relative_rows(index, count, rows))
+    spectrum = forward(signal, rows_t, twiddle, cols_t)
+    tables = (twiddle, back_t, jnp.concatenate([final_t[0], final_t[1]], axis=1))
+    (ready,) = inverse(place, skip_gain, signal, spectrum, tables, filters, own, 0, True)
+    first = lax.all_to_all(ready, "seq", split_axis=0, concat_axis=0, tiled=True)
+    near_filter = swap(filters[0])
+    far_filter = gather(filters[1:])
+    far_filter = swap(far_filter)
+    messages = inverse(
+        place, skip_gain, signal, spectrum, tables, (near_filter, far_filter), own, 1, False
+    )
+    second = exchange(messages, count)
+    mixed = unpack(place, [first], rows, channels, groups, half, 0, [])
+    mixed = unpack(place, second, rows, channels, groups, half, 1, [mixed])
+    return mixed.reshape(1, local_length, channels)
+
+
+def direct_fits(tokens, count, groups):
+    batch_rows, _, channels = tokens.shape
+    power = count > 2 and count & (count - 1) == 0
+    return power and groups == 2 and batch_rows == 1 and N1 // count % 16 == 0 and channels // groups % (LANES * count) == 0
+
+
+def body(tokens, filter_spectrum, skip_gain):
+    if direct_fits(tokens, lax.axis_size("seq"), lax.axis_size("bat")):
+        return direct_body(tokens, filter_spectrum, skip_gain)
+    return spread_body(tokens, filter_spectrum, skip_gain)
+
+
 def solution(mesh):
     placed = (P("bat", "seq", None), P(None, "seq", None, "bat"), P())
     return jax.shard_map(

time: 194 us -> 187 us (0.964)
  starting transfers between devices: 20.1 us -> 87.9 us
  waiting for transfers between devices: 93.8 us -> 42.4 us
  blocking collectives: 30.7 us -> 0 us
  Pallas kernels: 24.5 us -> 41.6 us
  local copies, waits for them, and re-layouts: 13.8 us -> 3.33 us
    all_to_all x3 -> x4, waiting for transfers between devices: 93.8 us -> 15.7 us  [the longest x1 8.31 us: direct_body(): lax.all_to_all(ready, 'seq', split_axis=0, concat_axis=0, tiled=True)]
    ppermute x0 -> x26, starting transfers between devices: none -> 66.1 us  [the longest x24 65.6 us: exchange(): lax.ppermute(block, 'seq', [(s, s ^ half + step) for s in range(count)])]
    all_to_all x1 -> x0, blocking collectives: 30.7 us -> none  [body(): lax.all_to_all(result, axes, split_axis=0, concat_axis=0, tiled=True)]
    ppermute x0 -> x26, waiting for transfers between devices: none -> 26.7 us  [the longest x24 22.7 us: exchange(): lax.ppermute(block, 'seq', [(s, s ^ half + step) for s in range(count)])]
    pallas_call x2 -> x8, Pallas kernels: 24.5 us -> 41.6 us  [the longest x2 14.6 us: inverse(): pl.pallas_call(functools.partial(inverse_kernel, half, own, other, whole,...]
    transpose x2 -> x0, local copies, waits for them, and re-layouts: 7.33 us -> none  [the longest x1 4.6 us: body(): filter_spectrum.transpose(3, 0, 1, 2)]
    reshape x1 -> x0, local copies, waits for them, and re-layouts: 4.5 us -> none  [body(): tokens.reshape(batch_rows, rows_local, N2, channels).transpose(3, 0, 1, 2)]
    cos x0 -> x1, other arithmetic: none -> 2.12 us  [dft_tables(): twiddle = jnp.stack([jnp.cos(angle), jnp.sin(angle)])]
  transfers between devices with their start and end apart: 3 -> 30, of which waited for: 3 -> 9; matrix products, arithmetic and copies ran while one was open for 8% -> 6% of each run, Pallas kernels for 6% -> 14%
where the time goes in v2:
time: 187 us
  starting transfers between devices  87.9 us (47%)
  waiting for transfers between devices  42.4 us (23%)
  Pallas kernels  41.6 us (22%)
  other arithmetic  11.2 us (6%)
  local copies, waits for them, and re-layouts  3.33 us (2%)
    ppermute x24, starting transfers between devices, exchange(): lax.ppermute(block, 'seq', [(s, s ^ half + step) for s in range(count)])  65.6 us
    ppermute x24, waiting for transfers between devices, exchange(): lax.ppermute(block, 'seq', [(s, s ^ half + step) for s in range(count)])  22.7 us
    all_to_all x3, starting transfers between devices, exchange(): lax.all_to_all(kept, 'seq', split_axis=0, concat_axis=0, tiled=True, axis...  14.7 us
    pallas_call x2, Pallas kernels, inverse(): pl.pallas_call(functools.partial(inverse_kernel, half, own, other, whole,...  14.6 us
    pallas_call x1, Pallas kernels, forward(): pl.pallas_call(functools.partial(forward_kernel, half, LANES), grid=(slot...  8.47 us
    all_to_all x1, waiting for transfers between devices, direct_body(): lax.all_to_all(ready, 'seq', split_axis=0, concat_axis=0, tiled=True)  8.31 us
    pallas_call x2, Pallas kernels, unpack(): pl.pallas_call(functools.partial(unpack_kernel, half, whole), grid_spec=p...  7.58 us
    all_to_all x3, waiting for transfers between devices, exchange(): lax.all_to_all(kept, 'seq', split_axis=0, concat_axis=0, tiled=True, axis...  7.38 us
  transfers between devices with their start and end apart: 30, of which 9 were waited for; matrix products, arithmetic and copies ran while one was open for 6% of the time, Pallas kernels for 14%

profile of v2, /device:TPU:0, one launch (start us, length us, event | category | flops | bytes accessed | tf_op | source)
XLA Modules:
  0.0 186.8 jit_solution(16217633192112692034)
XLA Ops:
  0.6 4.2 %pack_tokens.1 = (bf16[8,16,16,256]{3,2,1,0:T(8,128)(2,1)}, bf16[16,16,256]{2,1,0:T(8,128)(2,1)}, bf16[16,16,256]{2,1,0:T(8,128)(2,1)}, bf16[16,16,256]{2,1,0:T(...) custom-call(s32[3]{0:T(128)} %pad_add_fusion.place, ...), custom_call_target="tpu_custom_call" | custom-call | tf_op jit(solution)/shard_map/pack_tokens/pallas_call | solution.py:255
  4.8 6.3 %all-to-all-start = ((bf16[8,16,16,256]{3,2,1,0:T(8,128)(2,1)}), bf16[8,16,16,256]{3,2,1,0:T(8,128)(2,1)S(1)}, u32[]{:S(2)}, u32[]{:S(2)}) async-start(bf16[8,16,16,256]{3,2,1,0:T(8,128)(2,1)} %get-tuple-element.32), calls=%async_computation | async-start | bytes 2097152 | tf_op jit(solution)/shard_map/all_to_all | solution.py:450
  11.1 2.7 %collective-permute-start = (bf16[16,16,256]{2,1,0:T(8,128)(2,1)S(1)}, bf16[16,16,256]{2,1,0:T(8,128)(2,1)S(1)}, u32[]{:S(2)}, u32[]{:S(2)}) collective-permute-start(bf16[16,16,256]{2,1,0:T(8,128)(2,1)S(1)} %copy-done.39), channel_id=1, source_target_pairs={{0,16},{2,18},{4,20},{6,22},{8,24},{10,26},{12,28},{14,30},{16,0},... | collective-permute-start | bytes 393224 | tf_op jit(solution)/shard_map/ppermute | solution.py:447
  15.5 3.5 %collective-permute-start.2 = (bf16[16,16,256]{2,1,0:T(8,128)(2,1)}, bf16[16,16,256]{2,1,0:T(8,128)(2,1)S(1)}, u32[]{:S(2)}, u32[]{:S(2)}) collective-permute-start(bf16[16,16,256]{2,1,0:T(8,128)(2,1)} %get-tuple-element.35), channel_id=1, source_target_pairs={{0,20},{2,22},{4,16},{6,18},{8,28},{10,30},{12,24},{14,26},{16,4},... | collective-permute-start | bytes 393224 | tf_op jit(solution)/shard_map/ppermute | solution.py:447
  19.0 3.8 %collective-permute-start.4 = (bf16[16,16,256]{2,1,0:T(8,128)(2,1)}, bf16[16,16,256]{2,1,0:T(8,128)(2,1)S(1)}, u32[]{:S(2)}, u32[]{:S(2)}) collective-permute-start(bf16[16,16,256]{2,1,0:T(8,128)(2,1)} %get-tuple-element.37), channel_id=1, source_target_pairs={{0,24},{2,26},{4,28},{6,30},{8,16},{10,18},{12,20},{14,22},{16,8},... | collective-permute-start | bytes 393224 | tf_op jit(solution)/shard_map/ppermute | solution.py:447
  23.1 4.3 %pack_filters.1 = (bf16[8,16,16,256]{3,2,1,0:T(8,128)(2,1)}, bf16[16,16,256]{2,1,0:T(8,128)(2,1)}, bf16[16,16,256]{2,1,0:T(8,128)(2,1)}, bf16[16,16,256]{2,1,0:T...) custom-call(s32[3]{0:T(128)} %pad_add_fusion.place, ...), custom_call_target="tpu_custom_call" | custom-call | tf_op jit(solution)/shard_map/pack_filters/pallas_call | solution.py:269
  28.4 7.4 %all-to-all-done.kept = bf16[8,16,16,256]{3,2,1,0:T(8,128)(2,1)S(1)} async-done(((bf16[8,16,16,256]{3,2,1,0:T(8,128)(2,1)}), bf16[8,16,16,256]{3,2,1,0:T(8,128)(2,1)S(1)}, u32[]{:S(2)}, u32[]{:S(2)}) %all-to-all-start) | async-done | bytes 1048608 | tf_op jit(solution)/shard_map/all_to_all | solution.py:450
  35.8 3.7 %all-to-all-start.1 = ((bf16[8,16,16,256]{3,2,1,0:T(8,128)(2,1)}), bf16[8,16,16,256]{3,2,1,0:T(8,128)(2,1)S(1)}, u32[]{:S(2)}, u32[]{:S(2)}) async-start(bf16[8,16,16,256]{3,2,1,0:T(8,128)(2,1)} %get-tuple-element.41), calls=%async_computation.1 | async-start | bytes 2097152 | tf_op jit(solution)/shard_map/all_to_all | solution.py:450
  41.5 2.1 %fusion.22 = (f32[1,256,256]{2,1,0:T(8,128)S(1)}, f32[1,256,256]{2,1,0:T(8,128)S(1)}, f32[1,256,256]{2,1,0:T(8,128)S(1)}, f32[1,256,256]{2,1,0:T(8,128)S(1)}) fusion(s32[256]{0:T(256)S(1)} %add.94), kind=kLoop, calls=%fused_computation.46 | loop fusion | flops 1900544 | bytes 1049600 | tf_op jit(solution)/shard_map/cos | solution.py:39
  45.0 3.0 %collective-permute-start.5 = (bf16[16,16,256]{2,1,0:T(8,128)(2,1)S(1)}, bf16[16,16,256]{2,1,0:T(8,128)(2,1)S(1)}, u32[]{:S(2)}, u32[]{:S(2)}) collective-permute-start(bf16[16,16,256]{2,1,0:T(8,128)(2,1)S(1)} %copy-done.36), channel_id=1, source_target_pairs={{0,26},{2,24},{4,30},{6,28},{8,18},{10,16},{12,22},{14,20},{16,10}... | collective-permute-start | bytes 393224 | tf_op jit(solution)/shard_map/ppermute | solution.py:447
  48.9 3.1 %collective-permute-start.6 = (bf16[16,16,256]{2,1,0:T(8,128)(2,1)S(1)}, bf16[16,16,256]{2,1,0:T(8,128)(2,1)S(1)}, u32[]{:S(2)}, u32[]{:S(2)}) collective-permute-start(bf16[16,16,256]{2,1,0:T(8,128)(2,1)S(1)} %copy-done.34), channel_id=1, source_target_pairs={{0,28},{2,30},{4,24},{6,26},{8,20},{10,22},{12,16},{14,18},{16,12}... | collective-permute-start | bytes 393224 | tf_op jit(solution)/shard_map/ppermute | solution.py:447
  53.9 3.8 %collective-permute-start.10 = (bf16[16,16,256]{2,1,0:T(8,128)(2,1)S(1)}, bf16[16,16,256]{2,1,0:T(8,128)(2,1)S(1)}, u32[]{:S(2)}, u32[]{:S(2)}) collective-permute-start(bf16[16,16,256]{2,1,0:T(8,128)(2,1)S(1)} %copy-done.37), channel_id=1, source_target_pairs={{0,18},{2,16},{4,22},{6,20},{8,26},{10,24},{12,30},{14,28},{16,2},... | collective-permute-start | bytes 393224 | tf_op jit(solution)/shard_map/ppermute | solution.py:447
  58.4 13.3 %collective-permute-start.11 = (bf16[16,16,256]{2,1,0:T(8,128)(2,1)S(1)}, bf16[16,16,256]{2,1,0:T(8,128)(2,1)S(1)}, u32[]{:S(2)}, u32[]{:S(2)}) collective-permute-start(bf16[16,16,256]{2,1,0:T(8,128)(2,1)S(1)} %copy-done.35), channel_id=1, source_target_pairs={{0,20},{2,22},{4,16},{6,18},{8,28},{10,30},{12,24},{14,26},{16,4},... | collective-permute-start | bytes 393224 | tf_op jit(solution)/shard_map/ppermute | solution.py:447
  75.0 2.9 %collective-permute-start.13 = (bf16[16,16,256]{2,1,0:T(8,128)(2,1)}, bf16[16,16,256]{2,1,0:T(8,128)(2,1)S(1)}, u32[]{:S(2)}, u32[]{:S(2)}) collective-permute-start(bf16[16,16,256]{2,1,0:T(8,128)(2,1)} %get-tuple-element.46), channel_id=1, source_target_pairs={{0,24},{2,26},{4,28},{6,30},{8,16},{10,18},{12,20},{14,22},{16,8},... | collective-permute-start | bytes 393224 | tf_op jit(solution)/shard_map/ppermute | solution.py:447
  77.9 9.0 %collective-permute-done.9.refs_0_.rest_13_ = bf16[16,16,256]{2,1,0:T(8,128)(2,1)S(1)} collective-permute-done((bf16[16,16,256]{2,1,0:T(8,128)(2,1)S(1)}, bf16[16,16,256]{2,1,0:T(8,128)(2,1)S(1)}, u32[]{:S(2)}, u32[]{:S(2)}) %collective-permute-start.9) | collective-permute-done | bytes 131104 | tf_op jit(solution)/shard_map/ppermute | solution.py:447
  90.6 7.8 %collective-permute-done.11.refs_2_.rest_15_ = bf16[16,16,256]{2,1,0:T(8,128)(2,1)S(1)} collective-permute-done((bf16[16,16,256]{2,1,0:T(8,128)(2,1)S(1)}, bf16[16,16,256]{2,1,0:T(8,128)(2,1)S(1)}, u32[]{:S(2)}, u32[]{:S(2)}) %collective-permute-start.11) | collective-permute-done | bytes 131104 | tf_op jit(solution)/shard_map/ppermute | solution.py:447
  100.1 8.5 %forward.1.rest_8_ = bf16[16,256,512]{2,1,0:T(8,128)(2,1)} custom-call(bf16[8,16,16,256]{3,2,1,0:T(8,128)(2,1)} %copy-done, bf16[16,16,256]{2,1,0:T(8,128)(2,1)} %copy-done.5, bf16[16,16,256]{2,1,0:T(8,128)(2,1)} %copy-done.6, bf16[16,16,256]{2,1,0:T(8,128)(2,1)} %copy-done.7, bf16[16,16,256]{2,1,0:T(8,128)(2,1)} %copy-done.8, ...), custom_call_target="tpu_custom_call" | custom-call | tf_op jit(solution)/shard_map/forward/pallas_call | solution.py:324
  110.4 7.3 %shard_map.38 = bf16[16,8,16,256]{3,2,1,0:T(8,128)(2,1)} custom-call(s32[3]{0:T(128)} %pad_add_fusion.place, f32[256]{0:T(256)} %gain.3, bf16[8,16,16,256]{3,2,1,0:T(8,128)(2,1)} %copy-done, bf16[16,16,256]{2,1,0:T(8,128)(2,1)} %copy-done.5, bf16[16,16,256]{2,1,0:T(8,128)(2,1)} %copy-done.6, bf16[16,16,256]{2,1,0:T(8,128)(2,1)} %copy-done.7, ...), custom_call_target="tpu_custom_call" | custom-call | tf_op jit(solution)/shard_map/pallas_call | solution.py:385
  117.7 7.1 %all-to-all-start.3 = ((bf16[16,8,16,256]{3,2,1,0:T(8,128)(2,1)}), bf16[16,8,16,256]{3,2,1,0:T(8,128)(2,1)S(1)}, u32[]{:S(2)}, u32[]{:S(2)}) async-start(bf16[16,8,16,256]{3,2,1,0:T(8,128)(2,1)} %shard_map.38), calls=%async_computation.3 | async-start | bytes 2097152 | tf_op jit(solution)/shard_map/all_to_all | solution.py:476
  124.8 2.4 %gather.1 = bf16[8,16,16,256]{3,2,1,0:T(8,128)(2,1)} custom-call(bf16[16,16,256]{2,1,0:T(8,128)(2,1)} %copy-done.14, bf16[16,16,256]{2,1,0:T(8,128)(2,1)} %copy-done.15, bf16[16,16,256]{2,1,0:T(8,128)(2,1)} %copy-done.16, bf16[16,16,256]{2,1,0:T(8,128)(2,1)} %copy-done.17, bf16[16,16,256]{2,1,0:T(8,128)(2,1)} %copy-done.18, bf16[16,16,256]{2,1,0:T(8,128)(2,1)} %copy-done.19, ...), custom_call_target="tpu_custom_call" | custom-call | tf_op jit(solution)/shard_map/gather/pallas_call | solution.py:287
  127.8 2.4 %collective-permute-done.17.rest_13_ = bf16[8,16,16,256]{3,2,1,0:T(8,128)(2,1)S(1)} collective-permute-done((bf16[8,16,16,256]{3,2,1,0:T(8,128)(2,1)}, bf16[8,16,16,256]{3,2,1,0:T(8,128)(2,1)S(1)}, u32[]{:S(2)}, u32[]{:S(2)}) %collective-permute-start.17) | collective-permute-done | bytes 1048608 | tf_op jit(solution)/shard_map/ppermute | solution.py:455
  131.7 7.3 %shard_map.37 = (bf16[8,8,16,256]{3,2,1,0:T(8,128)(2,1)}, bf16[8,16,256]{2,1,0:T(8,128)(2,1)}, bf16[8,16,256]{2,1,0:T(8,128)(2,1)}, bf16[8,16,256]{2,1,0:T(8,128...) custom-call(s32[3]{0:T(128)} %pad_add_fusion.place, ...), custom_call_target="tpu_custom_call" | custom-call | tf_op jit(solution)/shard_map/pallas_call | solution.py:385
  139.0 8.3 %all-to-all-done.3.rest_0_ = bf16[16,8,16,256]{3,2,1,0:T(8,128)(2,1)S(1)} async-done(((bf16[16,8,16,256]{3,2,1,0:T(8,128)(2,1)}), bf16[16,8,16,256]{3,2,1,0:T(8,128)(2,1)S(1)}, u32[]{:S(2)}, u32[]{:S(2)}) %all-to-all-start.3) | async-done | bytes 1048608 | tf_op jit(solution)/shard_map/all_to_all | solution.py:476
  147.4 4.6 %all-to-all-start.2 = ((bf16[8,8,16,256]{3,2,1,0:T(8,128)(2,1)}), bf16[8,8,16,256]{3,2,1,0:T(8,128)(2,1)S(1)}, u32[]{:S(2)}, u32[]{:S(2)}) async-start(bf16[8,8,16,256]{3,2,1,0:T(8,128)(2,1)} %get-tuple-element.50), calls=%async_computation.2 | async-start | bytes 1048576 | tf_op jit(solution)/shard_map/all_to_all | solution.py:450
  153.4 2.9 %collective-permute-start.19 = (bf16[8,16,256]{2,1,0:T(8,128)(2,1)}, bf16[8,16,256]{2,1,0:T(8,128)(2,1)S(1)}, u32[]{:S(2)}, u32[]{:S(2)}) collective-permute-start(bf16[8,16,256]{2,1,0:T(8,128)(2,1)} %get-tuple-element.52), channel_id=1, source_target_pairs={{0,18},{2,16},{4,22},{6,20},{8,26},{10,24},{12,30},{14,28},{16,2},... | collective-permute-start | bytes 196616 | tf_op jit(solution)/shard_map/ppermute | solution.py:447
  156.3 2.3 %collective-permute-start.20 = (bf16[8,16,256]{2,1,0:T(8,128)(2,1)}, bf16[8,16,256]{2,1,0:T(8,128)(2,1)S(1)}, u32[]{:S(2)}, u32[]{:S(2)}) collective-permute-start(bf16[8,16,256]{2,1,0:T(8,128)(2,1)} %get-tuple-element.53), channel_id=1, source_target_pairs={{0,20},{2,22},{4,16},{6,18},{8,28},{10,30},{12,24},{14,26},{16,4},... | collective-permute-start | bytes 196616 | tf_op jit(solution)/shard_map/ppermute | solution.py:447
  159.6 2.9 %collective-permute-start.22 = (bf16[8,16,256]{2,1,0:T(8,128)(2,1)}, bf16[8,16,256]{2,1,0:T(8,128)(2,1)S(1)}, u32[]{:S(2)}, u32[]{:S(2)}) collective-permute-start(bf16[8,16,256]{2,1,0:T(8,128)(2,1)} %get-tuple-element.55), channel_id=1, source_target_pairs={{0,24},{2,26},{4,28},{6,30},{8,16},{10,18},{12,20},{14,22},{16,8},... | collective-permute-start | bytes 196616 | tf_op jit(solution)/shard_map/ppermute | solution.py:447
  162.5 2.4 %collective-permute-start.23 = (bf16[8,16,256]{2,1,0:T(8,128)(2,1)}, bf16[8,16,256]{2,1,0:T(8,128)(2,1)S(1)}, u32[]{:S(2)}, u32[]{:S(2)}) collective-permute-start(bf16[8,16,256]{2,1,0:T(8,128)(2,1)} %get-tuple-element.56), channel_id=1, source_target_pairs={{0,26},{2,24},{4,30},{6,28},{8,18},{10,16},{12,22},{14,20},{16,10}... | collective-permute-start | bytes 196616 | tf_op jit(solution)/shard_map/ppermute | solution.py:447
  164.9 8.6 %collective-permute-start.24 = (bf16[8,16,256]{2,1,0:T(8,128)(2,1)}, bf16[8,16,256]{2,1,0:T(8,128)(2,1)S(1)}, u32[]{:S(2)}, u32[]{:S(2)}) collective-permute-start(bf16[8,16,256]{2,1,0:T(8,128)(2,1)} %get-tuple-element.57), channel_id=1, source_target_pairs={{0,28},{2,30},{4,24},{6,26},{8,20},{10,22},{12,16},{14,18},{16,12}... | collective-permute-start | bytes 196616 | tf_op jit(solution)/shard_map/ppermute | solution.py:447
  173.8 3.8 %shard_map.39.rest_9_ = bf16[16,256,256]{2,1,0:T(8,128)(2,1)} custom-call(s32[3]{0:T(128)} %pad_add_fusion.place, bf16[16,8,16,256]{3,2,1,0:T(8,128)(2,1)} %copy-done.1), custom_call_target="tpu_custom_call" | custom-call | tf_op jit(solution)/shard_map/pallas_call | solution.py:428
  177.6 4.0 %collective-permute-done.25.rest_8_ = bf16[8,16,256]{2,1,0:T(8,128)(2,1)S(1)} collective-permute-done((bf16[8,16,256]{2,1,0:T(8,128)(2,1)}, bf16[8,16,256]{2,1,0:T(8,128)(2,1)S(1)}, u32[]{:S(2)}, u32[]{:S(2)}) %collective-permute-start.25) | collective-permute-done | bytes 65568 | tf_op jit(solution)/shard_map/ppermute | solution.py:447
  183.0 3.8 %shard_map.40 = bf16[16,256,256]{2,1,0:T(8,128)(2,1)} custom-call(s32[3]{0:T(128)} %pad_add_fusion.place, bf16[8,8,16,256]{3,2,1,0:T(8,128)(2,1)} %copy-done.4, bf16[8,16,256]{2,1,0:T(8,128)(2,1)} %copy-done.22, bf16[8,16,256]{2,1,0:T(8,128)(2,1)} %copy-done.23, bf16[8,16,256]{2,1,0:T(8,128)(2,1)} %copy-done.24, ...), custom_call_target="tpu_custom_call", output_to_operand_aliasing={{}: (10, {})} | custom-call | tf_op jit(solution)/shard_map/pallas_call | solution.py:428
  (135 shorter events, 26.8 us)
Async XLA Ops:
  4.8 31.0 %all-to-all-start = ((bf16[8,16,16,256]{3,2,1,0:T(8,128)(2,1)}), bf16[8,16,16,256]{3,2,1,0:T(8,128)(2,1)S(1)}, u32[]{:S(2)}, u32[]{:S(2)}) async-start(bf16[8,16,16,256]{3,2,1,0:T(8,128)(2,1)} %get-tuple-element.32), calls=%async_computation | async-start | bytes 2097152 | tf_op jit(solution)/shard_map/all_to_all | solution.py:450
  11.1 33.8 %collective-permute-start = (bf16[16,16,256]{2,1,0:T(8,128)(2,1)S(1)}, bf16[16,16,256]{2,1,0:T(8,128)(2,1)S(1)}, u32[]{:S(2)}, u32[]{:S(2)}) collective-permute-start(bf16[16,16,256]{2,1,0:T(8,128)(2,1)S(1)} %copy-done.39), channel_id=1, source_target_pairs={{0,16},{2,18},{4,20},{6,22},{8,24},{10,26},{12,28},{14,30},{16,0},... | collective-permute-start | bytes 393224 | tf_op jit(solution)/shard_map/ppermute | solution.py:447
  13.8 35.1 %collective-permute-start.1 = (bf16[16,16,256]{2,1,0:T(8,128)(2,1)}, bf16[16,16,256]{2,1,0:T(8,128)(2,1)S(1)}, u32[]{:S(2)}, u32[]{:S(2)}) collective-permute-start(bf16[16,16,256]{2,1,0:T(8,128)(2,1)} %get-tuple-element.34), channel_id=1, source_target_pairs={{0,18},{2,16},{4,22},{6,20},{8,26},{10,24},{12,30},{14,28},{16,2},... | collective-permute-start | bytes 393224 | tf_op jit(solution)/shard_map/ppermute | solution.py:447
  15.5 36.5 %collective-permute-start.2 = (bf16[16,16,256]{2,1,0:T(8,128)(2,1)}, bf16[16,16,256]{2,1,0:T(8,128)(2,1)S(1)}, u32[]{:S(2)}, u32[]{:S(2)}) collective-permute-start(bf16[16,16,256]{2,1,0:T(8,128)(2,1)} %get-tuple-element.35), channel_id=1, source_target_pairs={{0,20},{2,22},{4,16},{6,18},{8,28},{10,30},{12,24},{14,26},{16,4},... | collective-permute-start | bytes 393224 | tf_op jit(solution)/shard_map/ppermute | solution.py:447
  19.0 34.7 %collective-permute-start.3 = (bf16[16,16,256]{2,1,0:T(8,128)(2,1)}, bf16[16,16,256]{2,1,0:T(8,128)(2,1)S(1)}, u32[]{:S(2)}, u32[]{:S(2)}) collective-permute-start(bf16[16,16,256]{2,1,0:T(8,128)(2,1)} %get-tuple-element.36), channel_id=1, source_target_pairs={{0,22},{2,20},{4,18},{6,16},{8,30},{10,28},{12,26},{14,24},{16,6},... | collective-permute-start | bytes 393224 | tf_op jit(solution)/shard_map/ppermute | solution.py:447
  19.0 34.8 %collective-permute-start.4 = (bf16[16,16,256]{2,1,0:T(8,128)(2,1)}, bf16[16,16,256]{2,1,0:T(8,128)(2,1)S(1)}, u32[]{:S(2)}, u32[]{:S(2)}) collective-permute-start(bf16[16,16,256]{2,1,0:T(8,128)(2,1)} %get-tuple-element.37), channel_id=1, source_target_pairs={{0,24},{2,26},{4,28},{6,30},{8,16},{10,18},{12,20},{14,22},{16,8},... | collective-permute-start | bytes 393224 | tf_op jit(solution)/shard_map/ppermute | solution.py:447
  35.8 72.9 %all-to-all-start.1 = ((bf16[8,16,16,256]{3,2,1,0:T(8,128)(2,1)}), bf16[8,16,16,256]{3,2,1,0:T(8,128)(2,1)S(1)}, u32[]{:S(2)}, u32[]{:S(2)}) async-start(bf16[8,16,16,256]{3,2,1,0:T(8,128)(2,1)} %get-tuple-element.41), calls=%async_computation.1 | async-start | bytes 2097152 | tf_op jit(solution)/shard_map/all_to_all | solution.py:450
  45.0 13.5 %collective-permute-start.5 = (bf16[16,16,256]{2,1,0:T(8,128)(2,1)S(1)}, bf16[16,16,256]{2,1,0:T(8,128)(2,1)S(1)}, u32[]{:S(2)}, u32[]{:S(2)}) collective-permute-start(bf16[16,16,256]{2,1,0:T(8,128)(2,1)S(1)} %copy-done.36), channel_id=1, source_target_pairs={{0,26},{2,24},{4,30},{6,28},{8,18},{10,16},{12,22},{14,20},{16,10}... | collective-permute-start | bytes 393224 | tf_op jit(solution)/shard_map/ppermute | solution.py:447
  48.0 50.4 %copy-start.30 = (bf16[16,16,256]{2,1,0:T(8,128)(2,1)S(1)}, bf16[16,16,256]{2,1,0:T(8,128)(2,1)}, u32[]{:S(2)}) copy-start(bf16[16,16,256]{2,1,0:T(8,128)(2,1)} %get-tuple-element.49) | copy-start | bytes 393220
  48.9 51.1 %copy-start.6 = (bf16[16,16,256]{2,1,0:T(8,128)(2,1)}, bf16[16,16,256]{2,1,0:T(8,128)(2,1)S(1)}, u32[]{:S(2)}) copy-start(bf16[16,16,256]{2,1,0:T(8,128)(2,1)S(1)} %collective-permute-done.1.rest_1_) | copy-start | bytes 393220
  48.9 24.5 %collective-permute-start.6 = (bf16[16,16,256]{2,1,0:T(8,128)(2,1)S(1)}, bf16[16,16,256]{2,1,0:T(8,128)(2,1)S(1)}, u32[]{:S(2)}, u32[]{:S(2)}) collective-permute-start(bf16[16,16,256]{2,1,0:T(8,128)(2,1)S(1)} %copy-done.34), channel_id=1, source_target_pairs={{0,28},{2,30},{4,24},{6,26},{8,20},{10,22},{12,16},{14,18},{16,12}... | collective-permute-start | bytes 393224 | tf_op jit(solution)/shard_map/ppermute | solution.py:447
  52.0 23.0 %collective-permute-start.7 = (bf16[16,16,256]{2,1,0:T(8,128)(2,1)S(1)}, bf16[16,16,256]{2,1,0:T(8,128)(2,1)S(1)}, u32[]{:S(2)}, u32[]{:S(2)}) collective-permute-start(bf16[16,16,256]{2,1,0:T(8,128)(2,1)S(1)} %copy-done.33), channel_id=1, source_target_pairs={{0,30},{2,28},{4,26},{6,24},{8,22},{10,20},{12,18},{14,16},{16,14}... | collective-permute-start | bytes 393224 | tf_op jit(solution)/shard_map/ppermute | solution.py:447
  53.8 33.1 %collective-permute-start.9 = (bf16[16,16,256]{2,1,0:T(8,128)(2,1)S(1)}, bf16[16,16,256]{2,1,0:T(8,128)(2,1)S(1)}, u32[]{:S(2)}, u32[]{:S(2)}) collective-permute-start(bf16[16,16,256]{2,1,0:T(8,128)(2,1)S(1)} %copy-done.38), channel_id=1, source_target_pairs={{0,16},{2,18},{4,20},{6,22},{8,24},{10,26},{12,28},{14,30},{16,0},... | collective-permute-start | bytes 393224 | tf_op jit(solution)/shard_map/ppermute | solution.py:447
  53.9 34.8 %collective-permute-start.10 = (bf16[16,16,256]{2,1,0:T(8,128)(2,1)S(1)}, bf16[16,16,256]{2,1,0:T(8,128)(2,1)S(1)}, u32[]{:S(2)}, u32[]{:S(2)}) collective-permute-start(bf16[16,16,256]{2,1,0:T(8,128)(2,1)S(1)} %copy-done.37), channel_id=1, source_target_pairs={{0,18},{2,16},{4,22},{6,20},{8,26},{10,24},{12,30},{14,28},{16,2},... | collective-permute-start | bytes 393224 | tf_op jit(solution)/shard_map/ppermute | solution.py:447
  58.4 40.0 %collective-permute-start.11 = (bf16[16,16,256]{2,1,0:T(8,128)(2,1)S(1)}, bf16[16,16,256]{2,1,0:T(8,128)(2,1)S(1)}, u32[]{:S(2)}, u32[]{:S(2)}) collective-permute-start(bf16[16,16,256]{2,1,0:T(8,128)(2,1)S(1)} %copy-done.35), channel_id=1, source_target_pairs={{0,20},{2,22},{4,16},{6,18},{8,28},{10,30},{12,24},{14,26},{16,4},... | collective-permute-start | bytes 393224 | tf_op jit(solution)/shard_map/ppermute | solution.py:447
  73.4 35.1 %collective-permute-start.12 = (bf16[16,16,256]{2,1,0:T(8,128)(2,1)}, bf16[16,16,256]{2,1,0:T(8,128)(2,1)S(1)}, u32[]{:S(2)}, u32[]{:S(2)}) collective-permute-start(bf16[16,16,256]{2,1,0:T(8,128)(2,1)} %get-tuple-element.45), channel_id=1, source_target_pairs={{0,22},{2,20},{4,18},{6,16},{8,30},{10,28},{12,26},{14,24},{16,6},... | collective-permute-start | bytes 393224 | tf_op jit(solution)/shard_map/ppermute | solution.py:447
  75.0 33.5 %collective-permute-start.13 = (bf16[16,16,256]{2,1,0:T(8,128)(2,1)}, bf16[16,16,256]{2,1,0:T(8,128)(2,1)S(1)}, u32[]{:S(2)}, u32[]{:S(2)}) collective-permute-start(bf16[16,16,256]{2,1,0:T(8,128)(2,1)} %get-tuple-element.46), channel_id=1, source_target_pairs={{0,24},{2,26},{4,28},{6,30},{8,16},{10,18},{12,20},{14,22},{16,8},... | collective-permute-start | bytes 393224 | tf_op jit(solution)/shard_map/ppermute | solution.py:447
  86.9 21.7 %collective-permute-start.14 = (bf16[16,16,256]{2,1,0:T(8,128)(2,1)S(1)}, bf16[16,16,256]{2,1,0:T(8,128)(2,1)S(1)}, u32[]{:S(2)}, u32[]{:S(2)}) collective-permute-start(bf16[16,16,256]{2,1,0:T(8,128)(2,1)S(1)} %copy-done.32), channel_id=1, source_target_pairs={{0,26},{2,24},{4,30},{6,28},{8,18},{10,16},{12,22},{14,20},{16,10}... | collective-permute-start | bytes 393224 | tf_op jit(solution)/shard_map/ppermute | solution.py:447
  88.7 19.9 %collective-permute-start.15 = (bf16[16,16,256]{2,1,0:T(8,128)(2,1)S(1)}, bf16[16,16,256]{2,1,0:T(8,128)(2,1)S(1)}, u32[]{:S(2)}, u32[]{:S(2)}) collective-permute-start(bf16[16,16,256]{2,1,0:T(8,128)(2,1)S(1)} %copy-done.31), channel_id=1, source_target_pairs={{0,28},{2,30},{4,24},{6,26},{8,20},{10,22},{12,16},{14,18},{16,12}... | collective-permute-start | bytes 393224 | tf_op jit(solution)/shard_map/ppermute | solution.py:447
  98.4 10.2 %collective-permute-start.16 = (bf16[16,16,256]{2,1,0:T(8,128)(2,1)S(1)}, bf16[16,16,256]{2,1,0:T(8,128)(2,1)S(1)}, u32[]{:S(2)}, u32[]{:S(2)}) collective-permute-start(bf16[16,16,256]{2,1,0:T(8,128)(2,1)S(1)} %copy-done.30), channel_id=1, source_target_pairs={{0,30},{2,28},{4,26},{6,24},{8,22},{10,20},{12,18},{14,16},{16,14}... | collective-permute-start | bytes 393224 | tf_op jit(solution)/shard_map/ppermute | solution.py:447
  117.7 29.7 %all-to-all-start.3 = ((bf16[16,8,16,256]{3,2,1,0:T(8,128)(2,1)}), bf16[16,8,16,256]{3,2,1,0:T(8,128)(2,1)S(1)}, u32[]{:S(2)}, u32[]{:S(2)}) async-start(bf16[16,8,16,256]{3,2,1,0:T(8,128)(2,1)} %shard_map.38), calls=%async_computation.3 | async-start | bytes 2097152 | tf_op jit(solution)/shard_map/all_to_all | solution.py:476
  127.2 2.9 %collective-permute-start.17 = (bf16[8,16,16,256]{3,2,1,0:T(8,128)(2,1)}, bf16[8,16,16,256]{3,2,1,0:T(8,128)(2,1)S(1)}, u32[]{:S(2)}, u32[]{:S(2)}) collective-permute-start(bf16[8,16,16,256]{3,2,1,0:T(8,128)(2,1)} %gather.1), channel_id=1, source_target_pairs={{0,1},{1,0},{2,3},{3,2},{4,5},{5,4},{6,7},{7,6},{8,9},{9,8},{10,11... | collective-permute-start | bytes 3145736 | tf_op jit(solution)/shard_map/ppermute | solution.py:455
  127.2 4.5 %collective-permute-start.8 = (bf16[8,16,16,256]{3,2,1,0:T(8,128)(2,1)S(1)}, bf16[8,16,16,256]{3,2,1,0:T(8,128)(2,1)}, u32[]{:S(2)}, u32[]{:S(2)}) collective-permute-start(bf16[8,16,16,256]{3,2,1,0:T(8,128)(2,1)S(1)} %copy-done.3), channel_id=1, source_target_pairs={{0,1},{1,0},{2,3},{3,2},{4,5},{5,4},{6,7},{7,6},{8,9},{9,8},{10,11... | collective-permute-start | bytes 3145736 | tf_op jit(solution)/shard_map/ppermute | solution.py:455
  147.4 34.2 %all-to-all-start.2 = ((bf16[8,8,16,256]{3,2,1,0:T(8,128)(2,1)}), bf16[8,8,16,256]{3,2,1,0:T(8,128)(2,1)S(1)}, u32[]{:S(2)}, u32[]{:S(2)}) async-start(bf16[8,8,16,256]{3,2,1,0:T(8,128)(2,1)} %get-tuple-element.50), calls=%async_computation.2 | async-start | bytes 1048576 | tf_op jit(solution)/shard_map/all_to_all | solution.py:450
  151.9 10.5 %collective-permute-start.18 = (bf16[8,16,256]{2,1,0:T(8,128)(2,1)}, bf16[8,16,256]{2,1,0:T(8,128)(2,1)S(1)}, u32[]{:S(2)}, u32[]{:S(2)}) collective-permute-start(bf16[8,16,256]{2,1,0:T(8,128)(2,1)} %get-tuple-element.51), channel_id=1, source_target_pairs={{0,16},{2,18},{4,20},{6,22},{8,24},{10,26},{12,28},{14,30},{16,0},... | collective-permute-start | bytes 196616 | tf_op jit(solution)/shard_map/ppermute | solution.py:447
  153.4 11.5 %collective-permute-start.19 = (bf16[8,16,256]{2,1,0:T(8,128)(2,1)}, bf16[8,16,256]{2,1,0:T(8,128)(2,1)S(1)}, u32[]{:S(2)}, u32[]{:S(2)}) collective-permute-start(bf16[8,16,256]{2,1,0:T(8,128)(2,1)} %get-tuple-element.52), channel_id=1, source_target_pairs={{0,18},{2,16},{4,22},{6,20},{8,26},{10,24},{12,30},{14,28},{16,2},... | collective-permute-start | bytes 196616 | tf_op jit(solution)/shard_map/ppermute | solution.py:447
  156.3 17.2 %collective-permute-start.20 = (bf16[8,16,256]{2,1,0:T(8,128)(2,1)}, bf16[8,16,256]{2,1,0:T(8,128)(2,1)S(1)}, u32[]{:S(2)}, u32[]{:S(2)}) collective-permute-start(bf16[8,16,256]{2,1,0:T(8,128)(2,1)} %get-tuple-element.53), channel_id=1, source_target_pairs={{0,20},{2,22},{4,16},{6,18},{8,28},{10,30},{12,24},{14,26},{16,4},... | collective-permute-start | bytes 196616 | tf_op jit(solution)/shard_map/ppermute | solution.py:447
  158.6 18.9 %collective-permute-start.21 = (bf16[8,16,256]{2,1,0:T(8,128)(2,1)}, bf16[8,16,256]{2,1,0:T(8,128)(2,1)S(1)}, u32[]{:S(2)}, u32[]{:S(2)}) collective-permute-start(bf16[8,16,256]{2,1,0:T(8,128)(2,1)} %get-tuple-element.54), channel_id=1, source_target_pairs={{0,22},{2,20},{4,18},{6,16},{8,30},{10,28},{12,26},{14,24},{16,6},... | collective-permute-start | bytes 196616 | tf_op jit(solution)/shard_map/ppermute | solution.py:447
  159.6 18.0 %collective-permute-start.22 = (bf16[8,16,256]{2,1,0:T(8,128)(2,1)}, bf16[8,16,256]{2,1,0:T(8,128)(2,1)S(1)}, u32[]{:S(2)}, u32[]{:S(2)}) collective-permute-start(bf16[8,16,256]{2,1,0:T(8,128)(2,1)} %get-tuple-element.55), channel_id=1, source_target_pairs={{0,24},{2,26},{4,28},{6,30},{8,16},{10,18},{12,20},{14,22},{16,8},... | collective-permute-start | bytes 196616 | tf_op jit(solution)/shard_map/ppermute | solution.py:447
  162.5 15.1 %collective-permute-start.23 = (bf16[8,16,256]{2,1,0:T(8,128)(2,1)}, bf16[8,16,256]{2,1,0:T(8,128)(2,1)S(1)}, u32[]{:S(2)}, u32[]{:S(2)}) collective-permute-start(bf16[8,16,256]{2,1,0:T(8,128)(2,1)} %get-tuple-element.56), channel_id=1, source_target_pairs={{0,26},{2,24},{4,30},{6,28},{8,18},{10,16},{12,22},{14,20},{16,10}... | collective-permute-start | bytes 196616 | tf_op jit(solution)/shard_map/ppermute | solution.py:447
  164.9 12.7 %collective-permute-start.24 = (bf16[8,16,256]{2,1,0:T(8,128)(2,1)}, bf16[8,16,256]{2,1,0:T(8,128)(2,1)S(1)}, u32[]{:S(2)}, u32[]{:S(2)}) collective-permute-start(bf16[8,16,256]{2,1,0:T(8,128)(2,1)} %get-tuple-element.57), channel_id=1, source_target_pairs={{0,28},{2,30},{4,24},{6,26},{8,20},{10,22},{12,16},{14,18},{16,12}... | collective-permute-start | bytes 196616 | tf_op jit(solution)/shard_map/ppermute | solution.py:447
  173.5 8.1 %collective-permute-start.25 = (bf16[8,16,256]{2,1,0:T(8,128)(2,1)}, bf16[8,16,256]{2,1,0:T(8,128)(2,1)S(1)}, u32[]{:S(2)}, u32[]{:S(2)}) collective-permute-start(bf16[8,16,256]{2,1,0:T(8,128)(2,1)} %get-tuple-element.58), channel_id=1, source_target_pairs={{0,30},{2,28},{4,26},{6,24},{8,22},{10,20},{12,18},{14,16},{16,14}... | collective-permute-start | bytes 196616 | tf_op jit(solution)/shard_map/ppermute | solution.py:447
  (38 other events, 555.9 us)

commit v3 on v2

--- a/solution.py
+++ b/solution.py
@@ -172,6 +172,7 @@
 
 PAD = 8
 LANES = 4
+TRANSFORM_MIB = 32
 
 
 def blocks_of(half, place, kept, far):
@@ -192,14 +193,14 @@
         message[slot, :, side * 128 : side * 128 + 128] = piece.astype(jnp.bfloat16)
 
 
-def pack_tokens_kernel(half, groups, place, tokens, kept, *rest):
-    far, scratch = rest[:half], rest[half]
+def pack_tokens_kernel(half, place, tokens, *rest):
+    kept, *far, scratch = rest
     step = pl.program_id(0)
-    rows, _, channels = tokens.shape
-    stride = channels + PAD
-    own = channels // (groups * 2 * half)
+    rows, _, held = tokens.shape
+    stride = held + PAD
+    own = held // (2 * half)
     for row in range(rows):
-        at = pl.ds(pl.multiple_of((step * rows + row) * stride, PAD), channels)
+        at = pl.ds(pl.multiple_of((step * rows + row) * stride, PAD), held)
         put_rows(scratch, at, tokens[row].T.astype(jnp.float32))
 
     @pl.when(step == pl.num_programs(0) - 1)
@@ -207,15 +208,13 @@
         for target, message in blocks_of(half, place, kept, far):
 
             def fill(lane, _):
-                for group in range(groups):
-                    start = group * (channels // groups) + target * own + lane
-                    send_rows(scratch, start, stride, message, group * own + lane)
+                send_rows(scratch, target * own + lane, stride, message, lane)
                 return 0
 
-            lax.fori_loop(0, own, fill, 0, unroll=2)
-
-
-def pack_filters_kernel(half, place, filters, kept, *rest):
+            lax.fori_loop(0, own, fill, 0, unroll=4)
+
+
+def pack_filters_kernel(half, place, filters, before, kept, *rest):
     far, scratch = rest[:half], rest[half]
     step = pl.program_id(0)
     _, rows, _, held = filters.shape
@@ -229,12 +228,14 @@
 
     @pl.when(step == pl.num_programs(0) - 1)
     def _():
-        for target, message in blocks_of(half, place, kept, far):
+        kept[:, :own] = before[...]
+        for number, (target, message) in enumerate(blocks_of(half, place, kept, far)):
+            first = own if number < half else 0
 
             def fill(lane, _):
                 for part in range(2):
                     start = part * total * stride + target * own + lane
-                    send_rows(scratch, start, stride, message, 2 * lane + part)
+                    send_rows(scratch, start, stride, message, first + 2 * lane + part)
                 return 0
 
             lax.fori_loop(0, own, fill, 0, unroll=2)
@@ -249,32 +250,38 @@
     return [jax.ShapeDtypeStruct((half, slots, rows, N2), jnp.bfloat16)] + [message] * half
 
 
-def pack_tokens(place, tokens, half, groups):
+def pack_tokens(place, tokens, half, groups, other):
     rows, _, channels = tokens.shape
+    held = channels // groups
+    own = held // (2 * half)
     steps = 2
-    return pl.pallas_call(
-        functools.partial(pack_tokens_kernel, half, groups),
-        grid=(steps,),
-        in_specs=[SMEM, pl.BlockSpec((rows // steps, N2, channels), lambda s: (s, 0, 0))],
-        out_specs=[VMEM] * (half + 1),
-        out_shape=message_shapes(half, channels // (2 * half), rows),
-        scratch_shapes=[pltpu.VMEM((2, rows * (channels + PAD), 128), jnp.float32)],
-        name="pack_tokens",
+    block = pl.BlockSpec((rows // steps, N2, held), lambda s, place: (s, 0, place[2] ^ other))
+    return pl.pallas_call(
+        functools.partial(pack_tokens_kernel, half),
+        grid_spec=pltpu.PrefetchScalarGridSpec(
+            num_scalar_prefetch=1,
+            grid=(steps,),
+            in_specs=[block],
+            out_specs=[VMEM] * (half + 1),
+            scratch_shapes=[pltpu.VMEM((2, rows * (held + PAD), 128), jnp.float32)],
+        ),
+        out_shape=message_shapes(half, own, rows),
     )(place, tokens)
 
 
-def pack_filters(place, filters, half):
+def pack_filters(place, filters, before, half):
     _, rows, _, held = filters.shape
     steps = 2
+    kept = jax.ShapeDtypeStruct((half, before.shape[1] + held // half, rows, N2), jnp.bfloat16)
     return pl.pallas_call(
         functools.partial(pack_filters_kernel, half),
         grid=(steps,),
-        in_specs=[SMEM, pl.BlockSpec((2, rows // steps, N2, held), lambda s: (0, s, 0, 0))],
+        in_specs=[SMEM, pl.BlockSpec((2, rows // steps, N2, held), lambda s: (0, s, 0, 0)), VMEM],
         out_specs=[VMEM] * (half + 1),
-        out_shape=message_shapes(half, held // half, rows),
+        out_shape=[kept] + message_shapes(half, held // half, rows)[1:],
         scratch_shapes=[pltpu.VMEM((2, 2 * rows * (held + PAD), 128), jnp.float32)],
         name="pack_filters",
-    )(place, filters)
+    )(place, filters, before)
 
 
 def gather_kernel(*refs):
@@ -289,80 +296,56 @@
         in_specs=[VMEM] * len(far),
         out_specs=VMEM,
         out_shape=jax.ShapeDtypeStruct((len(far), *far[0].shape), jnp.bfloat16),
+        compiler_params=pltpu.CompilerParams(vmem_limit_bytes=8 * 1024 * 1024),
         name="gather",
     )(*far)
 
 
-def take(kept, far, slot):
-    near = kept[:, pl.ds(slot, 1)].reshape(N1 // 2, N2)
+def take(near, far, near_slot, far_slot):
     if not isinstance(far, (list, tuple)):
-        return near, far[:, pl.ds(slot, 1)].reshape(N1 // 2, N2)
-    across = [ref[pl.ds(slot, 1)].reshape(ref.shape[1], N2) for ref in far]
-    return near, jnp.concatenate(across, axis=0)
-
-
-def forward_kernel(half, lanes, kept, *rest):
+        across = [far[:, pl.ds(far_slot, 1)].reshape(N1 // 2, N2)]
+    else:
+        across = [ref[pl.ds(far_slot, 1)].reshape(ref.shape[1], N2) for ref in far]
+    return jnp.concatenate([near[:, pl.ds(near_slot, 1)].reshape(N1 // 2, N2), *across], axis=0)
+
+
+def transform_kernel(half, own, other, whole, parts, lanes, place, gain, kept, *rest):
     far = rest[:half]
-    rows_t, twiddle, cols_t, spectrum = rest[half:]
-    slots = [pl.program_id(0) * lanes + lane for lane in range(lanes)]
+    rows_t, twiddle, cols_t, back_t, final_t = rest[half : half + 5]
+    filters, outs = rest[half + 5 : half + 5 + parts], rest[half + 5 + parts :]
+    near_filter, far_filter = (kept, filters) if parts == half else filters
+    index, base, core = place[0], place[1], place[2]
+    piece = kept.shape[2]
+    channels = [pl.program_id(0) * lanes + number for number in range(lanes)]
+
     turned = []
-    for slot in slots:
-        signal = jnp.concatenate(take(kept, far, slot), axis=0)
-        section = dot(rows_t[...].reshape(2 * N1, N1), signal)
+    for lane in channels:
+        section = dot(rows_t[...].reshape(2 * N1, N1), take(kept, far, lane, lane))
         real, imag = section[:N1], section[N1:]
         turned_real = (real * twiddle[0] + imag * twiddle[1]).astype(jnp.bfloat16)
         turned_imag = (imag * twiddle[0] - real * twiddle[1]).astype(jnp.bfloat16)
         turned.append(jnp.concatenate([turned_real, turned_imag], axis=1))
-    result = dot(jnp.concatenate(turned, axis=0), cols_t[...].reshape(2 * N2, 2 * N2))
-    for lane, slot in enumerate(slots):
-        spectrum[slot] = result[lane * N1 : (lane + 1) * N1].astype(jnp.bfloat16)
-
-
-def forward(messages, rows_t, twiddle, cols_t):
-    kept, *far = messages
-    half, slots = kept.shape[:2]
-    return pl.pallas_call(
-        functools.partial(forward_kernel, half, LANES),
-        grid=(slots // LANES,),
-        in_specs=[VMEM] * (half + 4),
-        out_specs=VMEM,
-        out_shape=jax.ShapeDtypeStruct((slots, N1, 2 * N2), jnp.bfloat16),
-        name="forward",
-    )(kept, *far, rows_t, twiddle, cols_t)
-
-
-def inverse_kernel(half, own, other, whole, parts, lanes, place, gain, kept, *rest):
-    far = rest[:half]
-    spectrum, twiddle, back_t, final_t, near_filter = rest[half : half + 5]
-    far_filter = rest[half + 5 : half + 5 + parts]
-    if parts == 1:
-        far_filter = far_filter[0]
-    outs = rest[half + 5 + parts :]
-    index, base, core = place[0], place[1], place[2]
-    piece = kept.shape[2]
-    group = core ^ other
+    spectrum = dot(jnp.concatenate(turned, axis=0), cols_t[...].reshape(2 * N2, 2 * N2))
+    spectrum = spectrum.astype(jnp.bfloat16)
     products = []
-    lanes_all = [pl.program_id(0) * lanes + number for number in range(lanes)]
-    for lane in lanes_all:
-        slot = group * own + lane
-        weight_real = jnp.concatenate(take(near_filter, far_filter, 2 * lane), axis=0).astype(jnp.float32)
-        weight_imag = jnp.concatenate(take(near_filter, far_filter, 2 * lane + 1), axis=0).astype(jnp.float32)
-        spec_real = spectrum[slot, :, :N2].astype(jnp.float32)
-        spec_imag = spectrum[slot, :, N2:].astype(jnp.float32)
+    for number, lane in enumerate(channels):
+        real, imag = 2 * lane, 2 * lane + 1
+        weight_real = take(near_filter, far_filter, own + real, real).astype(jnp.float32)
+        weight_imag = take(near_filter, far_filter, own + imag, imag).astype(jnp.float32)
+        spec_real = spectrum[number * N1 : (number + 1) * N1, :N2].astype(jnp.float32)
+        spec_imag = spectrum[number * N1 : (number + 1) * N1, N2:].astype(jnp.float32)
         prod_real = (spec_real * weight_real - spec_imag * weight_imag).astype(jnp.bfloat16)
         prod_imag = (spec_real * weight_imag + spec_imag * weight_real).astype(jnp.bfloat16)
         products.append(jnp.concatenate([prod_real, prod_imag], axis=1))
     back = dot(jnp.concatenate(products, axis=0), back_t[...].reshape(2 * N2, 2 * N2))
-    for number, lane in enumerate(lanes_all):
+    for number, lane in enumerate(channels):
         back_real = back[number * N1 : (number + 1) * N1, :N2]
         back_imag = back[number * N1 : (number + 1) * N1, N2:]
         turned_real = (back_real * twiddle[0] - back_imag * twiddle[1]).astype(jnp.bfloat16)
         turned_imag = (back_real * twiddle[1] + back_imag * twiddle[0]).astype(jnp.bfloat16)
         filtered = dot(final_t[...], jnp.concatenate([turned_real, turned_imag], axis=0))
-        slot = group * own + lane
-        weight = gain[(group * 2 * half + index) * own + lane]
-        direct = jnp.concatenate(take(kept, far, slot), axis=0).astype(jnp.float32)
-        result = (filtered + weight * direct).astype(jnp.bfloat16)
+        weight = gain[((core ^ other) * 2 * half + index) * own + lane]
+        result = (filtered + weight * take(kept, far, lane, lane).astype(jnp.float32)).astype(jnp.bfloat16)
         near = pl.ds(base, half) if whole else pl.ds(0, half)
         outs[0][near, pl.ds(lane, 1)] = result[: N1 // 2].reshape(half, 1, piece, N2)
         for step in range(half):
@@ -374,20 +357,21 @@
                 outs[1 + step][pl.ds(lane, 1)] = rows
 
 
-def inverse(place, gain, messages, spectrum, tables, filters, own, other, whole):
-    kept, *far = messages
+def transform(place, gain, kept, far, tables, filters, other, whole):
     half, _, rows, _ = kept.shape
+    own = far[0].shape[0]
     if whole:
         out_shape = [jax.ShapeDtypeStruct((2 * half, own, rows, N2), jnp.bfloat16)]
     else:
         out_shape = message_shapes(half, own, rows)
-    inputs = [kept, *far, spectrum, *tables, *filters]
-    return pl.pallas_call(
-        functools.partial(inverse_kernel, half, own, other, whole, len(filters) - 1, LANES),
+    inputs = [kept, *far, *tables, *filters]
+    return pl.pallas_call(
+        functools.partial(transform_kernel, half, own, other, whole, len(filters), LANES),
         grid=(own // LANES,),
         in_specs=[SMEM, SMEM] + [VMEM] * len(inputs),
         out_specs=[VMEM] * len(out_shape),
         out_shape=out_shape,
+        compiler_params=pltpu.CompilerParams(vmem_limit_bytes=TRANSFORM_MIB * 1024 * 1024),
     )(place, gain, *inputs)
 
 
@@ -436,19 +420,22 @@
         ),
         out_shape=jax.ShapeDtypeStruct((rows, N2, channels), jnp.bfloat16),
         input_output_aliases={1 + len(received): 0} if partial else {},
+        compiler_params=pltpu.CompilerParams(vmem_limit_bytes=12 * 1024 * 1024),
     )(place, *inputs)
 
 
-def exchange(messages, count):
-    kept, *far = messages
+def cross(far, count):
     half = count // 2
-    halves = [list(range(half)), list(range(half, count))]
-    across = [
+    return [
         lax.ppermute(block, "seq", [(s, s ^ (half + step)) for s in range(count)])
         for step, block in enumerate(far)
     ]
-    near = lax.all_to_all(kept, "seq", split_axis=0, concat_axis=0, tiled=True, axis_index_groups=halves)
-    return [near, *across]
+
+
+def near(kept, count):
+    half = count // 2
+    halves = [list(range(half)), list(range(half, count))]
+    return lax.all_to_all(kept, "seq", split_axis=0, concat_axis=0, tiled=True, axis_index_groups=halves)
 
 
 def swap(array):
@@ -463,26 +450,27 @@
     _, local_length, channels = tokens.shape
     rows = N1 // count
     half = count // 2
-    own = channels // (groups * count)
     place = jnp.stack([index, index // half * half, core]).astype(jnp.int32)
-    messages = pack_tokens(place, tokens.reshape(rows, N2, channels), half, groups)
-    signal = exchange(messages, count)
-    messages = pack_filters(place, filter_spectrum, half)
-    filters = exchange(messages, count)
-    rows_t, twiddle, cols_t, back_t, final_t = dft_tables(relative_rows(index, count, rows))
-    spectrum = forward(signal, rows_t, twiddle, cols_t)
-    tables = (twiddle, back_t, jnp.concatenate([final_t[0], final_t[1]], axis=1))
-    (ready,) = inverse(place, skip_gain, signal, spectrum, tables, filters, own, 0, True)
+    laid = tokens.reshape(rows, N2, channels)
+    kept, *far = pack_tokens(place, laid, half, groups, 0)
+    far_own = cross(far, count)
+    kept, *far = pack_filters(place, filter_spectrum, kept, half)
+    far_filters = cross(far, count)
+    kept_own = near(kept, count)
+    kept, *far = pack_tokens(place, laid, half, groups, 1)
+    far_other = cross(far, count)
+    kept_other = near(kept, count)
+    *tables, final_t = dft_tables(relative_rows(index, count, rows))
+    tables.append(jnp.concatenate([final_t[0], final_t[1]], axis=1))
+    (ready,) = transform(place, skip_gain, kept_own, far_own, tables, far_filters, 0, True)
     first = lax.all_to_all(ready, "seq", split_axis=0, concat_axis=0, tiled=True)
-    near_filter = swap(filters[0])
-    far_filter = gather(filters[1:])
-    far_filter = swap(far_filter)
-    messages = inverse(
-        place, skip_gain, signal, spectrum, tables, (near_filter, far_filter), own, 1, False
-    )
-    second = exchange(messages, count)
+    gathered = gather(far_filters)
+    filters = (swap(kept_own), swap(gathered))
+    kept, *far = transform(place, skip_gain, kept_other, far_other, tables, filters, 1, False)
+    far = cross(far, count)
+    kept = near(kept, count)
     mixed = unpack(place, [first], rows, channels, groups, half, 0, [])
-    mixed = unpack(place, second, rows, channels, groups, half, 1, [mixed])
+    mixed = unpack(place, [kept, *far], rows, channels, groups, half, 1, [mixed])
     return mixed.reshape(1, local_length, channels)
 
 

time: 187 us -> 210 us (1.12)
  starting transfers between devices: 87.9 us -> 105 us
  Pallas kernels: 41.6 us -> 28.9 us
  local copies, waits for them, and re-layouts: 3.33 us -> 14.2 us
  waiting for transfers between devices: 42.4 us -> 50.1 us
    ppermute x24 -> x32, waiting for transfers between devices: 22.7 us -> 44 us  [cross(): lax.ppermute(block, 'seq', [(s, s ^ half + step) for s in range(count)])]
    ppermute x24 -> x32, starting transfers between devices: 65.6 us -> 86 us  [cross(): lax.ppermute(block, 'seq', [(s, s ^ half + step) for s in range(count)])]
    unnamed x80 -> x86, local copies, waits for them, and re-layouts: 3.23 us -> 14.1 us
    pallas_call x4, Pallas kernels: 27.3 us -> 18.1 us  [the longest x2 10.8 us: transform(): pl.pallas_call(functools.partial(transform_kernel, half, own, other, whol...]
    all_to_all x1, waiting for transfers between devices: 8.31 us -> 0.01 us  [direct_body(): lax.all_to_all(ready, 'seq', split_axis=0, concat_axis=0, tiled=True)]
    ppermute x2, waiting for transfers between devices: 3.99 us -> 0.01 us  [swap(): return lax.ppermute(array, 'bat', [(0, 1), (1, 0)])]
    all_to_all x1, starting transfers between devices: 7.14 us -> 4.48 us  [direct_body(): lax.all_to_all(ready, 'seq', split_axis=0, concat_axis=0, tiled=True)]
    pallas_call x1, Pallas kernels: 2.4 us -> 0.07 us  [gather(): pl.pallas_call(gather_kernel, in_specs=[VMEM] * len(far), out_specs=VMEM,...]
  transfers between devices with their start and end apart: 30 -> 38, of which waited for: 9 -> 13; matrix products, arithmetic and copies ran while one was open for 6% -> 5% of each run, Pallas kernels for 14% -> 9%
where the time goes in v3:
time: 210 us; the launch traced here: 209 us
  starting transfers between devices  105 us (50%)
  waiting for transfers between devices  50.1 us (24%)
  Pallas kernels  28.9 us (14%)
  local copies, waits for them, and re-layouts  14.2 us (7%)
  other arithmetic  9.95 us (5%)
    ppermute x32, starting transfers between devices, cross(): lax.ppermute(block, 'seq', [(s, s ^ half + step) for s in range(count)])  86 us
    ppermute x32, waiting for transfers between devices, cross(): lax.ppermute(block, 'seq', [(s, s ^ half + step) for s in range(count)])  44 us
    all_to_all x3, starting transfers between devices, near(): lax.all_to_all(kept, 'seq', split_axis=0, concat_axis=0, tiled=True, axis...  14.4 us
    unnamed x86, local copies, waits for them, and re-layouts  14.1 us
    pallas_call x2, Pallas kernels, transform(): pl.pallas_call(functools.partial(transform_kernel, half, own, other, whol...  10.8 us
    pallas_call x2, Pallas kernels, pack_tokens(): pl.pallas_call(functools.partial(pack_tokens_kernel, half), grid_spec=plt...  7.32 us
    pallas_call x2, Pallas kernels, unpack(): pl.pallas_call(functools.partial(unpack_kernel, half, whole), grid_spec=p...  6.16 us
    all_to_all x3, waiting for transfers between devices, near(): lax.all_to_all(kept, 'seq', split_axis=0, concat_axis=0, tiled=True, axis...  6.14 us
  transfers between devices with their start and end apart: 38, of which 13 were waited for; matrix products, arithmetic and copies ran while one was open for 5% of the time, Pallas kernels for 9%

profile of v3, /device:TPU:0, one launch (start us, length us, event | category | flops | bytes accessed | tf_op | source)
XLA Modules:
  0.0 209.1 jit_solution(9767735601896553588)
XLA Ops:
  0.6 3.6 %shard_map.38 = (bf16[8,8,16,256]{3,2,1,0:T(8,128)(2,1)}, bf16[8,16,256]{2,1,0:T(8,128)(2,1)}, bf16[8,16,256]{2,1,0:T(8,128)(2,1)}, bf16[8,16,256]{2,1,0:T(8,128...) custom-call(s32[3]{0:T(128)} %pad_add_fusion.place, ...), custom_call_target="tpu_custom_call" | custom-call | tf_op jit(solution)/shard_map/pallas_call | solution.py:259
  4.3 4.6 %pack_filters.1 = (bf16[8,24,16,256]{3,2,1,0:T(8,128)(2,1)}, bf16[16,16,256]{2,1,0:T(8,128)(2,1)}, bf16[16,16,256]{2,1,0:T(8,128)(2,1)}, bf16[16,16,256]{2,1,0:T...) custom-call(s32[3]{0:T(128)} %pad_add_fusion.place, ...), custom_call_target="tpu_custom_call" | custom-call | tf_op jit(solution)/shard_map/pack_filters/pallas_call | solution.py:276
  8.8 6.2 %all-to-all-start.1 = ((bf16[8,24,16,256]{3,2,1,0:T(8,128)(2,1)}), bf16[8,24,16,256]{3,2,1,0:T(8,128)(2,1)S(1)}, u32[]{:S(2)}, u32[]{:S(2)}) async-start(bf16[8,24,16,256]{3,2,1,0:T(8,128)(2,1)} %get-tuple-element.51), calls=%async_computation.1 | async-start | bytes 3145728 | tf_op jit(solution)/shard_map/all_to_all | solution.py:438
  15.0 4.0 %collective-permute-start.10 = (bf16[16,16,256]{2,1,0:T(8,128)(2,1)}, bf16[16,16,256]{2,1,0:T(8,128)(2,1)S(1)}, u32[]{:S(2)}, u32[]{:S(2)}) collective-permute-start(bf16[16,16,256]{2,1,0:T(8,128)(2,1)} %get-tuple-element.53), channel_id=1, source_target_pairs={{0,18},{2,16},{4,22},{6,20},{8,26},{10,24},{12,30},{14,28},{16,2},... | collective-permute-start | bytes 393224 | tf_op jit(solution)/shard_map/ppermute | solution.py:430
  23.2 3.5 %collective-permute-start.29 = (bf16[8,16,256]{2,1,0:T(8,128)(2,1)}, bf16[8,16,256]{2,1,0:T(8,128)(2,1)S(1)}, u32[]{:S(2)}, u32[]{:S(2)}) collective-permute-start(bf16[8,16,256]{2,1,0:T(8,128)(2,1)} %get-tuple-element.72), channel_id=1, source_target_pairs={{0,22},{2,20},{4,18},{6,16},{8,30},{10,28},{12,26},{14,24},{16,6},... | collective-permute-start | bytes 196616 | tf_op jit(solution)/shard_map/ppermute | solution.py:430
  26.7 3.7 %shard_map.37 = (bf16[8,8,16,256]{3,2,1,0:T(8,128)(2,1)}, bf16[8,16,256]{2,1,0:T(8,128)(2,1)}, bf16[8,16,256]{2,1,0:T(8,128)(2,1)}, bf16[8,16,256]{2,1,0:T(8,128...) custom-call(s32[3]{0:T(128)} %pad_add_fusion.place, ...), custom_call_target="tpu_custom_call" | custom-call | tf_op jit(solution)/shard_map/pallas_call | solution.py:259
  36.8 6.1 %all-to-all-done.1.kept = bf16[8,24,16,256]{3,2,1,0:T(8,128)(2,1)S(1)} async-done(((bf16[8,24,16,256]{3,2,1,0:T(8,128)(2,1)}), bf16[8,24,16,256]{3,2,1,0:T(8,128)(2,1)S(1)}, u32[]{:S(2)}, u32[]{:S(2)}) %all-to-all-start.1) | async-done | bytes 1572896 | tf_op jit(solution)/shard_map/all_to_all | solution.py:438
  42.9 4.7 %all-to-all-start = ((bf16[8,8,16,256]{3,2,1,0:T(8,128)(2,1)}), bf16[8,8,16,256]{3,2,1,0:T(8,128)(2,1)}, u32[]{:S(2)}, u32[]{:S(2)}) async-start(bf16[8,8,16,256]{3,2,1,0:T(8,128)(2,1)} %get-tuple-element.41), calls=%async_computation | async-start | bytes 1048576 | tf_op jit(solution)/shard_map/all_to_all | solution.py:438
  48.8 4.0 %collective-permute-start.11 = (bf16[16,16,256]{2,1,0:T(8,128)(2,1)}, bf16[16,16,256]{2,1,0:T(8,128)(2,1)S(1)}, u32[]{:S(2)}, u32[]{:S(2)}) collective-permute-start(bf16[16,16,256]{2,1,0:T(8,128)(2,1)} %get-tuple-element.54), channel_id=1, source_target_pairs={{0,20},{2,22},{4,16},{6,18},{8,28},{10,30},{12,24},{14,26},{16,4},... | collective-permute-start | bytes 393224 | tf_op jit(solution)/shard_map/ppermute | solution.py:430
  54.2 3.3 %collective-permute-start.30 = (bf16[8,16,256]{2,1,0:T(8,128)(2,1)}, bf16[8,16,256]{2,1,0:T(8,128)(2,1)S(1)}, u32[]{:S(2)}, u32[]{:S(2)}) collective-permute-start(bf16[8,16,256]{2,1,0:T(8,128)(2,1)} %get-tuple-element.73), channel_id=1, source_target_pairs={{0,24},{2,26},{4,28},{6,30},{8,16},{10,18},{12,20},{14,22},{16,8},... | collective-permute-start | bytes 196616 | tf_op jit(solution)/shard_map/ppermute | solution.py:430
  58.6 6.3 %collective-permute-done.30.rest_4_ = bf16[8,16,256]{2,1,0:T(8,128)(2,1)S(1)} collective-permute-done((bf16[8,16,256]{2,1,0:T(8,128)(2,1)}, bf16[8,16,256]{2,1,0:T(8,128)(2,1)S(1)}, u32[]{:S(2)}, u32[]{:S(2)}) %collective-permute-start.30) | collective-permute-done | bytes 65568 | tf_op jit(solution)/shard_map/ppermute | solution.py:430
  65.7 4.1 %collective-permute-start.33 = (bf16[8,16,256]{2,1,0:T(8,128)(2,1)S(1)}, bf16[8,16,256]{2,1,0:T(8,128)(2,1)S(1)}, u32[]{:S(2)}, u32[]{:S(2)}) collective-permute-start(bf16[8,16,256]{2,1,0:T(8,128)(2,1)S(1)} %copy-done.41), channel_id=1, source_target_pairs={{0,30},{2,28},{4,26},{6,24},{8,22},{10,20},{12,18},{14,16},{16,14}... | collective-permute-start | bytes 196616 | tf_op jit(solution)/shard_map/ppermute | solution.py:430
  74.1 3.7 %collective-permute-start.14 = (bf16[16,16,256]{2,1,0:T(8,128)(2,1)S(1)}, bf16[16,16,256]{2,1,0:T(8,128)(2,1)S(1)}, u32[]{:S(2)}, u32[]{:S(2)}) collective-permute-start(bf16[16,16,256]{2,1,0:T(8,128)(2,1)S(1)} %copy-done.31), channel_id=1, source_target_pairs={{0,26},{2,24},{4,30},{6,28},{8,18},{10,16},{12,22},{14,20},{16,10}... | collective-permute-start | bytes 393224 | tf_op jit(solution)/shard_map/ppermute | solution.py:430
  79.8 3.5 %collective-permute-start.16 = (bf16[16,16,256]{2,1,0:T(8,128)(2,1)S(1)}, bf16[16,16,256]{2,1,0:T(8,128)(2,1)S(1)}, u32[]{:S(2)}, u32[]{:S(2)}) collective-permute-start(bf16[16,16,256]{2,1,0:T(8,128)(2,1)S(1)} %copy-done.29), channel_id=1, source_target_pairs={{0,30},{2,28},{4,26},{6,24},{8,22},{10,20},{12,18},{14,16},{16,14}... | collective-permute-start | bytes 393224 | tf_op jit(solution)/shard_map/ppermute | solution.py:430
  83.3 12.2 %collective-permute-start.9 = (bf16[16,16,256]{2,1,0:T(8,128)(2,1)S(1)}, bf16[16,16,256]{2,1,0:T(8,128)(2,1)S(1)}, u32[]{:S(2)}, u32[]{:S(2)}) collective-permute-start(bf16[16,16,256]{2,1,0:T(8,128)(2,1)S(1)} %copy-done.28), channel_id=1, source_target_pairs={{0,16},{2,18},{4,20},{6,22},{8,24},{10,26},{12,28},{14,30},{16,0},... | collective-permute-start | bytes 393224 | tf_op jit(solution)/shard_map/ppermute | solution.py:430
  95.7 8.4 %collective-permute-done.9.refs_0_.rest_13_ = bf16[16,16,256]{2,1,0:T(8,128)(2,1)S(1)} collective-permute-done((bf16[16,16,256]{2,1,0:T(8,128)(2,1)S(1)}, bf16[16,16,256]{2,1,0:T(8,128)(2,1)S(1)}, u32[]{:S(2)}, u32[]{:S(2)}) %collective-permute-start.9) | collective-permute-done | bytes 131104 | tf_op jit(solution)/shard_map/ppermute | solution.py:430
  107.5 4.7 %shard_map.40 = bf16[16,8,16,256]{3,2,1,0:T(8,128)(2,1)S(1)} custom-call(s32[3]{0:T(128)S(1)} %copy-done.25, f32[256]{0:T(256)S(1)} %copy-done.26, bf16[8,24,16,256]{3,2,1,0:T(8,128)(2,1)S(1)} %all-to-all-done.1.kept, bf16[8,16,256]{2,1,0:T(8,128)(2,1)S(1)} %copy-done.18, bf16[8,16,256]{2,1,0:T(8,128)(2,1)S(1)} %copy-done.20, ...), custom_call_target="tpu_custom_call" | custom-call | tf_op jit(solution)/shard_map/pallas_call | solution.py:368
  116.4 4.5 %all-to-all-start.3 = ((bf16[16,8,16,256]{3,2,1,0:T(8,128)(2,1)}), bf16[16,8,16,256]{3,2,1,0:T(8,128)(2,1)}, u32[]{:S(2)}, u32[]{:S(2)}) async-start(bf16[16,8,16,256]{3,2,1,0:T(8,128)(2,1)} %copy-done), calls=%async_computation.3 | async-start | bytes 2097152 | tf_op jit(solution)/shard_map/all_to_all | solution.py:466
  128.1 2.8 %collective-permute-start = (bf16[8,16,256]{2,1,0:T(8,128)(2,1)S(1)}, bf16[8,16,256]{2,1,0:T(8,128)(2,1)S(1)}, u32[]{:S(2)}, u32[]{:S(2)}) collective-permute-start(bf16[8,16,256]{2,1,0:T(8,128)(2,1)S(1)} %copy-done.40), channel_id=1, source_target_pairs={{0,16},{2,18},{4,20},{6,22},{8,24},{10,26},{12,28},{14,30},{16,0},... | collective-permute-start | bytes 196616 | tf_op jit(solution)/shard_map/ppermute | solution.py:430
  132.4 3.3 %collective-permute-start.2 = (bf16[8,16,256]{2,1,0:T(8,128)(2,1)S(1)}, bf16[8,16,256]{2,1,0:T(8,128)(2,1)S(1)}, u32[]{:S(2)}, u32[]{:S(2)}) collective-permute-start(bf16[8,16,256]{2,1,0:T(8,128)(2,1)S(1)} %copy-done.38), channel_id=1, source_target_pairs={{0,20},{2,22},{4,16},{6,18},{8,28},{10,30},{12,24},{14,26},{16,4},... | collective-permute-start | bytes 196616 | tf_op jit(solution)/shard_map/ppermute | solution.py:430
  135.6 15.5 %collective-permute-done.rest_0_ = bf16[8,16,256]{2,1,0:T(8,128)(2,1)S(1)} collective-permute-done((bf16[8,16,256]{2,1,0:T(8,128)(2,1)S(1)}, bf16[8,16,256]{2,1,0:T(8,128)(2,1)S(1)}, u32[]{:S(2)}, u32[]{:S(2)}) %collective-permute-start) | collective-permute-done | bytes 65568 | tf_op jit(solution)/shard_map/ppermute | solution.py:430
  154.9 2.9 %collective-permute-start.5 = (bf16[8,16,256]{2,1,0:T(8,128)(2,1)S(1)}, bf16[8,16,256]{2,1,0:T(8,128)(2,1)S(1)}, u32[]{:S(2)}, u32[]{:S(2)}) collective-permute-start(bf16[8,16,256]{2,1,0:T(8,128)(2,1)S(1)} %copy-done.35), channel_id=1, source_target_pairs={{0,26},{2,24},{4,30},{6,28},{8,18},{10,16},{12,22},{14,20},{16,10}... | collective-permute-start | bytes 196616 | tf_op jit(solution)/shard_map/ppermute | solution.py:430
  162.5 2.6 %collective-permute-start.7 = (bf16[8,16,256]{2,1,0:T(8,128)(2,1)S(1)}, bf16[8,16,256]{2,1,0:T(8,128)(2,1)S(1)}, u32[]{:S(2)}, u32[]{:S(2)}) collective-permute-start(bf16[8,16,256]{2,1,0:T(8,128)(2,1)S(1)} %copy-done.33), channel_id=1, source_target_pairs={{0,30},{2,28},{4,26},{6,24},{8,22},{10,20},{12,18},{14,16},{16,14}... | collective-permute-start | bytes 196616 | tf_op jit(solution)/shard_map/ppermute | solution.py:430
  167.0 3.4 %collective-permute-done.7.rest_7_ = bf16[8,16,256]{2,1,0:T(8,128)(2,1)S(1)} collective-permute-done((bf16[8,16,256]{2,1,0:T(8,128)(2,1)S(1)}, bf16[8,16,256]{2,1,0:T(8,128)(2,1)S(1)}, u32[]{:S(2)}, u32[]{:S(2)}) %collective-permute-start.7) | collective-permute-done | bytes 65568 | tf_op jit(solution)/shard_map/ppermute | solution.py:430
  170.4 6.1 %shard_map.39 = (bf16[8,8,16,256]{3,2,1,0:T(8,128)(2,1)}, bf16[8,16,256]{2,1,0:T(8,128)(2,1)S(1)}, bf16[8,16,256]{2,1,0:T(8,128)(2,1)S(1)}, bf16[8,16,256]{2,1,0...) custom-call(s32[3]{0:T(128)S(1)} %copy-done.25, ...), custom_call_target="tpu_custom_call" | custom-call | tf_op jit(solution)/shard_map/pallas_call | solution.py:368
  176.5 3.5 %all-to-all-start.2 = ((bf16[8,8,16,256]{3,2,1,0:T(8,128)(2,1)}), bf16[8,8,16,256]{3,2,1,0:T(8,128)(2,1)S(1)}, u32[]{:S(2)}, u32[]{:S(2)}) async-start(bf16[8,8,16,256]{3,2,1,0:T(8,128)(2,1)} %get-tuple-element.60), calls=%async_computation.2 | async-start | bytes 1048576 | tf_op jit(solution)/shard_map/all_to_all | solution.py:438
  180.0 2.6 %collective-permute-start.18 = (bf16[8,16,256]{2,1,0:T(8,128)(2,1)S(1)}, bf16[8,16,256]{2,1,0:T(8,128)(2,1)S(1)}, u32[]{:S(2)}, u32[]{:S(2)}) collective-permute-start(bf16[8,16,256]{2,1,0:T(8,128)(2,1)S(1)} %get-tuple-element.61), channel_id=1, source_target_pairs={{0,16},{2,18},{4,20},{6,22},{8,24},{10,26},{12,28},{14,30},{16,0},... | collective-permute-start | bytes 196616 | tf_op jit(solution)/shard_map/ppermute | solution.py:430
  184.3 3.6 %collective-permute-start.20 = (bf16[8,16,256]{2,1,0:T(8,128)(2,1)S(1)}, bf16[8,16,256]{2,1,0:T(8,128)(2,1)S(1)}, u32[]{:S(2)}, u32[]{:S(2)}) collective-permute-start(bf16[8,16,256]{2,1,0:T(8,128)(2,1)S(1)} %get-tuple-element.63), channel_id=1, source_target_pairs={{0,20},{2,22},{4,16},{6,18},{8,28},{10,30},{12,24},{14,26},{16,4},... | collective-permute-start | bytes 196616 | tf_op jit(solution)/shard_map/ppermute | solution.py:430
  187.9 3.8 %collective-permute-start.22 = (bf16[8,16,256]{2,1,0:T(8,128)(2,1)}, bf16[8,16,256]{2,1,0:T(8,128)(2,1)S(1)}, u32[]{:S(2)}, u32[]{:S(2)}) collective-permute-start(bf16[8,16,256]{2,1,0:T(8,128)(2,1)} %get-tuple-element.65), channel_id=1, source_target_pairs={{0,24},{2,26},{4,28},{6,30},{8,16},{10,18},{12,20},{14,22},{16,8},... | collective-permute-start | bytes 196616 | tf_op jit(solution)/shard_map/ppermute | solution.py:430
  191.7 4.7 %collective-permute-start.23 = (bf16[8,16,256]{2,1,0:T(8,128)(2,1)}, bf16[8,16,256]{2,1,0:T(8,128)(2,1)S(1)}, u32[]{:S(2)}, u32[]{:S(2)}) collective-permute-start(bf16[8,16,256]{2,1,0:T(8,128)(2,1)} %get-tuple-element.66), channel_id=1, source_target_pairs={{0,26},{2,24},{4,30},{6,28},{8,18},{10,16},{12,22},{14,20},{16,10}... | collective-permute-start | bytes 196616 | tf_op jit(solution)/shard_map/ppermute | solution.py:430
  201.2 3.6 %shard_map.41.rest_9_ = bf16[16,256,256]{2,1,0:T(8,128)(2,1)} custom-call(s32[3]{0:T(128)S(1)} %copy-done.25, bf16[16,8,16,256]{3,2,1,0:T(8,128)(2,1)} %all-to-all-done.3.rest_0_), custom_call_target="tpu_custom_call" | custom-call | tf_op jit(solution)/shard_map/pallas_call | solution.py:412
  206.6 2.5 %shard_map.42 = bf16[16,256,256]{2,1,0:T(8,128)(2,1)} custom-call(s32[3]{0:T(128)S(1)} %copy-done.25, bf16[8,8,16,256]{3,2,1,0:T(8,128)(2,1)S(1)} %all-to-all-done.2.rest_0_, bf16[8,16,256]{2,1,0:T(8,128)(2,1)S(1)} %collective-permute-done.18.rest_1_, bf16[8,16,256]{2,1,0:T(8,128)(2,1)S(1)} %collective-permute-done.19.rest_2_, ...), custom_call_target="tpu_custom_call", output_to_operand_aliasing={{}: (10, {})} | custom-call | tf_op jit(solution)/shard_map/pallas_call | solution.py:412
  (157 shorter events, 56.7 us)
Async XLA Ops:
  8.8 34.1 %all-to-all-start.1 = ((bf16[8,24,16,256]{3,2,1,0:T(8,128)(2,1)}), bf16[8,24,16,256]{3,2,1,0:T(8,128)(2,1)S(1)}, u32[]{:S(2)}, u32[]{:S(2)}) async-start(bf16[8,24,16,256]{3,2,1,0:T(8,128)(2,1)} %get-tuple-element.51), calls=%async_computation.1 | async-start | bytes 3145728 | tf_op jit(solution)/shard_map/all_to_all | solution.py:438
  15.0 62.7 %collective-permute-start.10 = (bf16[16,16,256]{2,1,0:T(8,128)(2,1)}, bf16[16,16,256]{2,1,0:T(8,128)(2,1)S(1)}, u32[]{:S(2)}, u32[]{:S(2)}) collective-permute-start(bf16[16,16,256]{2,1,0:T(8,128)(2,1)} %get-tuple-element.53), channel_id=1, source_target_pairs={{0,18},{2,16},{4,22},{6,20},{8,26},{10,24},{12,30},{14,28},{16,2},... | collective-permute-start | bytes 393224 | tf_op jit(solution)/shard_map/ppermute | solution.py:430
  19.1 29.7 %collective-permute-start.26 = (bf16[8,16,256]{2,1,0:T(8,128)(2,1)}, bf16[8,16,256]{2,1,0:T(8,128)(2,1)S(1)}, u32[]{:S(2)}, u32[]{:S(2)}) collective-permute-start(bf16[8,16,256]{2,1,0:T(8,128)(2,1)} %get-tuple-element.69), channel_id=1, source_target_pairs={{0,16},{2,18},{4,20},{6,22},{8,24},{10,26},{12,28},{14,30},{16,0},... | collective-permute-start | bytes 196616 | tf_op jit(solution)/shard_map/ppermute | solution.py:430
  19.4 33.3 %collective-permute-start.27 = (bf16[8,16,256]{2,1,0:T(8,128)(2,1)}, bf16[8,16,256]{2,1,0:T(8,128)(2,1)S(1)}, u32[]{:S(2)}, u32[]{:S(2)}) collective-permute-start(bf16[8,16,256]{2,1,0:T(8,128)(2,1)} %get-tuple-element.70), channel_id=1, source_target_pairs={{0,18},{2,16},{4,22},{6,20},{8,26},{10,24},{12,30},{14,28},{16,2},... | collective-permute-start | bytes 196616 | tf_op jit(solution)/shard_map/ppermute | solution.py:430
  21.4 32.7 %collective-permute-start.28 = (bf16[8,16,256]{2,1,0:T(8,128)(2,1)}, bf16[8,16,256]{2,1,0:T(8,128)(2,1)S(1)}, u32[]{:S(2)}, u32[]{:S(2)}) collective-permute-start(bf16[8,16,256]{2,1,0:T(8,128)(2,1)} %get-tuple-element.71), channel_id=1, source_target_pairs={{0,20},{2,22},{4,16},{6,18},{8,28},{10,30},{12,24},{14,26},{16,4},... | collective-permute-start | bytes 196616 | tf_op jit(solution)/shard_map/ppermute | solution.py:430
  23.2 34.2 %collective-permute-start.29 = (bf16[8,16,256]{2,1,0:T(8,128)(2,1)}, bf16[8,16,256]{2,1,0:T(8,128)(2,1)S(1)}, u32[]{:S(2)}, u32[]{:S(2)}) collective-permute-start(bf16[8,16,256]{2,1,0:T(8,128)(2,1)} %get-tuple-element.72), channel_id=1, source_target_pairs={{0,22},{2,20},{4,18},{6,16},{8,30},{10,28},{12,26},{14,24},{16,6},... | collective-permute-start | bytes 196616 | tf_op jit(solution)/shard_map/ppermute | solution.py:430
  42.9 73.5 %all-to-all-start = ((bf16[8,8,16,256]{3,2,1,0:T(8,128)(2,1)}), bf16[8,8,16,256]{3,2,1,0:T(8,128)(2,1)}, u32[]{:S(2)}, u32[]{:S(2)}) async-start(bf16[8,8,16,256]{3,2,1,0:T(8,128)(2,1)} %get-tuple-element.41), calls=%async_computation | async-start | bytes 1048576 | tf_op jit(solution)/shard_map/all_to_all | solution.py:438
  48.8 31.0 %collective-permute-start.11 = (bf16[16,16,256]{2,1,0:T(8,128)(2,1)}, bf16[16,16,256]{2,1,0:T(8,128)(2,1)S(1)}, u32[]{:S(2)}, u32[]{:S(2)}) collective-permute-start(bf16[16,16,256]{2,1,0:T(8,128)(2,1)} %get-tuple-element.54), channel_id=1, source_target_pairs={{0,20},{2,22},{4,16},{6,18},{8,28},{10,30},{12,24},{14,26},{16,4},... | collective-permute-start | bytes 393224 | tf_op jit(solution)/shard_map/ppermute | solution.py:430
  52.7 30.6 %collective-permute-start.12 = (bf16[16,16,256]{2,1,0:T(8,128)(2,1)}, bf16[16,16,256]{2,1,0:T(8,128)(2,1)S(1)}, u32[]{:S(2)}, u32[]{:S(2)}) collective-permute-start(bf16[16,16,256]{2,1,0:T(8,128)(2,1)} %get-tuple-element.55), channel_id=1, source_target_pairs={{0,22},{2,20},{4,18},{6,16},{8,30},{10,28},{12,26},{14,24},{16,6},... | collective-permute-start | bytes 393224 | tf_op jit(solution)/shard_map/ppermute | solution.py:430
  54.2 10.7 %collective-permute-start.30 = (bf16[8,16,256]{2,1,0:T(8,128)(2,1)}, bf16[8,16,256]{2,1,0:T(8,128)(2,1)S(1)}, u32[]{:S(2)}, u32[]{:S(2)}) collective-permute-start(bf16[8,16,256]{2,1,0:T(8,128)(2,1)} %get-tuple-element.73), channel_id=1, source_target_pairs={{0,24},{2,26},{4,28},{6,30},{8,16},{10,18},{12,20},{14,22},{16,8},... | collective-permute-start | bytes 196616 | tf_op jit(solution)/shard_map/ppermute | solution.py:430
  71.9 23.8 %collective-permute-start.13 = (bf16[16,16,256]{2,1,0:T(8,128)(2,1)S(1)}, bf16[16,16,256]{2,1,0:T(8,128)(2,1)S(1)}, u32[]{:S(2)}, u32[]{:S(2)}) collective-permute-start(bf16[16,16,256]{2,1,0:T(8,128)(2,1)S(1)} %copy-done.32), channel_id=1, source_target_pairs={{0,24},{2,26},{4,28},{6,30},{8,16},{10,18},{12,20},{14,22},{16,8},... | collective-permute-start | bytes 393224 | tf_op jit(solution)/shard_map/ppermute | solution.py:430
  74.1 21.5 %collective-permute-start.14 = (bf16[16,16,256]{2,1,0:T(8,128)(2,1)S(1)}, bf16[16,16,256]{2,1,0:T(8,128)(2,1)S(1)}, u32[]{:S(2)}, u32[]{:S(2)}) collective-permute-start(bf16[16,16,256]{2,1,0:T(8,128)(2,1)S(1)} %copy-done.31), channel_id=1, source_target_pairs={{0,26},{2,24},{4,30},{6,28},{8,18},{10,16},{12,22},{14,20},{16,10}... | collective-permute-start | bytes 393224 | tf_op jit(solution)/shard_map/ppermute | solution.py:430
  77.8 17.9 %collective-permute-start.15 = (bf16[16,16,256]{2,1,0:T(8,128)(2,1)S(1)}, bf16[16,16,256]{2,1,0:T(8,128)(2,1)S(1)}, u32[]{:S(2)}, u32[]{:S(2)}) collective-permute-start(bf16[16,16,256]{2,1,0:T(8,128)(2,1)S(1)} %copy-done.30), channel_id=1, source_target_pairs={{0,28},{2,30},{4,24},{6,26},{8,20},{10,22},{12,16},{14,18},{16,12}... | collective-permute-start | bytes 393224 | tf_op jit(solution)/shard_map/ppermute | solution.py:430
  79.8 15.9 %collective-permute-start.16 = (bf16[16,16,256]{2,1,0:T(8,128)(2,1)S(1)}, bf16[16,16,256]{2,1,0:T(8,128)(2,1)S(1)}, u32[]{:S(2)}, u32[]{:S(2)}) collective-permute-start(bf16[16,16,256]{2,1,0:T(8,128)(2,1)S(1)} %copy-done.29), channel_id=1, source_target_pairs={{0,30},{2,28},{4,26},{6,24},{8,22},{10,20},{12,18},{14,16},{16,14}... | collective-permute-start | bytes 393224 | tf_op jit(solution)/shard_map/ppermute | solution.py:430
  83.3 20.8 %collective-permute-start.9 = (bf16[16,16,256]{2,1,0:T(8,128)(2,1)S(1)}, bf16[16,16,256]{2,1,0:T(8,128)(2,1)S(1)}, u32[]{:S(2)}, u32[]{:S(2)}) collective-permute-start(bf16[16,16,256]{2,1,0:T(8,128)(2,1)S(1)} %copy-done.28), channel_id=1, source_target_pairs={{0,16},{2,18},{4,20},{6,22},{8,24},{10,26},{12,28},{14,30},{16,0},... | collective-permute-start | bytes 393224 | tf_op jit(solution)/shard_map/ppermute | solution.py:430
  116.4 60.1 %all-to-all-start.3 = ((bf16[16,8,16,256]{3,2,1,0:T(8,128)(2,1)}), bf16[16,8,16,256]{3,2,1,0:T(8,128)(2,1)}, u32[]{:S(2)}, u32[]{:S(2)}) async-start(bf16[16,8,16,256]{3,2,1,0:T(8,128)(2,1)} %copy-done), calls=%async_computation.3 | async-start | bytes 2097152 | tf_op jit(solution)/shard_map/all_to_all | solution.py:466
  120.9 49.5 %collective-permute-start.8 = (bf16[8,24,16,256]{3,2,1,0:T(8,128)(2,1)S(1)}, bf16[8,24,16,256]{3,2,1,0:T(8,128)(2,1)S(1)}, u32[]{:S(2)}, u32[]{:S(2)}) collective-permute-start(bf16[8,24,16,256]{3,2,1,0:T(8,128)(2,1)S(1)} %all-to-all-done.1.kept), channel_id=1, source_target_pairs={{0,1},{1,0},{2,3},{3,2},{4,5},{5,4},{6,7},{7,6},{8,9},{9,8},{10,11... | collective-permute-start | bytes 4718600 | tf_op jit(solution)/shard_map/ppermute | solution.py:442
  127.4 42.9 %collective-permute-start.17 = (bf16[8,16,16,256]{3,2,1,0:T(8,128)(2,1)S(1)}, bf16[8,16,16,256]{3,2,1,0:T(8,128)(2,1)S(1)}, u32[]{:S(2)}, u32[]{:S(2)}) collective-permute-start(bf16[8,16,16,256]{3,2,1,0:T(8,128)(2,1)S(1)} %gather.1), channel_id=1, source_target_pairs={{0,1},{1,0},{2,3},{3,2},{4,5},{5,4},{6,7},{7,6},{8,9},{9,8},{10,11... | collective-permute-start | bytes 3145736 | tf_op jit(solution)/shard_map/ppermute | solution.py:442
  128.1 23.0 %collective-permute-start = (bf16[8,16,256]{2,1,0:T(8,128)(2,1)S(1)}, bf16[8,16,256]{2,1,0:T(8,128)(2,1)S(1)}, u32[]{:S(2)}, u32[]{:S(2)}) collective-permute-start(bf16[8,16,256]{2,1,0:T(8,128)(2,1)S(1)} %copy-done.40), channel_id=1, source_target_pairs={{0,16},{2,18},{4,20},{6,22},{8,24},{10,26},{12,28},{14,30},{16,0},... | collective-permute-start | bytes 196616 | tf_op jit(solution)/shard_map/ppermute | solution.py:430
  130.9 22.9 %collective-permute-start.1 = (bf16[8,16,256]{2,1,0:T(8,128)(2,1)S(1)}, bf16[8,16,256]{2,1,0:T(8,128)(2,1)S(1)}, u32[]{:S(2)}, u32[]{:S(2)}) collective-permute-start(bf16[8,16,256]{2,1,0:T(8,128)(2,1)S(1)} %copy-done.39), channel_id=1, source_target_pairs={{0,18},{2,16},{4,22},{6,20},{8,26},{10,24},{12,30},{14,28},{16,2},... | collective-permute-start | bytes 196616 | tf_op jit(solution)/shard_map/ppermute | solution.py:430
  132.4 22.5 %collective-permute-start.2 = (bf16[8,16,256]{2,1,0:T(8,128)(2,1)S(1)}, bf16[8,16,256]{2,1,0:T(8,128)(2,1)S(1)}, u32[]{:S(2)}, u32[]{:S(2)}) collective-permute-start(bf16[8,16,256]{2,1,0:T(8,128)(2,1)S(1)} %copy-done.38), channel_id=1, source_target_pairs={{0,20},{2,22},{4,16},{6,18},{8,28},{10,30},{12,24},{14,26},{16,4},... | collective-permute-start | bytes 196616 | tf_op jit(solution)/shard_map/ppermute | solution.py:430
  151.1 8.9 %collective-permute-start.3 = (bf16[8,16,256]{2,1,0:T(8,128)(2,1)S(1)}, bf16[8,16,256]{2,1,0:T(8,128)(2,1)S(1)}, u32[]{:S(2)}, u32[]{:S(2)}) collective-permute-start(bf16[8,16,256]{2,1,0:T(8,128)(2,1)S(1)} %copy-done.37), channel_id=1, source_target_pairs={{0,22},{2,20},{4,18},{6,16},{8,30},{10,28},{12,26},{14,24},{16,6},... | collective-permute-start | bytes 196616 | tf_op jit(solution)/shard_map/ppermute | solution.py:430
  153.8 8.7 %collective-permute-start.4 = (bf16[8,16,256]{2,1,0:T(8,128)(2,1)S(1)}, bf16[8,16,256]{2,1,0:T(8,128)(2,1)S(1)}, u32[]{:S(2)}, u32[]{:S(2)}) collective-permute-start(bf16[8,16,256]{2,1,0:T(8,128)(2,1)S(1)} %copy-done.36), channel_id=1, source_target_pairs={{0,24},{2,26},{4,28},{6,30},{8,16},{10,18},{12,20},{14,22},{16,8},... | collective-permute-start | bytes 196616 | tf_op jit(solution)/shard_map/ppermute | solution.py:430
  154.9 10.2 %collective-permute-start.5 = (bf16[8,16,256]{2,1,0:T(8,128)(2,1)S(1)}, bf16[8,16,256]{2,1,0:T(8,128)(2,1)S(1)}, u32[]{:S(2)}, u32[]{:S(2)}) collective-permute-start(bf16[8,16,256]{2,1,0:T(8,128)(2,1)S(1)} %copy-done.35), channel_id=1, source_target_pairs={{0,26},{2,24},{4,30},{6,28},{8,18},{10,16},{12,22},{14,20},{16,10}... | collective-permute-start | bytes 196616 | tf_op jit(solution)/shard_map/ppermute | solution.py:430
  176.5 30.1 %all-to-all-start.2 = ((bf16[8,8,16,256]{3,2,1,0:T(8,128)(2,1)}), bf16[8,8,16,256]{3,2,1,0:T(8,128)(2,1)S(1)}, u32[]{:S(2)}, u32[]{:S(2)}) async-start(bf16[8,8,16,256]{3,2,1,0:T(8,128)(2,1)} %get-tuple-element.60), calls=%async_computation.2 | async-start | bytes 1048576 | tf_op jit(solution)/shard_map/all_to_all | solution.py:438
  180.0 11.7 %collective-permute-start.18 = (bf16[8,16,256]{2,1,0:T(8,128)(2,1)S(1)}, bf16[8,16,256]{2,1,0:T(8,128)(2,1)S(1)}, u32[]{:S(2)}, u32[]{:S(2)}) collective-permute-start(bf16[8,16,256]{2,1,0:T(8,128)(2,1)S(1)} %get-tuple-element.61), channel_id=1, source_target_pairs={{0,16},{2,18},{4,20},{6,22},{8,24},{10,26},{12,28},{14,30},{16,0},... | collective-permute-start | bytes 196616 | tf_op jit(solution)/shard_map/ppermute | solution.py:430
  182.6 13.8 %collective-permute-start.19 = (bf16[8,16,256]{2,1,0:T(8,128)(2,1)S(1)}, bf16[8,16,256]{2,1,0:T(8,128)(2,1)S(1)}, u32[]{:S(2)}, u32[]{:S(2)}) collective-permute-start(bf16[8,16,256]{2,1,0:T(8,128)(2,1)S(1)} %get-tuple-element.62), channel_id=1, source_target_pairs={{0,18},{2,16},{4,22},{6,20},{8,26},{10,24},{12,30},{14,28},{16,2},... | collective-permute-start | bytes 196616 | tf_op jit(solution)/shard_map/ppermute | solution.py:430
  184.3 14.4 %collective-permute-start.20 = (bf16[8,16,256]{2,1,0:T(8,128)(2,1)S(1)}, bf16[8,16,256]{2,1,0:T(8,128)(2,1)S(1)}, u32[]{:S(2)}, u32[]{:S(2)}) collective-permute-start(bf16[8,16,256]{2,1,0:T(8,128)(2,1)S(1)} %get-tuple-element.63), channel_id=1, source_target_pairs={{0,20},{2,22},{4,16},{6,18},{8,28},{10,30},{12,24},{14,26},{16,4},... | collective-permute-start | bytes 196616 | tf_op jit(solution)/shard_map/ppermute | solution.py:430
  187.9 16.9 %collective-permute-start.21 = (bf16[8,16,256]{2,1,0:T(8,128)(2,1)}, bf16[8,16,256]{2,1,0:T(8,128)(2,1)S(1)}, u32[]{:S(2)}, u32[]{:S(2)}) collective-permute-start(bf16[8,16,256]{2,1,0:T(8,128)(2,1)} %get-tuple-element.64), channel_id=1, source_target_pairs={{0,22},{2,20},{4,18},{6,16},{8,30},{10,28},{12,26},{14,24},{16,6},... | collective-permute-start | bytes 196616 | tf_op jit(solution)/shard_map/ppermute | solution.py:430
  187.9 16.9 %collective-permute-start.22 = (bf16[8,16,256]{2,1,0:T(8,128)(2,1)}, bf16[8,16,256]{2,1,0:T(8,128)(2,1)S(1)}, u32[]{:S(2)}, u32[]{:S(2)}) collective-permute-start(bf16[8,16,256]{2,1,0:T(8,128)(2,1)} %get-tuple-element.65), channel_id=1, source_target_pairs={{0,24},{2,26},{4,28},{6,30},{8,16},{10,18},{12,20},{14,22},{16,8},... | collective-permute-start | bytes 196616 | tf_op jit(solution)/shard_map/ppermute | solution.py:430
  191.7 13.1 %collective-permute-start.23 = (bf16[8,16,256]{2,1,0:T(8,128)(2,1)}, bf16[8,16,256]{2,1,0:T(8,128)(2,1)S(1)}, u32[]{:S(2)}, u32[]{:S(2)}) collective-permute-start(bf16[8,16,256]{2,1,0:T(8,128)(2,1)} %get-tuple-element.66), channel_id=1, source_target_pairs={{0,26},{2,24},{4,30},{6,28},{8,18},{10,16},{12,22},{14,20},{16,10}... | collective-permute-start | bytes 196616 | tf_op jit(solution)/shard_map/ppermute | solution.py:430
  196.4 8.4 %collective-permute-start.24 = (bf16[8,16,256]{2,1,0:T(8,128)(2,1)S(1)}, bf16[8,16,256]{2,1,0:T(8,128)(2,1)S(1)}, u32[]{:S(2)}, u32[]{:S(2)}) collective-permute-start(bf16[8,16,256]{2,1,0:T(8,128)(2,1)S(1)} %get-tuple-element.67), channel_id=1, source_target_pairs={{0,28},{2,30},{4,24},{6,26},{8,20},{10,22},{12,16},{14,18},{16,12}... | collective-permute-start | bytes 196616 | tf_op jit(solution)/shard_map/ppermute | solution.py:430
  (49 other events, 813.9 us)

commit v4 on v3

--- a/solution.py
+++ b/solution.py
@@ -175,8 +175,9 @@
 TRANSFORM_MIB = 32
 
 
-def blocks_of(half, place, kept, far):
-    index, base = place[0], place[1]
+def blocks_of(half, kept, far):
+    index = lax.axis_index("seq")
+    base = index // half * half
     near = [(base + block, kept.at[block]) for block in range(half)]
     return near + [(index ^ (half + step), ref) for step, ref in enumerate(far)]
 
@@ -193,7 +194,7 @@
         message[slot, :, side * 128 : side * 128 + 128] = piece.astype(jnp.bfloat16)
 
 
-def pack_tokens_kernel(half, place, tokens, *rest):
+def pack_tokens_kernel(half, tokens, *rest):
     kept, *far, scratch = rest
     step = pl.program_id(0)
     rows, _, held = tokens.shape
@@ -205,7 +206,7 @@
 
     @pl.when(step == pl.num_programs(0) - 1)
     def _():
-        for target, message in blocks_of(half, place, kept, far):
+        for target, message in blocks_of(half, kept, far):
 
             def fill(lane, _):
                 send_rows(scratch, target * own + lane, stride, message, lane)
@@ -214,7 +215,7 @@
             lax.fori_loop(0, own, fill, 0, unroll=4)
 
 
-def pack_filters_kernel(half, place, filters, before, kept, *rest):
+def pack_filters_kernel(half, filters, before, kept, *rest):
     far, scratch = rest[:half], rest[half]
     step = pl.program_id(0)
     _, rows, _, held = filters.shape
@@ -229,7 +230,7 @@
     @pl.when(step == pl.num_programs(0) - 1)
     def _():
         kept[:, :own] = before[...]
-        for number, (target, message) in enumerate(blocks_of(half, place, kept, far)):
+        for number, (target, message) in enumerate(blocks_of(half, kept, far)):
             first = own if number < half else 0
 
             def fill(lane, _):
@@ -250,38 +251,35 @@
     return [jax.ShapeDtypeStruct((half, slots, rows, N2), jnp.bfloat16)] + [message] * half
 
 
-def pack_tokens(place, tokens, half, groups, other):
+def pack_tokens(tokens, half, groups, other):
     rows, _, channels = tokens.shape
     held = channels // groups
     own = held // (2 * half)
     steps = 2
-    block = pl.BlockSpec((rows // steps, N2, held), lambda s, place: (s, 0, place[2] ^ other))
+    block = pl.BlockSpec((rows // steps, N2, held), lambda s: (s, 0, lax.axis_index("bat") ^ other))
     return pl.pallas_call(
         functools.partial(pack_tokens_kernel, half),
-        grid_spec=pltpu.PrefetchScalarGridSpec(
-            num_scalar_prefetch=1,
-            grid=(steps,),
-            in_specs=[block],
-            out_specs=[VMEM] * (half + 1),
-            scratch_shapes=[pltpu.VMEM((2, rows * (held + PAD), 128), jnp.float32)],
-        ),
+        grid=(steps,),
+        in_specs=[block],
+        out_specs=[VMEM] * (half + 1),
+        scratch_shapes=[pltpu.VMEM((2, rows * (held + PAD), 128), jnp.float32)],
         out_shape=message_shapes(half, own, rows),
-    )(place, tokens)
-
-
-def pack_filters(place, filters, before, half):
+    )(tokens)
+
+
+def pack_filters(filters, before, half):
     _, rows, _, held = filters.shape
     steps = 2
     kept = jax.ShapeDtypeStruct((half, before.shape[1] + held // half, rows, N2), jnp.bfloat16)
     return pl.pallas_call(
         functools.partial(pack_filters_kernel, half),
         grid=(steps,),
-        in_specs=[SMEM, pl.BlockSpec((2, rows // steps, N2, held), lambda s: (0, s, 0, 0)), VMEM],
+        in_specs=[pl.BlockSpec((2, rows // steps, N2, held), lambda s: (0, s, 0, 0)), VMEM],
         out_specs=[VMEM] * (half + 1),
         out_shape=[kept] + message_shapes(half, held // half, rows)[1:],
         scratch_shapes=[pltpu.VMEM((2, 2 * rows * (held + PAD), 128), jnp.float32)],
         name="pack_filters",
-    )(place, filters, before)
+    )(filters, before)
 
 
 def gather_kernel(*refs):
@@ -309,12 +307,13 @@
     return jnp.concatenate([near[:, pl.ds(near_slot, 1)].reshape(N1 // 2, N2), *across], axis=0)
 
 
-def transform_kernel(half, own, other, whole, parts, lanes, place, gain, kept, *rest):
+def transform_kernel(half, own, other, whole, parts, lanes, gain, kept, *rest):
     far = rest[:half]
     rows_t, twiddle, cols_t, back_t, final_t = rest[half : half + 5]
     filters, outs = rest[half + 5 : half + 5 + parts], rest[half + 5 + parts :]
     near_filter, far_filter = (kept, filters) if parts == half else filters
-    index, base, core = place[0], place[1], place[2]
+    index, core = lax.axis_index("seq"), lax.axis_index("bat")
+    base = index // half * half
     piece = kept.shape[2]
     channels = [pl.program_id(0) * lanes + number for number in range(lanes)]
 
@@ -357,7 +356,7 @@
                 outs[1 + step][pl.ds(lane, 1)] = rows
 
 
-def transform(place, gain, kept, far, tables, filters, other, whole):
+def transform(gain, kept, far, tables, filters, other, whole):
     half, _, rows, _ = kept.shape
     own = far[0].shape[0]
     if whole:
@@ -368,14 +367,14 @@
     return pl.pallas_call(
         functools.partial(transform_kernel, half, own, other, whole, len(filters), LANES),
         grid=(own // LANES,),
-        in_specs=[SMEM, SMEM] + [VMEM] * len(inputs),
+        in_specs=[SMEM] + [VMEM] * len(inputs),
         out_specs=[VMEM] * len(out_shape),
         out_shape=out_shape,
         compiler_params=pltpu.CompilerParams(vmem_limit_bytes=TRANSFORM_MIB * 1024 * 1024),
-    )(place, gain, *inputs)
-
-
-def unpack_kernel(half, whole, place, *rest):
+    )(gain, *inputs)
+
+
+def unpack_kernel(half, whole, *rest):
     inputs, out, scratch = rest[: 1 if whole else half + 1], rest[-2], rest[-1]
     step = pl.program_id(0)
     rows, _, held = out.shape
@@ -388,7 +387,7 @@
         if whole:
             blocks = [(block, inputs[0].at[block]) for block in range(2 * half)]
         else:
-            blocks = blocks_of(half, place, inputs[0], inputs[1:])
+            blocks = blocks_of(half, inputs[0], inputs[1:])
         for source, message in blocks:
 
             def place_rows(lane, _):
@@ -404,32 +403,29 @@
         out[row] = block.astype(jnp.bfloat16).T
 
 
-def unpack(place, received, rows, channels, groups, half, other, partial):
+def unpack(received, rows, channels, groups, half, other, partial):
     whole = len(received) == 1
     held = channels // groups
     steps = 2
     inputs = [*received, *partial]
     return pl.pallas_call(
         functools.partial(unpack_kernel, half, whole),
-        grid_spec=pltpu.PrefetchScalarGridSpec(
-            num_scalar_prefetch=1,
-            grid=(steps,),
-            in_specs=[VMEM] * len(received) + [pl.BlockSpec(memory_space=pl.ANY)] * len(partial),
-            out_specs=pl.BlockSpec((rows // steps, N2, held), lambda s, place: (s, 0, place[2] ^ other)),
-            scratch_shapes=[pltpu.VMEM((2, rows * (held + PAD), 128), jnp.float32)],
-        ),
+        grid=(steps,),
+        in_specs=[VMEM] * len(received) + [pl.BlockSpec(memory_space=pl.ANY)] * len(partial),
+        out_specs=pl.BlockSpec((rows // steps, N2, held), lambda s: (s, 0, lax.axis_index("bat") ^ other)),
+        scratch_shapes=[pltpu.VMEM((2, rows * (held + PAD), 128), jnp.float32)],
         out_shape=jax.ShapeDtypeStruct((rows, N2, channels), jnp.bfloat16),
-        input_output_aliases={1 + len(received): 0} if partial else {},
+        input_output_aliases={len(received): 0} if partial else {},
         compiler_params=pltpu.CompilerParams(vmem_limit_bytes=12 * 1024 * 1024),
-    )(place, *inputs)
+    )(*inputs)
 
 
 def cross(far, count):
     half = count // 2
-    return [
-        lax.ppermute(block, "seq", [(s, s ^ (half + step)) for s in range(count)])
-        for step, block in enumerate(far)
-    ]
+    received = []
+    for step, block in enumerate(far):
+        received.append(lax.ppermute(block, "seq", [(s, s ^ (half + step)) for s in range(count)]))
+    return received
 
 
 def near(kept, count):
@@ -446,31 +442,29 @@
     count = lax.axis_size("seq")
     groups = lax.axis_size("bat")
     index = lax.axis_index("seq")
-    core = lax.axis_index("bat")
     _, local_length, channels = tokens.shape
     rows = N1 // count
     half = count // 2
-    place = jnp.stack([index, index // half * half, core]).astype(jnp.int32)
     laid = tokens.reshape(rows, N2, channels)
-    kept, *far = pack_tokens(place, laid, half, groups, 0)
+    kept, *far = pack_tokens(laid, half, groups, 0)
     far_own = cross(far, count)
-    kept, *far = pack_filters(place, filter_spectrum, kept, half)
+    kept, *far = pack_filters(filter_spectrum, kept, half)
     far_filters = cross(far, count)
     kept_own = near(kept, count)
-    kept, *far = pack_tokens(place, laid, half, groups, 1)
+    kept, *far = pack_tokens(laid, half, groups, 1)
     far_other = cross(far, count)
     kept_other = near(kept, count)
     *tables, final_t = dft_tables(relative_rows(index, count, rows))
     tables.append(jnp.concatenate([final_t[0], final_t[1]], axis=1))
-    (ready,) = transform(place, skip_gain, kept_own, far_own, tables, far_filters, 0, True)
+    (ready,) = transform(skip_gain, kept_own, far_own, tables, far_filters, 0, True)
     first = lax.all_to_all(ready, "seq", split_axis=0, concat_axis=0, tiled=True)
     gathered = gather(far_filters)
     filters = (swap(kept_own), swap(gathered))
-    kept, *far = transform(place, skip_gain, kept_other, far_other, tables, filters, 1, False)
+    kept, *far = transform(skip_gain, kept_other, far_other, tables, filters, 1, False)
     far = cross(far, count)
     kept = near(kept, count)
-    mixed = unpack(place, [first], rows, channels, groups, half, 0, [])
-    mixed = unpack(place, [kept, *far], rows, channels, groups, half, 1, [mixed])
+    mixed = unpack([first], rows, channels, groups, half, 0, [])
+    mixed = unpack([kept, *far], rows, channels, groups, half, 1, [mixed])
     return mixed.reshape(1, local_length, channels)
 
 

time: 210 us -> 208 us (level)
  Pallas kernels: 28.9 us -> 26.4 us
    pallas_call x4, Pallas kernels: 13.5 us -> 11 us  [the longest x2 6.06 us: pack_tokens(): pl.pallas_call(functools.partial(pack_tokens_kernel, half), grid=(steps,)...]
    unnamed x86 -> x84, local copies, waits for them, and re-layouts: 14.1 us -> 14.1 us
  transfers between devices with their start and end apart: 38 -> 38, of which waited for: 13 -> 12; matrix products, arithmetic and copies ran while one was open for 5% -> 5% of each run, Pallas kernels for 9% -> 8%
where the time goes in v4:
time: 208 us; the launch traced here: 207 us
  starting transfers between devices  106 us (51%)
  waiting for transfers between devices  51.2 us (25%)
  Pallas kernels  26.4 us (13%)
  local copies, waits for them, and re-layouts  14.2 us (7%)
  other arithmetic  9.36 us (4%)
    ppermute x32, starting transfers between devices, cross(): lax.ppermute(block, 'seq', [(s, s ^ half + step) for s in range(count)])  86 us
    ppermute x32, waiting for transfers between devices, cross(): lax.ppermute(block, 'seq', [(s, s ^ half + step) for s in range(count)])  44.5 us
    all_to_all x3, starting transfers between devices, near(): lax.all_to_all(kept, 'seq', split_axis=0, concat_axis=0, tiled=True, axis...  14.4 us
    unnamed x84, local copies, waits for them, and re-layouts  14.1 us
    pallas_call x2, Pallas kernels, transform(): pl.pallas_call(functools.partial(transform_kernel, half, own, other, whol...  10.8 us
    all_to_all x3, waiting for transfers between devices, near(): lax.all_to_all(kept, 'seq', split_axis=0, concat_axis=0, tiled=True, axis...  6.73 us
    pallas_call x2, Pallas kernels, pack_tokens(): pl.pallas_call(functools.partial(pack_tokens_kernel, half), grid=(steps,)...  6.06 us
    pallas_call x2, Pallas kernels, unpack(): pl.pallas_call(functools.partial(unpack_kernel, half, whole), grid=(steps...  4.93 us
  transfers between devices with their start and end apart: 38, of which 12 were waited for; matrix products, arithmetic and copies ran while one was open for 5% of the time, Pallas kernels for 8%

profile of v4, /device:TPU:0, one launch (start us, length us, event | category | flops | bytes accessed | tf_op | source)
XLA Modules:
  0.0 207.1 jit_solution(14174224011608975157)
XLA Ops:
  0.0 3.0 %shard_map.38 = (bf16[8,8,16,256]{3,2,1,0:T(8,128)(2,1)}, bf16[8,16,256]{2,1,0:T(8,128)(2,1)}, bf16[8,16,256]{2,1,0:T(8,128)(2,1)}, bf16[8,16,256]{2,1,0:T(8,128...) custom-call(bf16[16,256,256]{2,1,0:T(8,128)(2,1)} %bitcast.14), custom_call_target="tpu_custom_call" | custom-call | tf_op jit(solution)/shard_map/pallas_call | solution.py:260
  3.0 4.5 %pack_filters.1 = (bf16[8,24,16,256]{3,2,1,0:T(8,128)(2,1)}, bf16[16,16,256]{2,1,0:T(8,128)(2,1)}, bf16[16,16,256]{2,1,0:T(8,128)(2,1)}, bf16[16,16,256]{2,1,0:T...) custom-call(bf16[2,16,256,128]{3,2,1,0:T(8,128)(2,1)} %filters.1, ...), custom_call_target="tpu_custom_call" | custom-call | tf_op jit(solution)/shard_map/pack_filters/pallas_call | solution.py:274
  7.5 6.2 %all-to-all-start.1 = ((bf16[8,24,16,256]{3,2,1,0:T(8,128)(2,1)}), bf16[8,24,16,256]{3,2,1,0:T(8,128)(2,1)S(1)}, u32[]{:S(2)}, u32[]{:S(2)}) async-start(bf16[8,24,16,256]{3,2,1,0:T(8,128)(2,1)} %get-tuple-element.51), calls=%async_computation.1 | async-start | bytes 3145728 | tf_op jit(solution)/shard_map/all_to_all | solution.py:434
  13.8 4.0 %collective-permute-start.10 = (bf16[16,16,256]{2,1,0:T(8,128)(2,1)}, bf16[16,16,256]{2,1,0:T(8,128)(2,1)S(1)}, u32[]{:S(2)}, u32[]{:S(2)}) collective-permute-start(bf16[16,16,256]{2,1,0:T(8,128)(2,1)} %get-tuple-element.53), channel_id=1, source_target_pairs={{0,18},{2,16},{4,22},{6,20},{8,26},{10,24},{12,30},{14,28},{16,2},... | collective-permute-start | bytes 393224 | tf_op jit(solution)/shard_map/ppermute | solution.py:427
  22.0 3.5 %collective-permute-start.29 = (bf16[8,16,256]{2,1,0:T(8,128)(2,1)}, bf16[8,16,256]{2,1,0:T(8,128)(2,1)S(1)}, u32[]{:S(2)}, u32[]{:S(2)}) collective-permute-start(bf16[8,16,256]{2,1,0:T(8,128)(2,1)} %get-tuple-element.72), channel_id=1, source_target_pairs={{0,22},{2,20},{4,18},{6,16},{8,30},{10,28},{12,26},{14,24},{16,6},... | collective-permute-start | bytes 196616 | tf_op jit(solution)/shard_map/ppermute | solution.py:427
  25.5 3.1 %shard_map.37 = (bf16[8,8,16,256]{3,2,1,0:T(8,128)(2,1)}, bf16[8,16,256]{2,1,0:T(8,128)(2,1)}, bf16[8,16,256]{2,1,0:T(8,128)(2,1)}, bf16[8,16,256]{2,1,0:T(8,128...) custom-call(bf16[16,256,256]{2,1,0:T(8,128)(2,1)} %bitcast.15), custom_call_target="tpu_custom_call" | custom-call | tf_op jit(solution)/shard_map/pallas_call | solution.py:260
  34.9 6.7 %all-to-all-done.1.kept = bf16[8,24,16,256]{3,2,1,0:T(8,128)(2,1)S(1)} async-done(((bf16[8,24,16,256]{3,2,1,0:T(8,128)(2,1)}), bf16[8,24,16,256]{3,2,1,0:T(8,128)(2,1)S(1)}, u32[]{:S(2)}, u32[]{:S(2)}) %all-to-all-start.1) | async-done | bytes 1572896 | tf_op jit(solution)/shard_map/all_to_all | solution.py:434
  41.7 4.7 %all-to-all-start = ((bf16[8,8,16,256]{3,2,1,0:T(8,128)(2,1)}), bf16[8,8,16,256]{3,2,1,0:T(8,128)(2,1)}, u32[]{:S(2)}, u32[]{:S(2)}) async-start(bf16[8,8,16,256]{3,2,1,0:T(8,128)(2,1)} %get-tuple-element.41), calls=%async_computation | async-start | bytes 1048576 | tf_op jit(solution)/shard_map/all_to_all | solution.py:434
  47.5 4.0 %collective-permute-start.11 = (bf16[16,16,256]{2,1,0:T(8,128)(2,1)}, bf16[16,16,256]{2,1,0:T(8,128)(2,1)S(1)}, u32[]{:S(2)}, u32[]{:S(2)}) collective-permute-start(bf16[16,16,256]{2,1,0:T(8,128)(2,1)} %get-tuple-element.54), channel_id=1, source_target_pairs={{0,20},{2,22},{4,16},{6,18},{8,28},{10,30},{12,24},{14,26},{16,4},... | collective-permute-start | bytes 393224 | tf_op jit(solution)/shard_map/ppermute | solution.py:427
  52.9 3.2 %collective-permute-start.30 = (bf16[8,16,256]{2,1,0:T(8,128)(2,1)}, bf16[8,16,256]{2,1,0:T(8,128)(2,1)S(1)}, u32[]{:S(2)}, u32[]{:S(2)}) collective-permute-start(bf16[8,16,256]{2,1,0:T(8,128)(2,1)} %get-tuple-element.73), channel_id=1, source_target_pairs={{0,24},{2,26},{4,28},{6,30},{8,16},{10,18},{12,20},{14,22},{16,8},... | collective-permute-start | bytes 196616 | tf_op jit(solution)/shard_map/ppermute | solution.py:427
  57.3 6.4 %collective-permute-done.30.rest_4_ = bf16[8,16,256]{2,1,0:T(8,128)(2,1)S(1)} collective-permute-done((bf16[8,16,256]{2,1,0:T(8,128)(2,1)}, bf16[8,16,256]{2,1,0:T(8,128)(2,1)S(1)}, u32[]{:S(2)}, u32[]{:S(2)}) %collective-permute-start.30) | collective-permute-done | bytes 65568 | tf_op jit(solution)/shard_map/ppermute | solution.py:427
  64.5 4.1 %collective-permute-start.33 = (bf16[8,16,256]{2,1,0:T(8,128)(2,1)S(1)}, bf16[8,16,256]{2,1,0:T(8,128)(2,1)S(1)}, u32[]{:S(2)}, u32[]{:S(2)}) collective-permute-start(bf16[8,16,256]{2,1,0:T(8,128)(2,1)S(1)} %copy-done.40), channel_id=1, source_target_pairs={{0,30},{2,28},{4,26},{6,24},{8,22},{10,20},{12,18},{14,16},{16,14}... | collective-permute-start | bytes 196616 | tf_op jit(solution)/shard_map/ppermute | solution.py:427
  72.8 3.7 %collective-permute-start.14 = (bf16[16,16,256]{2,1,0:T(8,128)(2,1)S(1)}, bf16[16,16,256]{2,1,0:T(8,128)(2,1)S(1)}, u32[]{:S(2)}, u32[]{:S(2)}) collective-permute-start(bf16[16,16,256]{2,1,0:T(8,128)(2,1)S(1)} %copy-done.30), channel_id=1, source_target_pairs={{0,26},{2,24},{4,30},{6,28},{8,18},{10,16},{12,22},{14,20},{16,10}... | collective-permute-start | bytes 393224 | tf_op jit(solution)/shard_map/ppermute | solution.py:427
  78.5 3.5 %collective-permute-start.16 = (bf16[16,16,256]{2,1,0:T(8,128)(2,1)S(1)}, bf16[16,16,256]{2,1,0:T(8,128)(2,1)S(1)}, u32[]{:S(2)}, u32[]{:S(2)}) collective-permute-start(bf16[16,16,256]{2,1,0:T(8,128)(2,1)S(1)} %copy-done.28), channel_id=1, source_target_pairs={{0,30},{2,28},{4,26},{6,24},{8,22},{10,20},{12,18},{14,16},{16,14}... | collective-permute-start | bytes 393224 | tf_op jit(solution)/shard_map/ppermute | solution.py:427
  82.0 12.2 %collective-permute-start.9 = (bf16[16,16,256]{2,1,0:T(8,128)(2,1)S(1)}, bf16[16,16,256]{2,1,0:T(8,128)(2,1)S(1)}, u32[]{:S(2)}, u32[]{:S(2)}) collective-permute-start(bf16[16,16,256]{2,1,0:T(8,128)(2,1)S(1)} %copy-done.27), channel_id=1, source_target_pairs={{0,16},{2,18},{4,20},{6,22},{8,24},{10,26},{12,28},{14,30},{16,0},... | collective-permute-start | bytes 393224 | tf_op jit(solution)/shard_map/ppermute | solution.py:427
  94.4 8.4 %collective-permute-done.9.refs_0_.rest_13_ = bf16[16,16,256]{2,1,0:T(8,128)(2,1)S(1)} collective-permute-done((bf16[16,16,256]{2,1,0:T(8,128)(2,1)S(1)}, bf16[16,16,256]{2,1,0:T(8,128)(2,1)S(1)}, u32[]{:S(2)}, u32[]{:S(2)}) %collective-permute-start.9) | collective-permute-done | bytes 131104 | tf_op jit(solution)/shard_map/ppermute | solution.py:427
  106.2 4.7 %shard_map.40 = bf16[16,8,16,256]{3,2,1,0:T(8,128)(2,1)S(1)} custom-call(f32[256]{0:T(256)S(1)} %copy-done.25, bf16[8,24,16,256]{3,2,1,0:T(8,128)(2,1)S(1)} %all-to-all-done.1.kept, bf16[8,16,256]{2,1,0:T(8,128)(2,1)S(1)} %copy-done.18, bf16[8,16,256]{2,1,0:T(8,128)(2,1)S(1)} %copy-done.20, bf16[8,16,256]{2,1,0:T(8,128)(2,1)S(1)} %copy-done.22, ...), custom_call_target="tpu_custom_call" | custom-call | tf_op jit(solution)/shard_map/pallas_call | solution.py:367
  115.1 4.5 %all-to-all-start.3 = ((bf16[16,8,16,256]{3,2,1,0:T(8,128)(2,1)}), bf16[16,8,16,256]{3,2,1,0:T(8,128)(2,1)}, u32[]{:S(2)}, u32[]{:S(2)}) async-start(bf16[16,8,16,256]{3,2,1,0:T(8,128)(2,1)} %copy-done), calls=%async_computation.3 | async-start | bytes 2097152 | tf_op jit(solution)/shard_map/all_to_all | solution.py:460
  126.9 2.8 %collective-permute-start = (bf16[8,16,256]{2,1,0:T(8,128)(2,1)S(1)}, bf16[8,16,256]{2,1,0:T(8,128)(2,1)S(1)}, u32[]{:S(2)}, u32[]{:S(2)}) collective-permute-start(bf16[8,16,256]{2,1,0:T(8,128)(2,1)S(1)} %copy-done.39), channel_id=1, source_target_pairs={{0,16},{2,18},{4,20},{6,22},{8,24},{10,26},{12,28},{14,30},{16,0},... | collective-permute-start | bytes 196616 | tf_op jit(solution)/shard_map/ppermute | solution.py:427
  131.1 3.3 %collective-permute-start.2 = (bf16[8,16,256]{2,1,0:T(8,128)(2,1)S(1)}, bf16[8,16,256]{2,1,0:T(8,128)(2,1)S(1)}, u32[]{:S(2)}, u32[]{:S(2)}) collective-permute-start(bf16[8,16,256]{2,1,0:T(8,128)(2,1)S(1)} %copy-done.37), channel_id=1, source_target_pairs={{0,20},{2,22},{4,16},{6,18},{8,28},{10,30},{12,24},{14,26},{16,4},... | collective-permute-start | bytes 196616 | tf_op jit(solution)/shard_map/ppermute | solution.py:427
  134.4 15.4 %collective-permute-done.rest_0_ = bf16[8,16,256]{2,1,0:T(8,128)(2,1)S(1)} collective-permute-done((bf16[8,16,256]{2,1,0:T(8,128)(2,1)S(1)}, bf16[8,16,256]{2,1,0:T(8,128)(2,1)S(1)}, u32[]{:S(2)}, u32[]{:S(2)}) %collective-permute-start) | collective-permute-done | bytes 65568 | tf_op jit(solution)/shard_map/ppermute | solution.py:427
  153.6 2.9 %collective-permute-start.5 = (bf16[8,16,256]{2,1,0:T(8,128)(2,1)S(1)}, bf16[8,16,256]{2,1,0:T(8,128)(2,1)S(1)}, u32[]{:S(2)}, u32[]{:S(2)}) collective-permute-start(bf16[8,16,256]{2,1,0:T(8,128)(2,1)S(1)} %copy-done.34), channel_id=1, source_target_pairs={{0,26},{2,24},{4,30},{6,28},{8,18},{10,16},{12,22},{14,20},{16,10}... | collective-permute-start | bytes 196616 | tf_op jit(solution)/shard_map/ppermute | solution.py:427
  158.8 2.5 %collective-permute-start.6 = (bf16[8,16,256]{2,1,0:T(8,128)(2,1)S(1)}, bf16[8,16,256]{2,1,0:T(8,128)(2,1)S(1)}, u32[]{:S(2)}, u32[]{:S(2)}) collective-permute-start(bf16[8,16,256]{2,1,0:T(8,128)(2,1)S(1)} %copy-done.33), channel_id=1, source_target_pairs={{0,28},{2,30},{4,24},{6,26},{8,20},{10,22},{12,16},{14,18},{16,12}... | collective-permute-start | bytes 196616 | tf_op jit(solution)/shard_map/ppermute | solution.py:427
  161.3 2.6 %collective-permute-start.7 = (bf16[8,16,256]{2,1,0:T(8,128)(2,1)S(1)}, bf16[8,16,256]{2,1,0:T(8,128)(2,1)S(1)}, u32[]{:S(2)}, u32[]{:S(2)}) collective-permute-start(bf16[8,16,256]{2,1,0:T(8,128)(2,1)S(1)} %copy-done.32), channel_id=1, source_target_pairs={{0,30},{2,28},{4,26},{6,24},{8,22},{10,20},{12,18},{14,16},{16,14}... | collective-permute-start | bytes 196616 | tf_op jit(solution)/shard_map/ppermute | solution.py:427
  165.7 3.4 %collective-permute-done.7.rest_7_ = bf16[8,16,256]{2,1,0:T(8,128)(2,1)S(1)} collective-permute-done((bf16[8,16,256]{2,1,0:T(8,128)(2,1)S(1)}, bf16[8,16,256]{2,1,0:T(8,128)(2,1)S(1)}, u32[]{:S(2)}, u32[]{:S(2)}) %collective-permute-start.7) | collective-permute-done | bytes 65568 | tf_op jit(solution)/shard_map/ppermute | solution.py:427
  169.1 6.1 %shard_map.39 = (bf16[8,8,16,256]{3,2,1,0:T(8,128)(2,1)}, bf16[8,16,256]{2,1,0:T(8,128)(2,1)S(1)}, bf16[8,16,256]{2,1,0:T(8,128)(2,1)S(1)}, bf16[8,16,256]{2,1,0...) custom-call(f32[256]{0:T(256)S(1)} %copy-done.25, ...), custom_call_target="tpu_custom_call" | custom-call | tf_op jit(solution)/shard_map/pallas_call | solution.py:367
  175.2 3.5 %all-to-all-start.2 = ((bf16[8,8,16,256]{3,2,1,0:T(8,128)(2,1)}), bf16[8,8,16,256]{3,2,1,0:T(8,128)(2,1)S(1)}, u32[]{:S(2)}, u32[]{:S(2)}) async-start(bf16[8,8,16,256]{3,2,1,0:T(8,128)(2,1)} %get-tuple-element.60), calls=%async_computation.2 | async-start | bytes 1048576 | tf_op jit(solution)/shard_map/all_to_all | solution.py:434
  178.7 2.6 %collective-permute-start.18 = (bf16[8,16,256]{2,1,0:T(8,128)(2,1)S(1)}, bf16[8,16,256]{2,1,0:T(8,128)(2,1)S(1)}, u32[]{:S(2)}, u32[]{:S(2)}) collective-permute-start(bf16[8,16,256]{2,1,0:T(8,128)(2,1)S(1)} %get-tuple-element.61), channel_id=1, source_target_pairs={{0,16},{2,18},{4,20},{6,22},{8,24},{10,26},{12,28},{14,30},{16,0},... | collective-permute-start | bytes 196616 | tf_op jit(solution)/shard_map/ppermute | solution.py:427
  183.0 3.6 %collective-permute-start.20 = (bf16[8,16,256]{2,1,0:T(8,128)(2,1)S(1)}, bf16[8,16,256]{2,1,0:T(8,128)(2,1)S(1)}, u32[]{:S(2)}, u32[]{:S(2)}) collective-permute-start(bf16[8,16,256]{2,1,0:T(8,128)(2,1)S(1)} %get-tuple-element.63), channel_id=1, source_target_pairs={{0,20},{2,22},{4,16},{6,18},{8,28},{10,30},{12,24},{14,26},{16,4},... | collective-permute-start | bytes 196616 | tf_op jit(solution)/shard_map/ppermute | solution.py:427
  186.6 3.8 %collective-permute-start.22 = (bf16[8,16,256]{2,1,0:T(8,128)(2,1)}, bf16[8,16,256]{2,1,0:T(8,128)(2,1)S(1)}, u32[]{:S(2)}, u32[]{:S(2)}) collective-permute-start(bf16[8,16,256]{2,1,0:T(8,128)(2,1)} %get-tuple-element.65), channel_id=1, source_target_pairs={{0,24},{2,26},{4,28},{6,30},{8,16},{10,18},{12,20},{14,22},{16,8},... | collective-permute-start | bytes 196616 | tf_op jit(solution)/shard_map/ppermute | solution.py:427
  190.4 4.7 %collective-permute-start.23 = (bf16[8,16,256]{2,1,0:T(8,128)(2,1)}, bf16[8,16,256]{2,1,0:T(8,128)(2,1)S(1)}, u32[]{:S(2)}, u32[]{:S(2)}) collective-permute-start(bf16[8,16,256]{2,1,0:T(8,128)(2,1)} %get-tuple-element.66), channel_id=1, source_target_pairs={{0,26},{2,24},{4,30},{6,28},{8,18},{10,16},{12,22},{14,20},{16,10}... | collective-permute-start | bytes 196616 | tf_op jit(solution)/shard_map/ppermute | solution.py:427
  199.9 3.1 %shard_map.41.rest_9_ = bf16[16,256,256]{2,1,0:T(8,128)(2,1)} custom-call(bf16[16,8,16,256]{3,2,1,0:T(8,128)(2,1)} %all-to-all-done.3.rest_0_), custom_call_target="tpu_custom_call" | custom-call | tf_op jit(solution)/shard_map/pallas_call | solution.py:411
  (154 shorter events, 56.0 us)
Async XLA Ops:
  7.5 34.1 %all-to-all-start.1 = ((bf16[8,24,16,256]{3,2,1,0:T(8,128)(2,1)}), bf16[8,24,16,256]{3,2,1,0:T(8,128)(2,1)S(1)}, u32[]{:S(2)}, u32[]{:S(2)}) async-start(bf16[8,24,16,256]{3,2,1,0:T(8,128)(2,1)} %get-tuple-element.51), calls=%async_computation.1 | async-start | bytes 3145728 | tf_op jit(solution)/shard_map/all_to_all | solution.py:434
  13.8 62.8 %collective-permute-start.10 = (bf16[16,16,256]{2,1,0:T(8,128)(2,1)}, bf16[16,16,256]{2,1,0:T(8,128)(2,1)S(1)}, u32[]{:S(2)}, u32[]{:S(2)}) collective-permute-start(bf16[16,16,256]{2,1,0:T(8,128)(2,1)} %get-tuple-element.53), channel_id=1, source_target_pairs={{0,18},{2,16},{4,22},{6,20},{8,26},{10,24},{12,30},{14,28},{16,2},... | collective-permute-start | bytes 393224 | tf_op jit(solution)/shard_map/ppermute | solution.py:427
  17.8 29.7 %collective-permute-start.26 = (bf16[8,16,256]{2,1,0:T(8,128)(2,1)}, bf16[8,16,256]{2,1,0:T(8,128)(2,1)S(1)}, u32[]{:S(2)}, u32[]{:S(2)}) collective-permute-start(bf16[8,16,256]{2,1,0:T(8,128)(2,1)} %get-tuple-element.69), channel_id=1, source_target_pairs={{0,16},{2,18},{4,20},{6,22},{8,24},{10,26},{12,28},{14,30},{16,0},... | collective-permute-start | bytes 196616 | tf_op jit(solution)/shard_map/ppermute | solution.py:427
  18.1 33.3 %collective-permute-start.27 = (bf16[8,16,256]{2,1,0:T(8,128)(2,1)}, bf16[8,16,256]{2,1,0:T(8,128)(2,1)S(1)}, u32[]{:S(2)}, u32[]{:S(2)}) collective-permute-start(bf16[8,16,256]{2,1,0:T(8,128)(2,1)} %get-tuple-element.70), channel_id=1, source_target_pairs={{0,18},{2,16},{4,22},{6,20},{8,26},{10,24},{12,30},{14,28},{16,2},... | collective-permute-start | bytes 196616 | tf_op jit(solution)/shard_map/ppermute | solution.py:427
  20.2 32.8 %collective-permute-start.28 = (bf16[8,16,256]{2,1,0:T(8,128)(2,1)}, bf16[8,16,256]{2,1,0:T(8,128)(2,1)S(1)}, u32[]{:S(2)}, u32[]{:S(2)}) collective-permute-start(bf16[8,16,256]{2,1,0:T(8,128)(2,1)} %get-tuple-element.71), channel_id=1, source_target_pairs={{0,20},{2,22},{4,16},{6,18},{8,28},{10,30},{12,24},{14,26},{16,4},... | collective-permute-start | bytes 196616 | tf_op jit(solution)/shard_map/ppermute | solution.py:427
  22.0 34.2 %collective-permute-start.29 = (bf16[8,16,256]{2,1,0:T(8,128)(2,1)}, bf16[8,16,256]{2,1,0:T(8,128)(2,1)S(1)}, u32[]{:S(2)}, u32[]{:S(2)}) collective-permute-start(bf16[8,16,256]{2,1,0:T(8,128)(2,1)} %get-tuple-element.72), channel_id=1, source_target_pairs={{0,22},{2,20},{4,18},{6,16},{8,30},{10,28},{12,26},{14,24},{16,6},... | collective-permute-start | bytes 196616 | tf_op jit(solution)/shard_map/ppermute | solution.py:427
  41.7 73.5 %all-to-all-start = ((bf16[8,8,16,256]{3,2,1,0:T(8,128)(2,1)}), bf16[8,8,16,256]{3,2,1,0:T(8,128)(2,1)}, u32[]{:S(2)}, u32[]{:S(2)}) async-start(bf16[8,8,16,256]{3,2,1,0:T(8,128)(2,1)} %get-tuple-element.41), calls=%async_computation | async-start | bytes 1048576 | tf_op jit(solution)/shard_map/all_to_all | solution.py:434
  47.5 31.0 %collective-permute-start.11 = (bf16[16,16,256]{2,1,0:T(8,128)(2,1)}, bf16[16,16,256]{2,1,0:T(8,128)(2,1)S(1)}, u32[]{:S(2)}, u32[]{:S(2)}) collective-permute-start(bf16[16,16,256]{2,1,0:T(8,128)(2,1)} %get-tuple-element.54), channel_id=1, source_target_pairs={{0,20},{2,22},{4,16},{6,18},{8,28},{10,30},{12,24},{14,26},{16,4},... | collective-permute-start | bytes 393224 | tf_op jit(solution)/shard_map/ppermute | solution.py:427
  51.4 30.6 %collective-permute-start.12 = (bf16[16,16,256]{2,1,0:T(8,128)(2,1)}, bf16[16,16,256]{2,1,0:T(8,128)(2,1)S(1)}, u32[]{:S(2)}, u32[]{:S(2)}) collective-permute-start(bf16[16,16,256]{2,1,0:T(8,128)(2,1)} %get-tuple-element.55), channel_id=1, source_target_pairs={{0,22},{2,20},{4,18},{6,16},{8,30},{10,28},{12,26},{14,24},{16,6},... | collective-permute-start | bytes 393224 | tf_op jit(solution)/shard_map/ppermute | solution.py:427
  52.9 10.7 %collective-permute-start.30 = (bf16[8,16,256]{2,1,0:T(8,128)(2,1)}, bf16[8,16,256]{2,1,0:T(8,128)(2,1)S(1)}, u32[]{:S(2)}, u32[]{:S(2)}) collective-permute-start(bf16[8,16,256]{2,1,0:T(8,128)(2,1)} %get-tuple-element.73), channel_id=1, source_target_pairs={{0,24},{2,26},{4,28},{6,30},{8,16},{10,18},{12,20},{14,22},{16,8},... | collective-permute-start | bytes 196616 | tf_op jit(solution)/shard_map/ppermute | solution.py:427
  64.5 8.4 %collective-permute-start.33 = (bf16[8,16,256]{2,1,0:T(8,128)(2,1)S(1)}, bf16[8,16,256]{2,1,0:T(8,128)(2,1)S(1)}, u32[]{:S(2)}, u32[]{:S(2)}) collective-permute-start(bf16[8,16,256]{2,1,0:T(8,128)(2,1)S(1)} %copy-done.40), channel_id=1, source_target_pairs={{0,30},{2,28},{4,26},{6,24},{8,22},{10,20},{12,18},{14,16},{16,14}... | collective-permute-start | bytes 196616 | tf_op jit(solution)/shard_map/ppermute | solution.py:427
  70.6 23.8 %collective-permute-start.13 = (bf16[16,16,256]{2,1,0:T(8,128)(2,1)S(1)}, bf16[16,16,256]{2,1,0:T(8,128)(2,1)S(1)}, u32[]{:S(2)}, u32[]{:S(2)}) collective-permute-start(bf16[16,16,256]{2,1,0:T(8,128)(2,1)S(1)} %copy-done.31), channel_id=1, source_target_pairs={{0,24},{2,26},{4,28},{6,30},{8,16},{10,18},{12,20},{14,22},{16,8},... | collective-permute-start | bytes 393224 | tf_op jit(solution)/shard_map/ppermute | solution.py:427
  72.8 21.5 %collective-permute-start.14 = (bf16[16,16,256]{2,1,0:T(8,128)(2,1)S(1)}, bf16[16,16,256]{2,1,0:T(8,128)(2,1)S(1)}, u32[]{:S(2)}, u32[]{:S(2)}) collective-permute-start(bf16[16,16,256]{2,1,0:T(8,128)(2,1)S(1)} %copy-done.30), channel_id=1, source_target_pairs={{0,26},{2,24},{4,30},{6,28},{8,18},{10,16},{12,22},{14,20},{16,10}... | collective-permute-start | bytes 393224 | tf_op jit(solution)/shard_map/ppermute | solution.py:427
  76.5 17.9 %collective-permute-start.15 = (bf16[16,16,256]{2,1,0:T(8,128)(2,1)S(1)}, bf16[16,16,256]{2,1,0:T(8,128)(2,1)S(1)}, u32[]{:S(2)}, u32[]{:S(2)}) collective-permute-start(bf16[16,16,256]{2,1,0:T(8,128)(2,1)S(1)} %copy-done.29), channel_id=1, source_target_pairs={{0,28},{2,30},{4,24},{6,26},{8,20},{10,22},{12,16},{14,18},{16,12}... | collective-permute-start | bytes 393224 | tf_op jit(solution)/shard_map/ppermute | solution.py:427
  78.5 15.9 %collective-permute-start.16 = (bf16[16,16,256]{2,1,0:T(8,128)(2,1)S(1)}, bf16[16,16,256]{2,1,0:T(8,128)(2,1)S(1)}, u32[]{:S(2)}, u32[]{:S(2)}) collective-permute-start(bf16[16,16,256]{2,1,0:T(8,128)(2,1)S(1)} %copy-done.28), channel_id=1, source_target_pairs={{0,30},{2,28},{4,26},{6,24},{8,22},{10,20},{12,18},{14,16},{16,14}... | collective-permute-start | bytes 393224 | tf_op jit(solution)/shard_map/ppermute | solution.py:427
  82.0 20.8 %collective-permute-start.9 = (bf16[16,16,256]{2,1,0:T(8,128)(2,1)S(1)}, bf16[16,16,256]{2,1,0:T(8,128)(2,1)S(1)}, u32[]{:S(2)}, u32[]{:S(2)}) collective-permute-start(bf16[16,16,256]{2,1,0:T(8,128)(2,1)S(1)} %copy-done.27), channel_id=1, source_target_pairs={{0,16},{2,18},{4,20},{6,22},{8,24},{10,26},{12,28},{14,30},{16,0},... | collective-permute-start | bytes 393224 | tf_op jit(solution)/shard_map/ppermute | solution.py:427
  115.1 60.1 %all-to-all-start.3 = ((bf16[16,8,16,256]{3,2,1,0:T(8,128)(2,1)}), bf16[16,8,16,256]{3,2,1,0:T(8,128)(2,1)}, u32[]{:S(2)}, u32[]{:S(2)}) async-start(bf16[16,8,16,256]{3,2,1,0:T(8,128)(2,1)} %copy-done), calls=%async_computation.3 | async-start | bytes 2097152 | tf_op jit(solution)/shard_map/all_to_all | solution.py:460
  119.7 49.5 %collective-permute-start.8 = (bf16[8,24,16,256]{3,2,1,0:T(8,128)(2,1)S(1)}, bf16[8,24,16,256]{3,2,1,0:T(8,128)(2,1)S(1)}, u32[]{:S(2)}, u32[]{:S(2)}) collective-permute-start(bf16[8,24,16,256]{3,2,1,0:T(8,128)(2,1)S(1)} %all-to-all-done.1.kept), channel_id=1, source_target_pairs={{0,1},{1,0},{2,3},{3,2},{4,5},{5,4},{6,7},{7,6},{8,9},{9,8},{10,11... | collective-permute-start | bytes 4718600 | tf_op jit(solution)/shard_map/ppermute | solution.py:438
  126.2 42.9 %collective-permute-start.17 = (bf16[8,16,16,256]{3,2,1,0:T(8,128)(2,1)S(1)}, bf16[8,16,16,256]{3,2,1,0:T(8,128)(2,1)S(1)}, u32[]{:S(2)}, u32[]{:S(2)}) collective-permute-start(bf16[8,16,16,256]{3,2,1,0:T(8,128)(2,1)S(1)} %gather.1), channel_id=1, source_target_pairs={{0,1},{1,0},{2,3},{3,2},{4,5},{5,4},{6,7},{7,6},{8,9},{9,8},{10,11... | collective-permute-start | bytes 3145736 | tf_op jit(solution)/shard_map/ppermute | solution.py:438
  126.9 22.9 %collective-permute-start = (bf16[8,16,256]{2,1,0:T(8,128)(2,1)S(1)}, bf16[8,16,256]{2,1,0:T(8,128)(2,1)S(1)}, u32[]{:S(2)}, u32[]{:S(2)}) collective-permute-start(bf16[8,16,256]{2,1,0:T(8,128)(2,1)S(1)} %copy-done.39), channel_id=1, source_target_pairs={{0,16},{2,18},{4,20},{6,22},{8,24},{10,26},{12,28},{14,30},{16,0},... | collective-permute-start | bytes 196616 | tf_op jit(solution)/shard_map/ppermute | solution.py:427
  129.7 22.9 %collective-permute-start.1 = (bf16[8,16,256]{2,1,0:T(8,128)(2,1)S(1)}, bf16[8,16,256]{2,1,0:T(8,128)(2,1)S(1)}, u32[]{:S(2)}, u32[]{:S(2)}) collective-permute-start(bf16[8,16,256]{2,1,0:T(8,128)(2,1)S(1)} %copy-done.38), channel_id=1, source_target_pairs={{0,18},{2,16},{4,22},{6,20},{8,26},{10,24},{12,30},{14,28},{16,2},... | collective-permute-start | bytes 196616 | tf_op jit(solution)/shard_map/ppermute | solution.py:427
  131.1 22.5 %collective-permute-start.2 = (bf16[8,16,256]{2,1,0:T(8,128)(2,1)S(1)}, bf16[8,16,256]{2,1,0:T(8,128)(2,1)S(1)}, u32[]{:S(2)}, u32[]{:S(2)}) collective-permute-start(bf16[8,16,256]{2,1,0:T(8,128)(2,1)S(1)} %copy-done.37), channel_id=1, source_target_pairs={{0,20},{2,22},{4,16},{6,18},{8,28},{10,30},{12,24},{14,26},{16,4},... | collective-permute-start | bytes 196616 | tf_op jit(solution)/shard_map/ppermute | solution.py:427
  149.9 8.9 %collective-permute-start.3 = (bf16[8,16,256]{2,1,0:T(8,128)(2,1)S(1)}, bf16[8,16,256]{2,1,0:T(8,128)(2,1)S(1)}, u32[]{:S(2)}, u32[]{:S(2)}) collective-permute-start(bf16[8,16,256]{2,1,0:T(8,128)(2,1)S(1)} %copy-done.36), channel_id=1, source_target_pairs={{0,22},{2,20},{4,18},{6,16},{8,30},{10,28},{12,26},{14,24},{16,6},... | collective-permute-start | bytes 196616 | tf_op jit(solution)/shard_map/ppermute | solution.py:427
  152.5 8.7 %collective-permute-start.4 = (bf16[8,16,256]{2,1,0:T(8,128)(2,1)S(1)}, bf16[8,16,256]{2,1,0:T(8,128)(2,1)S(1)}, u32[]{:S(2)}, u32[]{:S(2)}) collective-permute-start(bf16[8,16,256]{2,1,0:T(8,128)(2,1)S(1)} %copy-done.35), channel_id=1, source_target_pairs={{0,24},{2,26},{4,28},{6,30},{8,16},{10,18},{12,20},{14,22},{16,8},... | collective-permute-start | bytes 196616 | tf_op jit(solution)/shard_map/ppermute | solution.py:427
  153.6 10.2 %collective-permute-start.5 = (bf16[8,16,256]{2,1,0:T(8,128)(2,1)S(1)}, bf16[8,16,256]{2,1,0:T(8,128)(2,1)S(1)}, u32[]{:S(2)}, u32[]{:S(2)}) collective-permute-start(bf16[8,16,256]{2,1,0:T(8,128)(2,1)S(1)} %copy-done.34), channel_id=1, source_target_pairs={{0,26},{2,24},{4,30},{6,28},{8,18},{10,16},{12,22},{14,20},{16,10}... | collective-permute-start | bytes 196616 | tf_op jit(solution)/shard_map/ppermute | solution.py:427
  175.2 30.1 %all-to-all-start.2 = ((bf16[8,8,16,256]{3,2,1,0:T(8,128)(2,1)}), bf16[8,8,16,256]{3,2,1,0:T(8,128)(2,1)S(1)}, u32[]{:S(2)}, u32[]{:S(2)}) async-start(bf16[8,8,16,256]{3,2,1,0:T(8,128)(2,1)} %get-tuple-element.60), calls=%async_computation.2 | async-start | bytes 1048576 | tf_op jit(solution)/shard_map/all_to_all | solution.py:434
  178.7 11.7 %collective-permute-start.18 = (bf16[8,16,256]{2,1,0:T(8,128)(2,1)S(1)}, bf16[8,16,256]{2,1,0:T(8,128)(2,1)S(1)}, u32[]{:S(2)}, u32[]{:S(2)}) collective-permute-start(bf16[8,16,256]{2,1,0:T(8,128)(2,1)S(1)} %get-tuple-element.61), channel_id=1, source_target_pairs={{0,16},{2,18},{4,20},{6,22},{8,24},{10,26},{12,28},{14,30},{16,0},... | collective-permute-start | bytes 196616 | tf_op jit(solution)/shard_map/ppermute | solution.py:427
  181.3 13.8 %collective-permute-start.19 = (bf16[8,16,256]{2,1,0:T(8,128)(2,1)S(1)}, bf16[8,16,256]{2,1,0:T(8,128)(2,1)S(1)}, u32[]{:S(2)}, u32[]{:S(2)}) collective-permute-start(bf16[8,16,256]{2,1,0:T(8,128)(2,1)S(1)} %get-tuple-element.62), channel_id=1, source_target_pairs={{0,18},{2,16},{4,22},{6,20},{8,26},{10,24},{12,30},{14,28},{16,2},... | collective-permute-start | bytes 196616 | tf_op jit(solution)/shard_map/ppermute | solution.py:427
  183.0 14.4 %collective-permute-start.20 = (bf16[8,16,256]{2,1,0:T(8,128)(2,1)S(1)}, bf16[8,16,256]{2,1,0:T(8,128)(2,1)S(1)}, u32[]{:S(2)}, u32[]{:S(2)}) collective-permute-start(bf16[8,16,256]{2,1,0:T(8,128)(2,1)S(1)} %get-tuple-element.63), channel_id=1, source_target_pairs={{0,20},{2,22},{4,16},{6,18},{8,28},{10,30},{12,24},{14,26},{16,4},... | collective-permute-start | bytes 196616 | tf_op jit(solution)/shard_map/ppermute | solution.py:427
  186.6 16.4 %collective-permute-start.21 = (bf16[8,16,256]{2,1,0:T(8,128)(2,1)}, bf16[8,16,256]{2,1,0:T(8,128)(2,1)S(1)}, u32[]{:S(2)}, u32[]{:S(2)}) collective-permute-start(bf16[8,16,256]{2,1,0:T(8,128)(2,1)} %get-tuple-element.64), channel_id=1, source_target_pairs={{0,22},{2,20},{4,18},{6,16},{8,30},{10,28},{12,26},{14,24},{16,6},... | collective-permute-start | bytes 196616 | tf_op jit(solution)/shard_map/ppermute | solution.py:427
  186.6 16.4 %collective-permute-start.22 = (bf16[8,16,256]{2,1,0:T(8,128)(2,1)}, bf16[8,16,256]{2,1,0:T(8,128)(2,1)S(1)}, u32[]{:S(2)}, u32[]{:S(2)}) collective-permute-start(bf16[8,16,256]{2,1,0:T(8,128)(2,1)} %get-tuple-element.65), channel_id=1, source_target_pairs={{0,24},{2,26},{4,28},{6,30},{8,16},{10,18},{12,20},{14,22},{16,8},... | collective-permute-start | bytes 196616 | tf_op jit(solution)/shard_map/ppermute | solution.py:427
  190.4 12.5 %collective-permute-start.23 = (bf16[8,16,256]{2,1,0:T(8,128)(2,1)}, bf16[8,16,256]{2,1,0:T(8,128)(2,1)S(1)}, u32[]{:S(2)}, u32[]{:S(2)}) collective-permute-start(bf16[8,16,256]{2,1,0:T(8,128)(2,1)} %get-tuple-element.66), channel_id=1, source_target_pairs={{0,26},{2,24},{4,30},{6,28},{8,18},{10,16},{12,22},{14,20},{16,10}... | collective-permute-start | bytes 196616 | tf_op jit(solution)/shard_map/ppermute | solution.py:427
  (48 other events, 757.5 us)
